TPU v7x, 32 devices: a whole 2x2x4 slice. The times are simulated.
32 devices in a mesh: tgt: 4 (over y, core), src: 8 (over z, x).
Axes of the slice: x: 2, y: 2, z: 4, core: 2. Of those that a mesh axis runs over, the one named last changes fastest.
Arguments:
- mobility: bfloat16 [3, 3, 4, 8, 64, 2048], P(None, None, None, 'src', None, 'tgt'), may hold values from -0.078125 to 0.078125
- right_side: float32 [3, 2048, 512], P(None, ('tgt', 'src')), may hold values from -6 to 6
- precond: float32 [96, 6144], P(None, ('tgt', 'src')), may hold values from -0.5 to 2.5
Outputs:
- solution: float32 [3, 2048, 512], P(None, ('tgt', 'src'))
- arnoldi: float32 [3, 2, 512], replicated
All inputs are finite; a program needn't handle non-finite values.
Results may differ from a plain program's by a relative error of at most 0.0012.
Values may be sent and summed in bfloat16 or wider, within the bound.
No kernel may reach another device: no remote copies, remote signals or barrier semaphores. Data moves between devices by JAX's collectives and lax.ppermute only.
A program may use at most 64 MiB of HBM per device.

v0:
```python
import jax
import jax.numpy as jnp
from jax import lax
from jax.sharding import PartitionSpec as P

FIBER_NODES = 32


def apply_blocks(blocks, vector):
    width = 3 * FIBER_NODES
    fibers = blocks.shape[1] // width
    case_count = vector.shape[2]
    tiles = blocks.reshape(width, fibers, width)
    arranged = (
        vector.reshape(3, fibers, FIBER_NODES, case_count)
        .transpose(1, 0, 2, 3)
        .reshape(fibers, width, case_count)
    )
    result = jnp.einsum("afb,fbr->far", tiles, arranged, precision=lax.Precision.HIGHEST)
    return (
        result.reshape(fibers, 3, FIBER_NODES, case_count)
        .transpose(1, 0, 2, 3)
        .reshape(3, fibers * FIBER_NODES, case_count)
    )


def least_squares(beta, h_one_one, h_two_one, h_one_two, h_two_two, h_three_two):
    rho_one = jnp.sqrt(h_one_one * h_one_one + h_two_one * h_two_one)
    cos_one = h_one_one / rho_one
    sin_one = h_two_one / rho_one
    g_one = cos_one * beta
    g_two = -sin_one * beta
    top = cos_one * h_one_two + sin_one * h_two_two
    low = cos_one * h_two_two - sin_one * h_one_two
    rho_two = jnp.sqrt(low * low + h_three_two * h_three_two)
    cos_two = low / rho_two
    sin_two = h_three_two / rho_two
    y_two = cos_two * g_two / rho_two
    y_one = (g_one - top * y_two) / rho_one
    return (y_one, y_two, jnp.abs(sin_two * g_two))


def inner(first, second):
    return jnp.sum(first * second, axis=(0, 1))


def local(mobility, right_side, precond):
    row_count = mobility.shape[5]
    local_tile = mobility.reshape(3, 3, mobility.shape[2] * mobility.shape[4], row_count)

    def accumulate(piece):
        return lax.dot_general(
            local_tile, piece, (((0, 2), (0, 1)), ((), ())), preferred_element_type=jnp.float32
        )

    def operate(vector):
        rounded = vector.astype(jnp.bfloat16)
        partial_value = accumulate(lax.all_gather(rounded, "tgt", axis=1, tiled=True))
        own_share = lax.psum_scatter(partial_value, "src", scatter_dimension=1, tiled=True)
        return vector + own_share

    initial = apply_blocks(precond, right_side)
    beta = jnp.sqrt(lax.psum(inner(initial, initial), ("tgt", "src")) + 1e-06)
    basis_one = initial / beta[None, None, :]
    work = apply_blocks(precond, operate(basis_one))
    h_one_one = lax.psum(inner(basis_one, work), ("tgt", "src"))
    work = work - h_one_one[None, None, :] * basis_one
    h_two_one = jnp.sqrt(lax.psum(inner(work, work), ("tgt", "src")) + 1e-06)
    basis_two = work / h_two_one[None, None, :]
    other = apply_blocks(precond, operate(basis_two))
    h_one_two = lax.psum(inner(basis_one, other), ("tgt", "src"))
    other = other - h_one_two[None, None, :] * basis_one
    h_two_two = lax.psum(inner(basis_two, other), ("tgt", "src"))
    other = other - h_two_two[None, None, :] * basis_two
    h_three_two = jnp.sqrt(lax.psum(inner(other, other), ("tgt", "src")) + 1e-06)
    y_one, y_two, estimate = least_squares(
        beta, h_one_one, h_two_one, h_one_two, h_two_two, h_three_two
    )
    solution = y_one[None, None, :] * basis_one + y_two[None, None, :] * basis_two
    arnoldi = jnp.stack(
        [
            jnp.stack([h_one_one, h_one_two]),
            jnp.stack([h_two_one, h_two_two]),
            jnp.stack([estimate, h_three_two]),
        ]
    )
    return (solution, arnoldi)


def solution(mesh):
    placed = (
        P(None, None, None, "src", None, "tgt"),
        P(None, ("tgt", "src"), None),
        P(None, ("tgt", "src")),
    )
    return jax.shard_map(
        local,
        mesh=mesh,
        in_specs=placed,
        out_specs=(P(None, ("tgt", "src"), None), P()),
        check_vma=False,
    )
```

profile of v0, /device:TPU:0, one launch (start us, length us, event | category | flops | bytes accessed | tf_op | source)
XLA Modules:
  0.0 447.6 jit_solution(8032743537599464176)
XLA Ops:
  7.2 1.2 reshape.53
  8.4 1.1 copy.5
  10.0 42.0 %psum.42 = f32[512]{0:T(512)S(1)} all-reduce(f32[512]{0:T(512)S(1)} %multiply_reduce_fusion.5), channel_id=1, replica_groups=mesh['tgt'=4,'src'=8] {'tgt','src'}, use_global_device_ids=true, to_apply=%region_1.0 | all-reduce | flops 512 | bytes 4096 | tf_op jit(solution)/shard_map/psum | solution.py:63
  52.1 9.4 %all_gather.6 = bf16[3,256,512]{2,1,0:T(8,128)(2,1)S(1)} all-gather(bf16[3,64,512]{2,1,0:T(8,128)(2,1)S(1)} %fusion.12), channel_id=1, replica_groups=mesh['tgt'=4,'src'=8] {'tgt'}, dimensions={1}, use_global_device_ids=true | all-gather | bytes 983040 | tf_op jit(solution)/shard_map/all_gather | solution.py:58
  61.5 3.1 convolution_bitcast_fusion.1
  64.7 73.9 %reduce-scatter.3.cloned.1.call-done = f32[3,64,512]{2,1,0:T(8,128)} async-done(((f32[3,512,512]{2,1,0:T(8,128)}), f32[3,64,512]{2,1,0:T(8,128)}) %reduce-scatter.3.cloned.1.call-update) | async-done | bytes 393232 | tf_op jit(solution)/shard_map/reduce_scatter | solution.py:59
  138.6 1.0 fusion.11
  139.7 1.4 fusion.5
  141.2 0.8 copy.12
  141.9 39.6 %psum.43 = f32[512]{0:T(512)S(1)} all-reduce(f32[512]{0:T(512)S(1)} %multiply_reduce_fusion.4), channel_id=1, replica_groups=mesh['tgt'=4,'src'=8] {'tgt','src'}, use_global_device_ids=true, to_apply=%region_4.0 | all-reduce | flops 512 | bytes 4096 | tf_op jit(solution)/shard_map/psum | solution.py:66
  181.6 39.5 %psum.44 = f32[512]{0:T(512)S(1)} all-reduce(f32[512]{0:T(512)S(1)} %multiply_reduce_fusion.3), channel_id=1, replica_groups=mesh['tgt'=4,'src'=8] {'tgt','src'}, use_global_device_ids=true, to_apply=%region_6.0 | all-reduce | flops 512 | bytes 4096 | tf_op jit(solution)/shard_map/psum | solution.py:68
  221.1 1.8 fusion.13
  222.9 9.4 %all_gather.7 = bf16[3,256,512]{2,1,0:T(8,128)(2,1)S(1)} all-gather(bf16[3,64,512]{2,1,0:T(8,128)(2,1)S(1)} %get-tuple-element.4), channel_id=1, replica_groups=mesh['tgt'=4,'src'=8] {'tgt'}, dimensions={1}, use_global_device_ids=true | all-gather | bytes 983040 | tf_op jit(solution)/shard_map/all_gather | solution.py:58
  232.3 3.1 convolution_bitcast_fusion
  235.4 73.5 %reduce-scatter.5.cloned.1.call-done = f32[3,64,512]{2,1,0:T(8,128)} async-done(((f32[3,512,512]{2,1,0:T(8,128)}), f32[3,64,512]{2,1,0:T(8,128)}) %reduce-scatter.5.cloned.1.call-update) | async-done | bytes 393232 | tf_op jit(solution)/shard_map/reduce_scatter | solution.py:59
  308.9 1.2 add.47
  310.1 1.4 fusion.3
  311.5 0.7 copy-done.1
  312.9 39.9 %psum.45 = f32[512]{0:T(512)S(1)} all-reduce(f32[512]{0:T(512)} %multiply_reduce_fusion.2), channel_id=1, replica_groups=mesh['tgt'=4,'src'=8] {'tgt','src'}, use_global_device_ids=true, to_apply=%region_9.0 | all-reduce | flops 512 | bytes 4096 | tf_op jit(solution)/shard_map/psum | solution.py:71
  352.8 1.7 multiply_reduce_fusion.1
  354.5 39.7 %psum.46 = f32[512]{0:T(512)} all-reduce(f32[512]{0:T(512)} %multiply_reduce_fusion.1), channel_id=1, replica_groups=mesh['tgt'=4,'src'=8] {'tgt','src'}, use_global_device_ids=true, to_apply=%region_11.0 | all-reduce | flops 512 | bytes 4096 | tf_op jit(solution)/shard_map/psum | solution.py:73
  394.1 1.8 multiply_reduce_fusion
  395.9 40.9 %psum.47 = f32[512]{0:T(512)S(1)} all-reduce(f32[512]{0:T(512)} %multiply_reduce_fusion), channel_id=1, replica_groups=mesh['tgt'=4,'src'=8] {'tgt','src'}, use_global_device_ids=true, to_apply=%region_13.0 | all-reduce | flops 512 | bytes 4096 | tf_op jit(solution)/shard_map/psum | solution.py:75
  438.3 1.8 multiply_add_fusion
  (29 shorter events, 3.7 us)
Async XLA Ops:
  7.2 54.3 %copy-start = (bf16[3,3,4,1,64,512]{5,4,3,2,1,0:T(8,128)(2,1)S(1)}, bf16[3,3,4,1,64,512]{5,4,3,2,1,0:T(8,128)(2,1)}, u32[]{:S(2)}) copy-start(bf16[3,3,4,1,64,512]{5,4,3,2,1,0:T(8,128)(2,1)} %param.3) | copy-start | bytes 7077892
  7.2 131.4 %reduce-scatter.3.cloned.1.call-start = ((), (), s32[]{:S(2)}) async-start(), calls=%async_computation.2 | async-start | bytes 3538944 | tf_op jit(solution)/shard_map/reduce_scatter | solution.py:59
  8.4 1.6 copy-start.2
  52.0 12.5 %copy-start.3 = (f32[512]{0:T(512)}, f32[512]{0:T(512)S(1)}, u32[]{:S(2)}) copy-start(f32[512]{0:T(512)S(1)} %psum.42) | copy-start | bytes 6148
  64.6 244.3 %reduce-scatter.5.cloned.1.call-start = ((), (), s32[]{:S(2)}) async-start(), calls=%async_computation.3 | async-start | bytes 3538944 | tf_op jit(solution)/shard_map/reduce_scatter | solution.py:59
  221.1 14.3 %copy-start.4 = (f32[512]{0:T(512)}, f32[512]{0:T(512)S(1)}, u32[]{:S(2)}) copy-start(f32[512]{0:T(512)S(1)} %psum.44) | copy-start | bytes 6148
  311.5 0.7 copy-start.1
Sparse Core Ops, SparseCore 0:
  64.7 73.8 reduce-scatter.2
  235.6 73.2 reduce-scatter.4
where the time goes:
time: 449 us; the launch traced here: 448 us
  blocking collectives  260 us (58%)
  waiting for transfers between devices  147 us (33%)
  between operations  14.2 us (3%)
  other arithmetic  12.4 us (3%)
  matrix products  9.42 us (2%)
    reduce_scatter x2, waiting for transfers between devices, operate(): lax.psum_scatter(partial_value, 'src', scatter_dimension=1, tiled=True)  147 us
    psum x1, blocking collectives, local(): beta = jnp.sqrt(lax.psum(inner(initial, initial), ('tgt', 'src')) + 1e-06)  42 us
    psum x1, blocking collectives, local(): lax.psum(inner(other, other), ('tgt', 'src')) + 1e-06  40.9 us
    psum x1, blocking collectives, local(): h_one_two = lax.psum(inner(basis_one, other), ('tgt', 'src'))  39.9 us
    psum x1, blocking collectives, local(): h_two_two = lax.psum(inner(basis_two, other), ('tgt', 'src'))  39.7 us
    psum x1, blocking collectives, local(): h_one_one = lax.psum(inner(basis_one, work), ('tgt', 'src'))  39.6 us
    psum x1, blocking collectives, local(): h_two_one = jnp.sqrt(lax.psum(inner(work, work), ('tgt', 'src')) + 1e-06)  39.5 us
    all_gather x2, blocking collectives, operate(): lax.all_gather(rounded, 'tgt', axis=1, tiled=True)  18.7 us
  transfers between devices with their start and end apart: 2, of which 2 were waited for; matrix products, arithmetic and copies ran while one was open for 0% of the time, Pallas kernels for 0%

commit v1 on v0

--- a/solution.py
+++ b/solution.py
@@ -4,6 +4,8 @@
 from jax.sharding import PartitionSpec as P
 
 FIBER_NODES = 32
+PIECES = 3
+PAD_ROWS = 16
 
 
 def apply_blocks(blocks, vector):
@@ -44,35 +46,106 @@
     return jnp.sum(first * second, axis=(0, 1))
 
 
+def split_rows(rows):
+    pieces = []
+    rest = rows
+    for _ in range(PIECES):
+        head = lax.reduce_precision(rest, 8, 7)
+        pieces.append(head)
+        rest = rest - head
+    stacked = jnp.concatenate(pieces)
+    stacked = jnp.pad(stacked, ((0, PAD_ROWS - stacked.shape[0]), (0, 0)))
+    return stacked.astype(jnp.bfloat16)
+
+
+def join_rows(stacked, count):
+    wide = stacked[:, : PIECES * count].astype(jnp.float32)
+    total = jnp.sum(wide, axis=0).reshape(PIECES, count, -1)
+    return jnp.sum(total, axis=0)
+
+
 def local(mobility, right_side, precond):
     row_count = mobility.shape[5]
-    local_tile = mobility.reshape(3, 3, mobility.shape[2] * mobility.shape[4], row_count)
+    sources = mobility.shape[2]
+    node_dev = mobility.shape[4]
+    targets = row_count // node_dev
+    cases = right_side.shape[2]
+    local_tile = mobility.reshape(3, 3, sources * node_dev, row_count)
 
-    def accumulate(piece):
-        return lax.dot_general(
-            local_tile, piece, (((0, 2), (0, 1)), ((), ())), preferred_element_type=jnp.float32
+    height = 3 * node_dev
+
+    def operate(vector, rows, terms):
+        count = rows.shape[0]
+        heads = []
+        rest = vector.reshape(height, cases)
+        for _ in range(terms):
+            head = lax.reduce_precision(rest, 8, 7)
+            heads.append(head.astype(jnp.bfloat16))
+            rest = rest - head
+        got = lax.all_gather(jnp.concatenate(heads + [split_rows(rows)]), "tgt")
+        partial_value = 0.0
+        for term in range(terms):
+            piece = got[:, term * height : (term + 1) * height].reshape(sources, 3, node_dev, cases)
+            piece = piece.transpose(1, 0, 2, 3).reshape(3, sources * node_dev, cases)
+            partial_value = partial_value + lax.dot_general(
+                local_tile, piece, (((0, 2), (0, 1)), ((), ())), preferred_element_type=jnp.float32
+            )
+        outgoing = (
+            partial_value.astype(jnp.bfloat16)
+            .reshape(3, targets, node_dev, cases)
+            .transpose(1, 0, 2, 3)
+            .reshape(targets, height, cases)
         )
+        extra = split_rows(join_rows(got[:, terms * height :], count))
+        outgoing = jnp.concatenate(
+            [outgoing, jnp.broadcast_to(extra, (targets,) + extra.shape)], axis=1
+        )
+        arrived = lax.all_to_all(outgoing, "src", 0, 0)
+        own_share = jnp.sum(arrived[:, : height].astype(jnp.float32), axis=0)
+        total = join_rows(arrived[:, height :], count)
+        return vector + own_share.reshape(3, node_dev, cases), total
 
-    def operate(vector):
-        rounded = vector.astype(jnp.bfloat16)
-        partial_value = accumulate(lax.all_gather(rounded, "tgt", axis=1, tiled=True))
-        own_share = lax.psum_scatter(partial_value, "src", scatter_dimension=1, tiled=True)
-        return vector + own_share
+    def total_of(rows):
+        first = jnp.sum(lax.all_to_all(jnp.broadcast_to(rows, (sources,) + rows.shape), "tgt", 0, 0), axis=0)
+        return jnp.sum(lax.all_to_all(jnp.broadcast_to(first, (targets,) + rows.shape), "src", 0, 0), axis=0)
 
-    initial = apply_blocks(precond, right_side)
-    beta = jnp.sqrt(lax.psum(inner(initial, initial), ("tgt", "src")) + 1e-06)
-    basis_one = initial / beta[None, None, :]
-    work = apply_blocks(precond, operate(basis_one))
-    h_one_one = lax.psum(inner(basis_one, work), ("tgt", "src"))
+    start = apply_blocks(precond, right_side)
+    moved, sums = operate(start, inner(start, start)[None], 2)
+    beta = jnp.sqrt(sums[0] + 1e-06)
+    basis_one = start / beta[None, None, :]
+    work = apply_blocks(precond, moved) / beta[None, None, :]
+    moved, sums = operate(work, inner(basis_one, work)[None], 1)
+    h_one_one = sums[0]
+    other = apply_blocks(precond, moved) - h_one_one[None, None, :] * work
     work = work - h_one_one[None, None, :] * basis_one
-    h_two_one = jnp.sqrt(lax.psum(inner(work, work), ("tgt", "src")) + 1e-06)
+    gram = total_of(
+        jnp.stack(
+            [
+                inner(work, work),
+                inner(basis_one, other),
+                inner(work, other),
+                inner(other, other),
+                inner(basis_one, work),
+                inner(basis_one, basis_one),
+                jnp.zeros((cases,), jnp.float32),
+                jnp.zeros((cases,), jnp.float32),
+            ]
+        )
+    )
+    work_work, one_other, work_other, other_other, one_work, one_one = (gram[k] for k in range(6))
+    h_two_one = jnp.sqrt(work_work + 1e-06)
     basis_two = work / h_two_one[None, None, :]
-    other = apply_blocks(precond, operate(basis_two))
-    h_one_two = lax.psum(inner(basis_one, other), ("tgt", "src"))
-    other = other - h_one_two[None, None, :] * basis_one
-    h_two_two = lax.psum(inner(basis_two, other), ("tgt", "src"))
-    other = other - h_two_two[None, None, :] * basis_two
-    h_three_two = jnp.sqrt(lax.psum(inner(other, other), ("tgt", "src")) + 1e-06)
+    h_one_two = one_other / h_two_one
+    h_two_two = work_other / (h_two_one * h_two_one)
+    two_two = work_work / (h_two_one * h_two_one)
+    one_two = one_work / h_two_one
+    rest = (
+        other_other / (h_two_one * h_two_one)
+        - h_one_two * h_one_two * (2.0 - one_one)
+        - h_two_two * h_two_two * (2.0 - two_two)
+        + 2.0 * h_one_two * h_two_two * one_two
+    )
+    h_three_two = jnp.sqrt(jnp.maximum(rest, 0.0) + 1e-06)
     y_one, y_two, estimate = least_squares(
         beta, h_one_one, h_two_one, h_one_two, h_two_two, h_three_two
     )

time: 449 us -> 169 us (0.38)
  blocking collectives: 260 us -> 115 us
  waiting for transfers between devices: 147 us -> 22.9 us
  other arithmetic: 12.4 us -> 5.37 us
    psum x6 -> x0, blocking collectives: 241 us -> none  [the longest x1 42 us: local(): beta = jnp.sqrt(lax.psum(inner(initial, initial), ('tgt', 'src')) + 1e-06)]
    reduce_scatter x2 -> x0, waiting for transfers between devices: 147 us -> none  [operate(): lax.psum_scatter(partial_value, 'src', scatter_dimension=1, tiled=True)]
    all_to_all x0 -> x4, blocking collectives: none -> 107 us  [the longest x2 89.9 us: operate(): arrived = lax.all_to_all(outgoing, 'src', 0, 0)]
    all_gather x0 -> x1, waiting for transfers between devices: none -> 22.9 us  [operate(): got = lax.all_gather(jnp.concatenate(heads + [split_rows(rows)]), 'tgt')]
    all_gather x2 -> x1, blocking collectives: 18.7 us -> 8 us  [operate(): got = lax.all_gather(jnp.concatenate(heads + [split_rows(rows)]), 'tgt')]
  transfers between devices with their start and end apart: 2 -> 1, of which waited for: 2 -> 1; matrix products, arithmetic and copies ran while one was open for 0% -> 0% of each run, Pallas kernels for 0% -> 0%
where the time goes in v1:
time: 169 us
  blocking collectives  115 us (68%)
  waiting for transfers between devices  22.9 us (14%)
  between operations  14.4 us (9%)
  matrix products  5.76 us (3%)
  local copies, waits for them, and re-layouts  5.69 us (3%)
  other arithmetic  5.37 us (3%)
    all_to_all x2, blocking collectives, operate(): arrived = lax.all_to_all(outgoing, 'src', 0, 0)  89.9 us
    all_gather x1, waiting for transfers between devices, operate(): got = lax.all_gather(jnp.concatenate(heads + [split_rows(rows)]), 'tgt')  22.9 us
    all_to_all x1, blocking collectives, total_of(): lax.all_to_all(jnp.broadcast_to(first, (targets,) + rows.shape), 'src', 0...  10.4 us
    all_gather x1, blocking collectives, operate(): got = lax.all_gather(jnp.concatenate(heads + [split_rows(rows)]), 'tgt')  8 us
    all_to_all x1, blocking collectives, total_of(): lax.all_to_all(jnp.broadcast_to(rows, (sources,) + rows.shape), 'tgt', 0, 0)  6.49 us
    dot_general x3, matrix products, operate(): lax.dot_general(local_tile, piece, (((0, 2), (0, 1)), ((), ())), preferre...  4.32 us
  transfers between devices with their start and end apart: 1, of which 1 were waited for; matrix products, arithmetic and copies ran while one was open for 0% of the time, Pallas kernels for 0%

profile of v1, /device:TPU:0, one launch (start us, length us, event | category | flops | bytes accessed | tf_op | source)
XLA Modules:
  0.0 169.0 jit_solution(6821109476687685410)
XLA Ops:
  7.2 1.2 reshape.354
  8.4 1.1 copy.46
  9.5 0.5 fusion.13
  10.1 0.8 pad_maximum_fusion.2
  10.9 22.9 %all-gather.4.cloned.1.call-done = bf16[1600,512]{1,0:T(8,128)(2,1)} async-done(((bf16[400,512]{1,0:T(8,128)(2,1)}), bf16[1600,512]{1,0:T(8,128)(2,1)}) %all-gather.4.cloned.1.call-update) | async-done | bytes 1638416 | tf_op jit(solution)/shard_map/all_gather | solution.py:85
  33.8 0.8 convert_reduce_fusion.5
  34.6 1.5 fusion.45
  36.2 1.4 fusion.46
  37.7 1.4 fusion
  39.5 45.8 %all_to_all.20 = bf16[8,208,512]{2,1,0:T(8,128)(2,1)S(1)} all-to-all(bf16[8,208,512]{2,1,0:T(8,128)(2,1)S(1)} %pad_maximum_fusion), channel_id=1, replica_groups=mesh['tgt'=4,'src'=8] {'src'}, dimensions={0} | all-to-all | bytes 3407872 | tf_op jit(solution)/shard_map/all_to_all | solution.py:103
  85.3 0.2 convert_reduce_fusion.1
  85.7 0.5 fusion.11
  86.5 8.0 %all-gather.1 = bf16[832,512]{1,0:T(8,128)(2,1)S(1)} all-gather(bf16[208,512]{1,0:T(8,128)(2,1)S(1)} %pad_maximum_fusion.3), channel_id=3, replica_groups=mesh['tgt'=4,'src'=8] {'tgt'}, dimensions={0}, use_global_device_ids=true | all-gather | bytes 1064960 | tf_op jit(solution)/shard_map/all_gather | solution.py:85
  94.6 1.4 bitcast_convert_fusion
  96.4 44.1 %all_to_all.21 = bf16[8,208,512]{2,1,0:T(8,128)(2,1)S(1)} all-to-all(bf16[8,208,512]{2,1,0:T(8,128)(2,1)S(1)} %pad_maximum_fusion.1), channel_id=1, replica_groups=mesh['tgt'=4,'src'=8] {'src'}, dimensions={0} | all-to-all | bytes 3407872 | tf_op jit(solution)/shard_map/all_to_all | solution.py:103
  140.5 0.2 convert_reduce_fusion
  140.9 0.5 copy-done.2
  141.4 0.5 fusion.9
  141.9 0.9 multiply_reduce_fusion.3
  142.8 0.7 stack.57
  143.6 6.5 %all_to_all.22 = f32[4,8,512]{2,1,0:T(8,128)S(1)} all-to-all(f32[4,8,512]{2,1,0:T(8,128)S(1)} %broadcast_in_dim.10), channel_id=1, replica_groups=mesh['tgt'=4,'src'=8] {'tgt'}, dimensions={0} | all-to-all | bytes 131072 | tf_op jit(solution)/shard_map/all_to_all | solution.py:109
  150.1 10.4 %all_to_all.23 = f32[8,8,512]{2,1,0:T(8,128)S(1)} all-to-all(f32[8,8,512]{2,1,0:T(8,128)S(1)} %broadcast_in_dim.22), channel_id=1, replica_groups=mesh['tgt'=4,'src'=8] {'src'}, dimensions={0} | all-to-all | bytes 262144 | tf_op jit(solution)/shard_map/all_to_all | solution.py:110
  160.6 0.6 pad_maximum_fusion.4
  161.2 0.9 multiply_add_fusion
  (49 shorter events, 1.8 us)
Async XLA Ops:
  7.2 29.1 %copy-start = (bf16[3,3,4,1,64,512]{5,4,3,2,1,0:T(8,128)(2,1)S(1)}, bf16[3,3,4,1,64,512]{5,4,3,2,1,0:T(8,128)(2,1)}, u32[]{:S(2)}) copy-start(bf16[3,3,4,1,64,512]{5,4,3,2,1,0:T(8,128)(2,1)} %param.3) | copy-start | bytes 7077892
  7.2 26.6 %all-gather.4.cloned.1.call-start = ((), (), s32[]{:S(2)}) async-start(), calls=%async_computation.4 | async-start | bytes 2048000 | tf_op jit(solution)/shard_map/all_gather | solution.py:85
  8.4 77.3 %copy-start.1 = (f32[96,2,96]{2,1,0:T(2,128)}, f32[96,2,96]{2,1,0:T(2,128)S(1)}, u32[]{:S(2)}) copy-start(f32[96,2,96]{2,1,0:T(2,128)S(1)} %reshape.354) | copy-start | bytes 221188
  140.5 0.9 copy-start.2
Sparse Core Ops, SparseCore 0:
  11.1 22.7 all-gather.3

commit v2 on v1

--- a/solution.py
+++ b/solution.py
@@ -1,11 +1,11 @@
 import jax
 import jax.numpy as jnp
 from jax import lax
-from jax.sharding import PartitionSpec as P
+from jax.sharding import Mesh, PartitionSpec as P
 
 FIBER_NODES = 32
 PIECES = 3
-PAD_ROWS = 16
+PAD_ROWS = 8
 
 
 def apply_blocks(blocks, vector):
@@ -82,10 +82,16 @@
             head = lax.reduce_precision(rest, 8, 7)
             heads.append(head.astype(jnp.bfloat16))
             rest = rest - head
-        got = lax.all_gather(jnp.concatenate(heads + [split_rows(rows)]), "tgt")
+        near = lax.all_gather(jnp.concatenate(heads + [split_rows(rows)]), "row")
+        cuts = [term * height for term in range(terms)] + [near.shape[1]]
+        got = [
+            lax.all_gather(near[:, first:last], "core", axis=1)
+            for first, last in zip(cuts[:-1], cuts[1:])
+        ]
+        got = [part.reshape((sources,) + part.shape[2:]) for part in got]
         partial_value = 0.0
         for term in range(terms):
-            piece = got[:, term * height : (term + 1) * height].reshape(sources, 3, node_dev, cases)
+            piece = got[term][:, :height].reshape(sources, 3, node_dev, cases)
             piece = piece.transpose(1, 0, 2, 3).reshape(3, sources * node_dev, cases)
             partial_value = partial_value + lax.dot_general(
                 local_tile, piece, (((0, 2), (0, 1)), ((), ())), preferred_element_type=jnp.float32
@@ -96,18 +102,26 @@
             .transpose(1, 0, 2, 3)
             .reshape(targets, height, cases)
         )
-        extra = split_rows(join_rows(got[:, terms * height :], count))
+        extra = split_rows(join_rows(got[-1][:, height:], count))
         outgoing = jnp.concatenate(
             [outgoing, jnp.broadcast_to(extra, (targets,) + extra.shape)], axis=1
         )
-        arrived = lax.all_to_all(outgoing, "src", 0, 0)
-        own_share = jnp.sum(arrived[:, : height].astype(jnp.float32), axis=0)
-        total = join_rows(arrived[:, height :], count)
+        outgoing = outgoing.reshape(2, targets // 2, height + PAD_ROWS, cases)
+        arrived = lax.all_to_all(outgoing, "near", 1, 1)
+        summed = jnp.sum(arrived[:, :, :height].astype(jnp.float32), axis=1)
+        sums = jnp.stack([join_rows(arrived[half, :, height:], count) for half in range(2)])
+        side = lax.axis_index("half")
+        keep = jnp.where(side == 0, summed[0], summed[1])
+        give = jnp.where(side == 0, summed[1], summed[0])
+        give = jnp.concatenate([give.astype(jnp.bfloat16), split_rows(sums[0])])
+        taken = lax.ppermute(give, "half", [(0, 1), (1, 0)])
+        own_share = keep + taken[:height].astype(jnp.float32)
+        total = sums[0] + join_rows(taken[None, height:], count)
         return vector + own_share.reshape(3, node_dev, cases), total
 
     def total_of(rows):
-        first = jnp.sum(lax.all_to_all(jnp.broadcast_to(rows, (sources,) + rows.shape), "tgt", 0, 0), axis=0)
-        return jnp.sum(lax.all_to_all(jnp.broadcast_to(first, (targets,) + rows.shape), "src", 0, 0), axis=0)
+        first = jnp.sum(lax.all_to_all(jnp.broadcast_to(rows, (sources,) + rows.shape), ("row", "core"), 0, 0), axis=0)
+        return jnp.sum(lax.all_to_all(jnp.broadcast_to(first, (targets,) + rows.shape), ("half", "near"), 0, 0), axis=0)
 
     start = apply_blocks(precond, right_side)
     moved, sums = operate(start, inner(start, start)[None], 2)
@@ -161,15 +175,20 @@
 
 
 def solution(mesh):
+    count_tgt, count_src = mesh.shape["tgt"], mesh.shape["src"]
+    grid = mesh.devices.reshape(count_tgt // 2, 2, 2, count_src // 2)
+    fine = Mesh(grid, ("row", "core", "half", "near"))
+    tgt = ("row", "core")
+    src = ("half", "near")
     placed = (
-        P(None, None, None, "src", None, "tgt"),
-        P(None, ("tgt", "src"), None),
-        P(None, ("tgt", "src")),
+        P(None, None, None, src, None, tgt),
+        P(None, tgt + src, None),
+        P(None, tgt + src),
     )
     return jax.shard_map(
         local,
-        mesh=mesh,
+        mesh=fine,
         in_specs=placed,
-        out_specs=(P(None, ("tgt", "src"), None), P()),
+        out_specs=(P(None, tgt + src, None), P()),
         check_vma=False,
     )

time: 169 us -> 138 us (0.82)
  blocking collectives: 115 us -> 69.6 us
  waiting for transfers between devices: 22.9 us -> 37.8 us
  between operations: 14.4 us -> 1.13 us
  starting transfers between devices: 0.04 us -> 10.2 us
    all_to_all x4 -> x3, blocking collectives: 107 us -> 43 us  [the longest x1 24.4 us: operate(): arrived = lax.all_to_all(outgoing, 'near', 1, 1)]
    all_gather x1 -> x0, waiting for transfers between devices: 22.9 us -> none  [operate(): got = lax.all_gather(jnp.concatenate(heads + [split_rows(rows)]), 'tgt')]
    all_to_all x0 -> x1, waiting for transfers between devices: none -> 20.7 us  [operate(): arrived = lax.all_to_all(outgoing, 'near', 1, 1)]
    all_gather x1 -> x5, blocking collectives: 8 us -> 26.5 us  [the longest x2 19.4 us: operate(): near = lax.all_gather(jnp.concatenate(heads + [split_rows(rows)]), 'row')]
    ppermute x0 -> x2, waiting for transfers between devices: none -> 17.1 us  [operate(): taken = lax.ppermute(give, 'half', [(0, 1), (1, 0)])]
    ppermute x0 -> x2, starting transfers between devices: none -> 5.85 us  [operate(): taken = lax.ppermute(give, 'half', [(0, 1), (1, 0)])]
    all_to_all x0 -> x1, starting transfers between devices: none -> 4.34 us  [operate(): arrived = lax.all_to_all(outgoing, 'near', 1, 1)]
  transfers between devices with their start and end apart: 1 -> 3, of which waited for: 1 -> 3; matrix products, arithmetic and copies ran while one was open for 0% -> 0% of each run, Pallas kernels for 0% -> 0%
where the time goes in v2:
time: 138 us
  blocking collectives  69.6 us (50%)
  waiting for transfers between devices  37.8 us (27%)
  starting transfers between devices  10.2 us (7%)
  local copies, waits for them, and re-layouts  6.95 us (5%)
  other arithmetic  6.43 us (5%)
  matrix products  5.82 us (4%)
    all_to_all x1, blocking collectives, operate(): arrived = lax.all_to_all(outgoing, 'near', 1, 1)  24.4 us
    all_to_all x1, waiting for transfers between devices, operate(): arrived = lax.all_to_all(outgoing, 'near', 1, 1)  20.7 us
    all_gather x2, blocking collectives, operate(): near = lax.all_gather(jnp.concatenate(heads + [split_rows(rows)]), 'row')  19.4 us
    ppermute x2, waiting for transfers between devices, operate(): taken = lax.ppermute(give, 'half', [(0, 1), (1, 0)])  17.1 us
    all_to_all x1, blocking collectives, total_of(): lax.all_to_all(jnp.broadcast_to(first, (targets,) + rows.shape), ('half',...  12 us
    all_gather x3, blocking collectives, operate(): lax.all_gather(near[:, first:last], 'core', axis=1)  7.14 us
    all_to_all x1, blocking collectives, total_of(): lax.all_to_all(jnp.broadcast_to(rows, (sources,) + rows.shape), ('row', '...  6.71 us
    ppermute x2, starting transfers between devices, operate(): taken = lax.ppermute(give, 'half', [(0, 1), (1, 0)])  5.85 us
  transfers between devices with their start and end apart: 3, of which 3 were waited for; matrix products, arithmetic and copies ran while one was open for 0% of the time, Pallas kernels for 0%

profile of v2, /device:TPU:0, one launch (start us, length us, event | category | flops | bytes accessed | tf_op | source)
XLA Modules:
  0.0 137.9 jit_solution(2743001289889312805)
XLA Ops:
  0.6 1.2 reshape.487
  1.8 1.1 copy.65
  3.6 13.0 %all-gather = bf16[784,512]{1,0:T(8,128)(2,1)S(1)} all-gather(bf16[392,512]{1,0:T(8,128)(2,1)S(1)} %pad_maximum_fusion.2), channel_id=2, replica_groups=mesh['row'=2,'core'=2,'half'=2,'near'=4] {'row'}, dimensions={0}, use_global_device_ids=true | all-gather | bytes 1204224 | tf_op jit(solution)/shard_map/all_gather | solution.py:85
  16.6 2.4 %all-gather.2 = bf16[2,400,512]{2,1,0:T(8,128)(2,1)S(1)} all-gather(bf16[2,200,512]{2,1,0:T(8,128)(2,1)S(1)} %slice.121), channel_id=4, replica_groups=mesh['row'=2,'core'=2,'half'=2,'near'=4] {'core'}, dimensions={1}, use_global_device_ids=true | all-gather | bytes 1228800 | tf_op jit(solution)/shard_map/all_gather | solution.py:88
  19.1 2.4 %all-gather.1 = bf16[2,384,512]{2,1,0:T(8,128)(2,1)S(1)} all-gather(bf16[2,192,512]{2,1,0:T(8,128)(2,1)S(1)} %slice.120), channel_id=3, replica_groups=mesh['row'=2,'core'=2,'half'=2,'near'=4] {'core'}, dimensions={1}, use_global_device_ids=true | all-gather | bytes 1179648 | tf_op jit(solution)/shard_map/all_gather | solution.py:88
  21.7 1.4 %fusion.61 = f32[512,3,512,1]{0,2,1,3:T(8,128)S(1)} fusion(bf16[3,256,512,1]{2,1,3,0:T(8,128)(2,1)S(1)} %bitcast.233, bf16[3,3,256,512]{3,2,1,0:T(8,128)(2,1)S(1)} %bitcast.202), kind=kOutput, calls=%fused_computation.148 | convolution fusion | flops 1207959552 | bytes 6291456 | tf_op jit(solution)/shard_map/dot_general | solution.py:96
  23.1 1.5 %fusion = bf16[512,3,512]{0,2,1:T(8,128)(2,1)S(1)} fusion(f32[512,3,512,1]{0,2,1,3:T(8,128)S(1)} %fusion.61, bf16[3,256,512,1]{2,1,3,0:T(8,128)(2,1)S(1)} %bitcast.234, bf16[3,3,256,512]{3,2,1,0:T(8,128)(2,1)S(1)} %bitcast.203), kind=kOutput, calls=%fused_computation.2 | convolution fusion | flops 1209532416 | bytes 7864320 | tf_op jit(solution)/shard_map/dot_general | solution.py:96
  25.0 1.3 copy.73
  26.3 4.3 %all-to-all-start = ((bf16[2,4,200,512]{3,2,0,1:T(8,128)(2,1)}), bf16[2,4,200,512]{3,2,0,1:T(8,128)(2,1)}, u32[]{:S(2)}, u32[]{:S(2)}) async-start(bf16[2,4,200,512]{3,2,0,1:T(8,128)(2,1)} %copy.73), calls=%async_computation | async-start | bytes 3276800 | tf_op jit(solution)/shard_map/all_to_all | solution.py:110
  30.7 20.7 %all-to-all-done = bf16[2,4,200,512]{3,2,0,1:T(8,128)(2,1)} async-done(((bf16[2,4,200,512]{3,2,0,1:T(8,128)(2,1)}), bf16[2,4,200,512]{3,2,0,1:T(8,128)(2,1)}, u32[]{:S(2)}, u32[]{:S(2)}) %all-to-all-start) | async-done | bytes 1638432 | tf_op jit(solution)/shard_map/all_to_all | solution.py:110
  52.1 1.8 %convert_reduce_fusion.1 = f32[2,192,512]{2,1,0:T(8,128)S(1)} fusion(bf16[2,4,200,512]{3,2,0,1:T(8,128)(2,1)} %all-to-all-done), kind=kLoop, calls=%fused_computation.4 | loop fusion | flops 1376256 | bytes 2359296 | tf_op jit(solution)/shard_map/reduce_sum | solution.py:111
  54.0 2.8 %collective-permute-start = (bf16[200,512]{1,0:T(8,128)(2,1)S(1)}, bf16[200,512]{1,0:T(8,128)(2,1)S(1)}, u32[]{:S(2)}, u32[]{:S(2)}) collective-permute-start(bf16[200,512]{1,0:T(8,128)(2,1)S(1)} %pad_maximum_fusion.3), channel_id=1, source_target_pairs={{0,4},{4,0},{1,5},{5,1},{2,6},{6,2},{3,7},{7,3},{8,12},{12,8},{9,1... | collective-permute-start | bytes 614408 | tf_op jit(solution)/shard_map/ppermute | solution.py:117
  56.8 8.9 %collective-permute-done = bf16[200,512]{1,0:T(8,128)(2,1)S(1)} collective-permute-done((bf16[200,512]{1,0:T(8,128)(2,1)S(1)}, bf16[200,512]{1,0:T(8,128)(2,1)S(1)}, u32[]{:S(2)}, u32[]{:S(2)}) %collective-permute-start) | collective-permute-done | bytes 204832 | tf_op jit(solution)/shard_map/ppermute | solution.py:117
  67.0 6.4 %all-gather.3 = bf16[400,512]{1,0:T(8,128)(2,1)S(1)} all-gather(bf16[200,512]{1,0:T(8,128)(2,1)S(1)} %pad_maximum_fusion.4), channel_id=5, replica_groups=mesh['row'=2,'core'=2,'half'=2,'near'=4] {'row'}, dimensions={0}, use_global_device_ids=true | all-gather | bytes 614400 | tf_op jit(solution)/shard_map/all_gather | solution.py:85
  73.5 2.4 %all-gather.4 = bf16[2,400,512]{2,1,0:T(8,128)(2,1)S(1)} all-gather(bf16[2,200,512]{2,1,0:T(8,128)(2,1)S(1)} %bitcast.224), channel_id=6, replica_groups=mesh['row'=2,'core'=2,'half'=2,'near'=4] {'core'}, dimensions={1}, use_global_device_ids=true | all-gather | bytes 1228800 | tf_op jit(solution)/shard_map/all_gather | solution.py:88
  76.0 1.4 %bitcast_convert_fusion = bf16[512,3,512]{0,2,1:T(8,128)(2,1)S(1)} fusion(bf16[3,256,512,1]{2,1,3,0:T(8,128)(2,1)S(1)} %bitcast.235, bf16[3,3,256,512]{3,2,1,0:T(8,128)(2,1)S(1)} %bitcast.201), kind=kOutput, calls=%fused_computation | convolution fusion | flops 1208745984 | bytes 4718592 | tf_op jit(solution)/shard_map/dot_general | solution.py:96
  77.9 24.4 %all_to_all.20 = bf16[2,4,200,512]{3,2,0,1:T(8,128)(2,1)S(1)} all-to-all(bf16[2,4,200,512]{3,2,0,1:T(8,128)(2,1)S(1)} %copy.80), channel_id=1, replica_groups=mesh['row'=2,'core'=2,'half'=2,'near'=4] {'near'}, dimensions={1} | all-to-all | bytes 3276800 | tf_op jit(solution)/shard_map/all_to_all | solution.py:110
  102.6 3.0 %collective-permute-start.1 = (bf16[200,512]{1,0:T(8,128)(2,1)S(1)}, bf16[200,512]{1,0:T(8,128)(2,1)S(1)}, u32[]{:S(2)}, u32[]{:S(2)}) collective-permute-start(bf16[200,512]{1,0:T(8,128)(2,1)S(1)} %pad_maximum_fusion.5), channel_id=1, source_target_pairs={{0,4},{4,0},{1,5},{5,1},{2,6},{6,2},{3,7},{7,3},{8,12},{12,8},{9,1... | collective-permute-start | bytes 614408 | tf_op jit(solution)/shard_map/ppermute | solution.py:117
  105.7 8.2 %collective-permute-done.1 = bf16[200,512]{1,0:T(8,128)(2,1)S(1)} collective-permute-done((bf16[200,512]{1,0:T(8,128)(2,1)S(1)}, bf16[200,512]{1,0:T(8,128)(2,1)S(1)}, u32[]{:S(2)}, u32[]{:S(2)}) %collective-permute-start.1) | collective-permute-done | bytes 204832 | tf_op jit(solution)/shard_map/ppermute | solution.py:117
  115.2 0.8 multiply_reduce_fusion.3
  116.8 6.7 %all_to_all.21 = f32[4,8,512]{2,1,0:T(8,128)S(1)} all-to-all(f32[4,8,512]{2,1,0:T(8,128)S(1)} %broadcast_in_dim.29), channel_id=1, replica_groups=mesh['row'=2,'core'=2,'half'=2,'near'=4] {'row','core'}, dimensions={0} | all-to-all | bytes 131072 | tf_op jit(solution)/shard_map/all_to_all | solution.py:123
  123.6 12.0 %all_to_all.22 = f32[8,8,512]{2,1,0:T(8,128)S(1)} all-to-all(f32[8,8,512]{2,1,0:T(8,128)S(1)} %broadcast_in_dim.30), channel_id=1, replica_groups=mesh['row'=2,'core'=2,'half'=2,'near'=4] {'half','near'}, dimensions={0} | all-to-all | bytes 262144 | tf_op jit(solution)/shard_map/all_to_all | solution.py:124
  135.5 0.8 multiply_abs_fusion
  137.0 0.9 multiply_add_fusion
  (80 shorter events, 7.0 us)
Async XLA Ops:
  0.6 21.0 %copy-start = (bf16[3,3,4,1,64,512]{5,4,3,2,1,0:T(8,128)(2,1)S(1)}, bf16[3,3,4,1,64,512]{5,4,3,2,1,0:T(8,128)(2,1)}, u32[]{:S(2)}) copy-start(bf16[3,3,4,1,64,512]{5,4,3,2,1,0:T(8,128)(2,1)} %param.3) | copy-start | bytes 7077892
  1.8 64.5 %copy-start.1 = (f32[96,2,96]{2,1,0:T(2,128)}, f32[96,2,96]{2,1,0:T(2,128)S(1)}, u32[]{:S(2)}) copy-start(f32[96,2,96]{2,1,0:T(2,128)S(1)} %reshape.487) | copy-start | bytes 221188
  26.3 25.0 %all-to-all-start = ((bf16[2,4,200,512]{3,2,0,1:T(8,128)(2,1)}), bf16[2,4,200,512]{3,2,0,1:T(8,128)(2,1)}, u32[]{:S(2)}, u32[]{:S(2)}) async-start(bf16[2,4,200,512]{3,2,0,1:T(8,128)(2,1)} %copy.73), calls=%async_computation | async-start | bytes 3276800 | tf_op jit(solution)/shard_map/all_to_all | solution.py:110
  54.0 11.7 %collective-permute-start = (bf16[200,512]{1,0:T(8,128)(2,1)S(1)}, bf16[200,512]{1,0:T(8,128)(2,1)S(1)}, u32[]{:S(2)}, u32[]{:S(2)}) collective-permute-start(bf16[200,512]{1,0:T(8,128)(2,1)S(1)} %pad_maximum_fusion.3), channel_id=1, source_target_pairs={{0,4},{4,0},{1,5},{5,1},{2,6},{6,2},{3,7},{7,3},{8,12},{12,8},{9,1... | collective-permute-start | bytes 614408 | tf_op jit(solution)/shard_map/ppermute | solution.py:117
  65.7 0.6 copy-start.3
  102.6 11.5 %copy-start.2 = (f32[96,2,96]{2,1,0:T(2,128)S(1)}, f32[96,2,96]{2,1,0:T(2,128)}, u32[]{:S(2)}) copy-start(f32[96,2,96]{2,1,0:T(2,128)} %copy-done.1) | copy-start | bytes 221188
  102.6 11.3 %collective-permute-start.1 = (bf16[200,512]{1,0:T(8,128)(2,1)S(1)}, bf16[200,512]{1,0:T(8,128)(2,1)S(1)}, u32[]{:S(2)}, u32[]{:S(2)}) collective-permute-start(bf16[200,512]{1,0:T(8,128)(2,1)S(1)} %pad_maximum_fusion.5), channel_id=1, source_target_pairs={{0,4},{4,0},{1,5},{5,1},{2,6},{6,2},{3,7},{7,3},{8,12},{12,8},{9,1... | collective-permute-start | bytes 614408 | tf_op jit(solution)/shard_map/ppermute | solution.py:117
  114.7 0.6 copy-start.4

commit v3 on v0

v3 whole, which is shorter than its diff:
```python
import jax
import jax.numpy as jnp
from jax import lax
from jax.sharding import Mesh, PartitionSpec as P

FIBER_NODES = 32
PIECES = 3
EXTRA = 8
SWAP = [(0, 1), (1, 0)]
TINY = 1e-06


def apply_blocks(blocks, vector):
    width = 3 * FIBER_NODES
    fibers = blocks.shape[1] // width
    case_count = vector.shape[2]
    tiles = blocks.reshape(width, fibers, width)
    arranged = (
        vector.reshape(3, fibers, FIBER_NODES, case_count)
        .transpose(1, 0, 2, 3)
        .reshape(fibers, width, case_count)
    )
    result = jnp.einsum("afb,fbr->far", tiles, arranged, precision=lax.Precision.HIGHEST)
    return (
        result.reshape(fibers, 3, FIBER_NODES, case_count)
        .transpose(1, 0, 2, 3)
        .reshape(3, fibers * FIBER_NODES, case_count)
    )


def least_squares(beta, h_one_one, h_two_one, h_one_two, h_two_two, h_three_two):
    rho_one = jnp.sqrt(h_one_one * h_one_one + h_two_one * h_two_one)
    cos_one = h_one_one / rho_one
    sin_one = h_two_one / rho_one
    g_one = cos_one * beta
    g_two = -sin_one * beta
    top = cos_one * h_one_two + sin_one * h_two_two
    low = cos_one * h_two_two - sin_one * h_one_two
    rho_two = jnp.sqrt(low * low + h_three_two * h_three_two)
    cos_two = low / rho_two
    sin_two = h_three_two / rho_two
    y_two = cos_two * g_two / rho_two
    y_one = (g_one - top * y_two) / rho_one
    return (y_one, y_two, jnp.abs(sin_two * g_two))


def inner(first, second):
    return jnp.sum(first * second, axis=(0, 1))


def pad_rows(rows):
    return jnp.pad(rows, ((0, EXTRA - rows.shape[0]), (0, 0)))


class Sums:
    dtype = jnp.bfloat16

    def __init__(self, rows):
        self.rows = rows

    def pack(self, body):
        pieces = []
        rest = self.rows
        for _ in range(PIECES):
            head = lax.reduce_precision(rest, 8, 7)
            pieces.append(head)
            rest = rest - head
        return body.astype(self.dtype), pad_rows(jnp.concatenate(pieces)).astype(self.dtype)

    def unpack(self, body, rows):
        count = self.rows.shape[0]
        wide = rows[: PIECES * count].astype(jnp.float32).reshape(PIECES, count, -1)
        return body.astype(jnp.float32), jnp.sum(wide, axis=0)

    def merge(self, other):
        return Sums(self.rows + other)

    def columns(self, first, last):
        return Sums(self.rows[:, first:last])


class Scale:
    dtype = jnp.float16

    def __init__(self, size):
        factors = []
        scale = jnp.ones_like(size)
        rest = size
        for _ in range(PIECES):
            factor = lax.reduce_precision(jnp.clip(rest, 2.0**-13, 2.0**15), 5, 10)
            factors.append(factor)
            scale = scale * factor
            rest = rest / factor
        self.factors = jnp.stack(factors)
        self.scale = scale

    def pack(self, body):
        scaled = body * (1.0 / self.scale)
        return scaled.astype(self.dtype), pad_rows(self.factors).astype(self.dtype)

    def unpack(self, body, rows):
        wide = rows[:PIECES].astype(jnp.float32)
        scale = wide[0] * wide[1] * wide[2]
        return body.astype(jnp.float32) * scale, scale

    def merge(self, other):
        return Scale(jnp.maximum(self.scale, other))

    def columns(self, first, last):
        return Scale(self.scale[first:last])


def pick(array, index, axis):
    return jnp.where(
        index == 0,
        lax.index_in_dim(array, 0, axis, False),
        lax.index_in_dim(array, 1, axis, False),
    )


def halve(array, note, names, name):
    axis = 1 + names.index(name)
    side = lax.axis_index(name)
    keep = pick(array, side, axis)
    body, rows = note.pack(pick(array, 1 - side, axis))
    sent = jnp.concatenate([body.reshape(-1, body.shape[-1]), rows])
    got = lax.ppermute(sent, name, SWAP)
    value, other = note.unpack(got[:-EXTRA].reshape(keep.shape), got[-EXTRA:])
    return keep + value, note.merge(other), [n for n in names if n != name]


def exchange(array, note, names):
    cases = array.shape[-1]
    half = cases // 2
    lower = names[1:]
    colours = [
        (array[..., :half], note.columns(0, half), names),
        (array[..., half:], note.columns(half, cases), names),
    ]
    for first, second in zip(reversed(lower), lower):
        colours = [halve(*colours[0], first), halve(*colours[1], second)]
    parts = [colour[0] for colour in colours]
    array = jnp.concatenate(parts, axis=-1)
    if isinstance(note, Sums):
        note = Sums(jnp.concatenate([colour[1].rows for colour in colours], axis=-1))
    else:
        note = Scale(jnp.concatenate([colour[1].scale for colour in colours], axis=-1))
    array, note, _ = halve(array, note, names[:1], names[0])
    return array, note


def build(bits):
    def local(mobility, right_side, precond):
        row_count = mobility.shape[5]
        sources = mobility.shape[2]
        node_dev = mobility.shape[4]
        cases = right_side.shape[2]
        height = 3 * node_dev
        local_tile = mobility.reshape(3, 3, sources * node_dev, row_count)

        def gather(vector, note):
            body, rows = note.pack(vector.reshape(height, cases))
            got = lax.all_gather(jnp.concatenate([body, rows]), ("row", "core"))
            return got[:, :height], got[:, height:]

        def arrange(got):
            piece = got.reshape(sources, 3, node_dev, cases).transpose(1, 0, 2, 3)
            return piece.reshape(3, sources * node_dev, cases)

        def couple(piece):
            return lax.dot_general(
                local_tile, piece, (((0, 2), (0, 1)), ((), ())), preferred_element_type=jnp.float32
            )

        def chunks(partial_value):
            return partial_value.reshape((3,) + (2,) * len(bits) + (node_dev, cases))

        start = apply_blocks(precond, right_side)
        note = Scale(jnp.max(jnp.abs(start), axis=(0, 1)))
        got, rows = gather(start, note)
        pairs = [note.unpack(got[k], rows[k]) for k in range(sources)]
        value = arrange(jnp.stack([pair[0] for pair in pairs]))
        head = lax.reduce_precision(value, 8, 7)
        tail = value - head
        partial_value = couple(head.astype(jnp.bfloat16)) + couple(tail.astype(jnp.bfloat16))
        size = jnp.max(jnp.stack([pair[1] for pair in pairs]), axis=0)
        share, _ = exchange(chunks(partial_value), Scale(size), bits)
        work = apply_blocks(precond, start + share)

        note = Sums(jnp.stack([inner(start, start), inner(start, work)]))
        got, rows = gather(work, note)
        total = sum(note.unpack(got[k], rows[k])[1] for k in range(sources))
        share, note = exchange(chunks(couple(arrange(got))), Sums(total), bits)
        start_start, start_work = note.rows[0], note.rows[1]
        square = start_start + TINY
        beta = jnp.sqrt(square)
        h_one_one = start_work / square
        other = apply_blocks(precond, work + share) - h_one_one[None, None, :] * work
        work = work - h_one_one[None, None, :] * start

        gram = jnp.stack(
            [inner(work, work), inner(start, other), inner(work, other), inner(other, other)]
        )
        flat = gram.reshape(-1, 128)
        flat = flat + lax.ppermute(flat, "core", SWAP)
        members = sources // 2 * 2 ** len(bits)
        flat = lax.all_to_all(
            jnp.broadcast_to(flat, (members,) + flat.shape), ("row",) + tuple(bits), 0, 0
        )
        work_work, start_other, work_other, other_other = jnp.sum(flat, axis=0).reshape(4, cases)

        norm = work_work / square
        h_two_one = jnp.sqrt(norm + TINY)
        length = beta * h_two_one
        h_one_two = start_other / (beta * length)
        h_two_two = work_other / (length * length)
        loss_one = TINY / square
        loss_two = TINY / (h_two_one * h_two_one)
        one_two = h_one_one * loss_one / h_two_one
        rest = (
            other_other / (length * length)
            - h_one_two * h_one_two * (1.0 + loss_one)
            - h_two_two * h_two_two * (1.0 + loss_two)
            + 2.0 * h_one_two * h_two_two * one_two
        )
        h_three_two = jnp.sqrt(jnp.maximum(rest, 0.0) + TINY)
        y_one, y_two, estimate = least_squares(
            beta, h_one_one, h_two_one, h_one_two, h_two_two, h_three_two
        )
        solution = (y_one / beta)[None, None, :] * start + (y_two / length)[None, None, :] * work
        arnoldi = jnp.stack(
            [
                jnp.stack([h_one_one, h_one_two]),
                jnp.stack([h_two_one, h_two_two]),
                jnp.stack([estimate, h_three_two]),
            ]
        )
        return (solution, arnoldi)

    return local


def solution(mesh):
    count_tgt, count_src = mesh.shape["tgt"], mesh.shape["src"]
    depth = count_src.bit_length() - 1
    bits = ["bit%d" % k for k in reversed(range(depth))]
    tgt = ("row", "core")
    src = tuple(bits)
    grid = mesh.devices.reshape((count_tgt // 2, 2) + (2,) * depth)
    placed = (
        P(None, None, None, src, None, tgt),
        P(None, tgt + src, None),
        P(None, tgt + src),
    )
    return jax.shard_map(
        build(bits),
        mesh=Mesh(grid, tgt + src),
        in_specs=placed,
        out_specs=(P(None, tgt + src, None), P()),
        check_vma=False,
    )
```

time: 449 us -> 167 us (0.37)
  blocking collectives: 260 us -> 18.8 us
  waiting for transfers between devices: 147 us -> 54.9 us
  other arithmetic: 12.4 us -> 37.9 us
  local copies, waits for them, and re-layouts: 3.84 us -> 27 us
  starting transfers between devices: 0.08 us -> 17.2 us
  between operations: 14.2 us -> 1.65 us
    psum x6 -> x0, blocking collectives: 241 us -> none  [the longest x1 42 us: local(): beta = jnp.sqrt(lax.psum(inner(initial, initial), ('tgt', 'src')) + 1e-06)]
    reduce_scatter x2 -> x0, waiting for transfers between devices: 147 us -> none  [operate(): lax.psum_scatter(partial_value, 'src', scatter_dimension=1, tiled=True)]
    ppermute x0 -> x11, waiting for transfers between devices: none -> 47 us  [the longest x10 45.9 us: halve(): got = lax.ppermute(sent, name, SWAP)]
    ppermute x0 -> x11, starting transfers between devices: none -> 12.8 us  [the longest x10 12.8 us: halve(): got = lax.ppermute(sent, name, SWAP)]
    slice x0 -> x14, local copies, waits for them, and re-layouts: none -> 8.15 us  [the longest x3 4.13 us: pick(): lax.index_in_dim(array, 0, axis, False)]
    all_to_all x0 -> x1, waiting for transfers between devices: none -> 7.82 us  [local(): lax.all_to_all(jnp.broadcast_to(flat, (members,) + flat.shape), ('row',)...]
    reduce_sum x0 -> x10, other arithmetic: none -> 7.73 us  [the longest x9 6.81 us: unpack(): return (body.astype(jnp.float32), jnp.sum(wide, axis=0))]
    unnamed x10 -> x56, local copies, waits for them, and re-layouts: 0.76 us -> 6.74 us
  transfers between devices with their start and end apart: 2 -> 12, of which waited for: 2 -> 12; matrix products, arithmetic and copies ran while one was open for 0% -> 12% of each run, Pallas kernels for 0% -> 0%
where the time goes in v3:
time: 167 us; the launch traced here: 166 us
  waiting for transfers between devices  54.9 us (33%)
  other arithmetic  37.9 us (23%)
  local copies, waits for them, and re-layouts  27 us (16%)
  blocking collectives  18.8 us (11%)
  starting transfers between devices  17.2 us (10%)
  matrix products  8.25 us (5%)
    ppermute x10, waiting for transfers between devices, halve(): got = lax.ppermute(sent, name, SWAP)  45.9 us
    all_gather x2, blocking collectives, gather(): got = lax.all_gather(jnp.concatenate([body, rows]), ('row', 'core'))  18.8 us
    ppermute x10, starting transfers between devices, halve(): got = lax.ppermute(sent, name, SWAP)  12.8 us
    all_to_all x1, waiting for transfers between devices, local(): lax.all_to_all(jnp.broadcast_to(flat, (members,) + flat.shape), ('row',)...  7.82 us
    reduce_sum x9, other arithmetic, unpack(): return (body.astype(jnp.float32), jnp.sum(wide, axis=0))  6.81 us
    unnamed x56, local copies, waits for them, and re-layouts  6.74 us
    dot_general x3, matrix products, couple(): lax.dot_general(local_tile, piece, (((0, 2), (0, 1)), ((), ())), preferre...  6.06 us
    add x8, other arithmetic, halve(): return (keep + value, note.merge(other), [n for n in names if n != name])  5.68 us
  transfers between devices with their start and end apart: 12, of which 12 were waited for; matrix products, arithmetic and copies ran while one was open for 12% of the time, Pallas kernels for 0%

profile of v3, /device:TPU:0, one launch (start us, length us, event | category | flops | bytes accessed | tf_op | source)
XLA Modules:
  0.0 165.7 jit_solution(11777195593562557468)
XLA Ops:
  4.3 10.3 %all-gather = f16[800,512]{1,0:T(8,128)(2,1)S(1)} all-gather(f16[200,512]{1,0:T(8,128)(2,1)S(1)} %pad_maximum_fusion.6), channel_id=2, replica_groups=mesh['row'=2,'core'=2,'bit2'=2,'bit1'=2,'bit0'=2] {'row','core'}, dimensions={0}, use_global_device_ids=true | all-gather | bytes 1024000 | tf_op jit(solution)/shard_map/all_gather | solution.py:163
  21.1 3.2 %bitcast_add_fusion = f32[512,3,512]{0,2,1:T(8,128)} fusion(f32[512,3,512,1]{0,2,1,3:T(8,128)S(1)} %fusion.136, bf16[3,256,512,1]{2,1,3,0:T(8,128)(2,1)S(1)} %bitcast.318, bf16[3,3,256,512]{3,2,1,0:T(8,128)(2,1)S(1)} %bitcast.298), kind=kOutput, calls=%fused_computation | convolution fusion | flops 1208745984 | bytes 9437184 | tf_op jit(solution)/shard_map/dot_general | solution.py:171
  28.3 2.4 %fusion.134 = (f32[3,2,1,2,64,256]{5,4,3,2,1,0:T(8,128)S(1)}, f32[3,2,1,2,64,256]{5,4,3,2,1,0:T(8,128)}) fusion(f32[3,2,2,2,64,512]{5,4,3,2,1,0:T(8,128)} %bitcast.300), kind=kLoop, calls=%fused_computation.339 | loop fusion | bytes 3145728 | tf_op jit(solution)/shard_map/slice | solution.py:116
  34.3 1.6 collective-permute-start.2
  35.9 2.7 %collective-permute-done = f16[776,256]{1,0:T(8,128)(2,1)} collective-permute-done((f16[776,256]{1,0:T(8,128)(2,1)}, f16[776,256]{1,0:T(8,128)(2,1)}, u32[]{:S(2)}, u32[]{:S(2)}) %collective-permute-start) | collective-permute-done | bytes 397344 | tf_op jit(solution)/shard_map/ppermute | solution.py:127
  40.3 1.6 fusion.1
  42.0 3.7 %collective-permute-done.2 = f16[776,256]{1,0:T(8,128)(2,1)} collective-permute-done((f16[776,256]{1,0:T(8,128)(2,1)}, f16[776,256]{1,0:T(8,128)(2,1)}, u32[]{:S(2)}, u32[]{:S(2)}) %collective-permute-start.2) | collective-permute-done | bytes 397344 | tf_op jit(solution)/shard_map/ppermute | solution.py:127
  46.8 1.6 collective-permute-start.1
  50.5 2.4 %collective-permute-done.1 = f16[392,256]{1,0:T(8,128)(2,1)S(1)} collective-permute-done((f16[392,256]{1,0:T(8,128)(2,1)S(1)}, f16[392,256]{1,0:T(8,128)(2,1)S(1)}, u32[]{:S(2)}, u32[]{:S(2)}) %collective-permute-start.1) | collective-permute-done | bytes 200736 | tf_op jit(solution)/shard_map/ppermute | solution.py:127
  53.0 2.8 %collective-permute-done.3 = f16[392,256]{1,0:T(8,128)(2,1)S(1)} collective-permute-done((f16[392,256]{1,0:T(8,128)(2,1)S(1)}, f16[392,256]{1,0:T(8,128)(2,1)S(1)}, u32[]{:S(2)}, u32[]{:S(2)}) %collective-permute-start.3) | collective-permute-done | bytes 200736 | tf_op jit(solution)/shard_map/ppermute | solution.py:127
  56.5 2.7 %collective-permute-start.4 = (f16[200,512]{1,0:T(8,128)(2,1)S(1)}, f16[200,512]{1,0:T(8,128)(2,1)S(1)}, u32[]{:S(2)}, u32[]{:S(2)}) collective-permute-start(f16[200,512]{1,0:T(8,128)(2,1)S(1)} %pad_maximum_fusion.7), channel_id=1, source_target_pairs={{0,4},{4,0},{1,5},{5,1},{2,6},{6,2},{3,7},{7,3},{8,12},{12,8},{9,1... | collective-permute-start | bytes 614408 | tf_op jit(solution)/shard_map/ppermute | solution.py:127
  59.2 7.6 %collective-permute-done.4 = f16[200,512]{1,0:T(8,128)(2,1)S(1)} collective-permute-done((f16[200,512]{1,0:T(8,128)(2,1)S(1)}, f16[200,512]{1,0:T(8,128)(2,1)S(1)}, u32[]{:S(2)}, u32[]{:S(2)}) %collective-permute-start.4) | collective-permute-done | bytes 204832 | tf_op jit(solution)/shard_map/ppermute | solution.py:127
  67.7 8.6 %all-gather.1 = bf16[800,512]{1,0:T(8,128)(2,1)S(1)} all-gather(bf16[200,512]{1,0:T(8,128)(2,1)S(1)} %pad_maximum_fusion.8), channel_id=3, replica_groups=mesh['row'=2,'core'=2,'bit2'=2,'bit1'=2,'bit0'=2] {'row','core'}, dimensions={0}, use_global_device_ids=true | all-gather | bytes 1024000 | tf_op jit(solution)/shard_map/all_gather | solution.py:163
  94.0 8.2 %collective-permute-done.5 = bf16[776,256]{1,0:T(8,128)(2,1)S(1)} collective-permute-done((bf16[776,256]{1,0:T(8,128)(2,1)S(1)}, bf16[776,256]{1,0:T(8,128)(2,1)S(1)}, u32[]{:S(2)}, u32[]{:S(2)}) %collective-permute-start.5) | collective-permute-done | bytes 397344 | tf_op jit(solution)/shard_map/ppermute | solution.py:127
  107.2 2.0 %collective-permute-start.7 = (bf16[776,256]{1,0:T(8,128)(2,1)}, bf16[776,256]{1,0:T(8,128)(2,1)S(1)}, u32[]{:S(2)}, u32[]{:S(2)}) collective-permute-start(bf16[776,256]{1,0:T(8,128)(2,1)} %pad_maximum_fusion.3), channel_id=1, source_target_pairs={{0,2},{2,0},{1,3},{3,1},{4,6},{6,4},{5,7},{7,5},{8,10},{10,8},{9,1... | collective-permute-start | bytes 1191944 | tf_op jit(solution)/shard_map/ppermute | solution.py:127
  109.2 5.0 %collective-permute-done.6 = bf16[392,256]{1,0:T(8,128)(2,1)S(1)} collective-permute-done((bf16[392,256]{1,0:T(8,128)(2,1)S(1)}, bf16[392,256]{1,0:T(8,128)(2,1)S(1)}, u32[]{:S(2)}, u32[]{:S(2)}) %collective-permute-start.6) | collective-permute-done | bytes 200736 | tf_op jit(solution)/shard_map/ppermute | solution.py:127
  117.4 1.6 slice.527
  119.1 2.2 %collective-permute-done.7 = bf16[776,256]{1,0:T(8,128)(2,1)S(1)} collective-permute-done((bf16[776,256]{1,0:T(8,128)(2,1)}, bf16[776,256]{1,0:T(8,128)(2,1)S(1)}, u32[]{:S(2)}, u32[]{:S(2)}) %collective-permute-start.7) | collective-permute-done | bytes 397344 | tf_op jit(solution)/shard_map/ppermute | solution.py:127
  122.0 1.5 bitcast_add_fusion.1
  127.2 3.9 %collective-permute-done.8 = bf16[392,256]{1,0:T(8,128)(2,1)S(1)} collective-permute-done((bf16[392,256]{1,0:T(8,128)(2,1)S(1)}, bf16[392,256]{1,0:T(8,128)(2,1)S(1)}, u32[]{:S(2)}, u32[]{:S(2)}) %collective-permute-start.8) | collective-permute-done | bytes 200736 | tf_op jit(solution)/shard_map/ppermute | solution.py:127
  134.5 1.5 collective-permute-start.9
  137.1 7.2 %collective-permute-done.9 = bf16[200,512]{1,0:T(8,128)(2,1)S(1)} collective-permute-done((bf16[200,512]{1,0:T(8,128)(2,1)S(1)}, bf16[200,512]{1,0:T(8,128)(2,1)S(1)}, u32[]{:S(2)}, u32[]{:S(2)}) %collective-permute-start.9) | collective-permute-done | bytes 204832 | tf_op jit(solution)/shard_map/ppermute | solution.py:127
  150.8 4.4 %all-to-all-start = ((f32[16,16,128]{2,1,0:T(8,128)}), f32[16,16,128]{2,1,0:T(8,128)}, u32[]{:S(2)}, u32[]{:S(2)}) async-start(f32[16,16,128]{2,1,0:T(8,128)} %broadcast_in_dim.2), calls=%async_computation | async-start | bytes 262144 | tf_op jit(solution)/shard_map/all_to_all | solution.py:207
  155.2 7.8 %all-to-all-done = f32[16,16,128]{2,1,0:T(8,128)} async-done(((f32[16,16,128]{2,1,0:T(8,128)}), f32[16,16,128]{2,1,0:T(8,128)}, u32[]{:S(2)}, u32[]{:S(2)}) %all-to-all-start) | async-done | bytes 131104 | tf_op jit(solution)/shard_map/all_to_all | solution.py:207
  (242 shorter events, 67.3 us)
Async XLA Ops:
  0.6 19.0 %copy-start = (bf16[3,3,4,1,64,512]{5,4,3,2,1,0:T(8,128)(2,1)S(1)}, bf16[3,3,4,1,64,512]{5,4,3,2,1,0:T(8,128)(2,1)}, u32[]{:S(2)}) copy-start(bf16[3,3,4,1,64,512]{5,4,3,2,1,0:T(8,128)(2,1)} %param.3) | copy-start | bytes 7077892
  1.8 12.8 %copy-start.14 = (f32[96,2,96]{2,1,0:T(2,128)}, f32[96,2,96]{2,1,0:T(2,128)S(1)}, u32[]{:S(2)}) copy-start(f32[96,2,96]{2,1,0:T(2,128)S(1)} %reshape.723) | copy-start | bytes 221188
  26.8 11.8 %collective-permute-start = (f16[776,256]{1,0:T(8,128)(2,1)}, f16[776,256]{1,0:T(8,128)(2,1)}, u32[]{:S(2)}, u32[]{:S(2)}) collective-permute-start(f16[776,256]{1,0:T(8,128)(2,1)} %pad_maximum_fusion), channel_id=1, source_target_pairs={{0,1},{1,0},{2,3},{3,2},{4,5},{5,4},{6,7},{7,6},{8,9},{9,8},{10,11... | collective-permute-start | bytes 1191944 | tf_op jit(solution)/shard_map/ppermute | solution.py:127
  34.3 11.5 %collective-permute-start.2 = (f16[776,256]{1,0:T(8,128)(2,1)}, f16[776,256]{1,0:T(8,128)(2,1)}, u32[]{:S(2)}, u32[]{:S(2)}) collective-permute-start(f16[776,256]{1,0:T(8,128)(2,1)} %pad_maximum_fusion.1), channel_id=1, source_target_pairs={{0,2},{2,0},{1,3},{3,1},{4,6},{6,4},{5,7},{7,5},{8,10},{10,8},{9,1... | collective-permute-start | bytes 1191944 | tf_op jit(solution)/shard_map/ppermute | solution.py:127
  39.3 7.2 %copy-start.23 = (f32[256]{0:T(256)S(1)}, f32[256]{0:T(256)}, u32[]{:S(2)}) copy-start(f32[256]{0:T(256)} %copy-done.22) | copy-start | bytes 3076
  40.3 9.1 %copy-start.1 = (f32[3,2,1,2,64,256]{5,4,3,2,1,0:T(8,128)S(1)}, f32[3,2,1,2,64,256]{5,4,3,2,1,0:T(8,128)}, u32[]{:S(2)}) copy-start(f32[3,2,1,2,64,256]{5,4,3,2,1,0:T(8,128)} %get-tuple-element.43) | copy-start | bytes 2359300
  46.8 6.2 %collective-permute-start.1 = (f16[392,256]{1,0:T(8,128)(2,1)S(1)}, f16[392,256]{1,0:T(8,128)(2,1)S(1)}, u32[]{:S(2)}, u32[]{:S(2)}) collective-permute-start(f16[392,256]{1,0:T(8,128)(2,1)S(1)} %pad_maximum_fusion.10), channel_id=1, source_target_pairs={{0,2},{2,0},{1,3},{3,1},{4,6},{6,4},{5,7},{7,5},{8,10},{10,8},{9,1... | collective-permute-start | bytes 602120 | tf_op jit(solution)/shard_map/ppermute | solution.py:127
  49.9 5.9 %collective-permute-start.3 = (f16[392,256]{1,0:T(8,128)(2,1)S(1)}, f16[392,256]{1,0:T(8,128)(2,1)S(1)}, u32[]{:S(2)}, u32[]{:S(2)}) collective-permute-start(f16[392,256]{1,0:T(8,128)(2,1)S(1)} %pad_maximum_fusion.11), channel_id=1, source_target_pairs={{0,1},{1,0},{2,3},{3,2},{4,5},{5,4},{6,7},{7,6},{8,9},{9,8},{10,11... | collective-permute-start | bytes 602120 | tf_op jit(solution)/shard_map/ppermute | solution.py:127
  56.3 10.8 %copy-start.15 = (f32[96,2,96]{2,1,0:T(2,128)S(1)}, f32[96,2,96]{2,1,0:T(2,128)}, u32[]{:S(2)}) copy-start(f32[96,2,96]{2,1,0:T(2,128)} %copy-done.14) | copy-start | bytes 221188
  56.5 10.3 %collective-permute-start.4 = (f16[200,512]{1,0:T(8,128)(2,1)S(1)}, f16[200,512]{1,0:T(8,128)(2,1)S(1)}, u32[]{:S(2)}, u32[]{:S(2)}) collective-permute-start(f16[200,512]{1,0:T(8,128)(2,1)S(1)} %pad_maximum_fusion.7), channel_id=1, source_target_pairs={{0,4},{4,0},{1,5},{5,1},{2,6},{6,2},{3,7},{7,3},{8,12},{12,8},{9,1... | collective-permute-start | bytes 614408 | tf_op jit(solution)/shard_map/ppermute | solution.py:127
  78.5 1.9 %copy-start.13 = (f32[512,3,512,1]{0,2,1,3:T(8,128)}, f32[512,3,512,1]{0,2,1,3:T(8,128)S(1)}, u32[]{:S(2)}) copy-start(f32[512,3,512,1]{0,2,1,3:T(8,128)S(1)} %fusion.137) | copy-start | bytes 9437188
  78.7 1.9 %copy-start.6 = (f32[3,2,2,1,64,256]{5,4,3,2,1,0:T(8,128)}, f32[3,2,2,1,64,256]{5,4,3,2,1,0:T(8,128)S(1)}, u32[]{:S(2)}) copy-start(f32[3,2,2,1,64,256]{5,4,3,2,1,0:T(8,128)S(1)} %get-tuple-element.39) | copy-start | bytes 2359300
  90.7 11.5 %collective-permute-start.5 = (bf16[776,256]{1,0:T(8,128)(2,1)S(1)}, bf16[776,256]{1,0:T(8,128)(2,1)S(1)}, u32[]{:S(2)}, u32[]{:S(2)}) collective-permute-start(bf16[776,256]{1,0:T(8,128)(2,1)S(1)} %pad_maximum_fusion.2), channel_id=1, source_target_pairs={{0,1},{1,0},{2,3},{3,2},{4,5},{5,4},{6,7},{7,6},{8,9},{9,8},{10,11... | collective-permute-start | bytes 1191944 | tf_op jit(solution)/shard_map/ppermute | solution.py:127
  92.8 9.4 %copy-start.5 = (f32[3,2,2,1,64,256]{5,4,3,2,1,0:T(8,128)S(1)}, f32[3,2,2,1,64,256]{5,4,3,2,1,0:T(8,128)}, u32[]{:S(2)}) copy-start(f32[3,2,2,1,64,256]{5,4,3,2,1,0:T(8,128)} %copy-done.4) | copy-start | bytes 2359300
  92.8 9.4 %copy-start.7 = (f32[3,2,2,1,64,256]{5,4,3,2,1,0:T(8,128)S(1)}, f32[3,2,2,1,64,256]{5,4,3,2,1,0:T(8,128)}, u32[]{:S(2)}) copy-start(f32[3,2,2,1,64,256]{5,4,3,2,1,0:T(8,128)} %copy-done.6) | copy-start | bytes 2359300
  106.3 7.9 %collective-permute-start.6 = (bf16[392,256]{1,0:T(8,128)(2,1)S(1)}, bf16[392,256]{1,0:T(8,128)(2,1)S(1)}, u32[]{:S(2)}, u32[]{:S(2)}) collective-permute-start(bf16[392,256]{1,0:T(8,128)(2,1)S(1)} %pad_maximum_fusion.12), channel_id=1, source_target_pairs={{0,2},{2,0},{1,3},{3,1},{4,6},{6,4},{5,7},{7,5},{8,10},{10,8},{9,1... | collective-permute-start | bytes 602120 | tf_op jit(solution)/shard_map/ppermute | solution.py:127
  107.2 14.1 %collective-permute-start.7 = (bf16[776,256]{1,0:T(8,128)(2,1)}, bf16[776,256]{1,0:T(8,128)(2,1)S(1)}, u32[]{:S(2)}, u32[]{:S(2)}) collective-permute-start(bf16[776,256]{1,0:T(8,128)(2,1)} %pad_maximum_fusion.3), channel_id=1, source_target_pairs={{0,2},{2,0},{1,3},{3,1},{4,6},{6,4},{5,7},{7,5},{8,10},{10,8},{9,1... | collective-permute-start | bytes 1191944 | tf_op jit(solution)/shard_map/ppermute | solution.py:127
  125.2 5.9 %copy-start.10 = (f32[3,2,2,64,256]{4,3,1,0,2:T(8,128)S(1)}, f32[3,2,2,64,256]{4,3,1,0,2:T(8,128)}, u32[]{:S(2)}) copy-start(f32[3,2,2,64,256]{4,3,1,0,2:T(8,128)} %copy-done.9) | copy-start | bytes 2359300
  125.3 5.8 %collective-permute-start.8 = (bf16[392,256]{1,0:T(8,128)(2,1)S(1)}, bf16[392,256]{1,0:T(8,128)(2,1)S(1)}, u32[]{:S(2)}, u32[]{:S(2)}) collective-permute-start(bf16[392,256]{1,0:T(8,128)(2,1)S(1)} %pad_maximum_fusion.13), channel_id=1, source_target_pairs={{0,1},{1,0},{2,3},{3,2},{4,5},{5,4},{6,7},{7,6},{8,9},{9,8},{10,11... | collective-permute-start | bytes 602120 | tf_op jit(solution)/shard_map/ppermute | solution.py:127
  132.6 11.8 %copy-start.16 = (f32[96,2,96]{2,1,0:T(2,128)S(1)}, f32[96,2,96]{2,1,0:T(2,128)}, u32[]{:S(2)}) copy-start(f32[96,2,96]{2,1,0:T(2,128)} %copy-done.14) | copy-start | bytes 221188
  134.5 9.8 %collective-permute-start.9 = (bf16[200,512]{1,0:T(8,128)(2,1)S(1)}, bf16[200,512]{1,0:T(8,128)(2,1)S(1)}, u32[]{:S(2)}, u32[]{:S(2)}) collective-permute-start(bf16[200,512]{1,0:T(8,128)(2,1)S(1)} %pad_maximum_fusion.9), channel_id=1, source_target_pairs={{0,4},{4,0},{1,5},{5,1},{2,6},{6,2},{3,7},{7,3},{8,12},{12,8},{9,1... | collective-permute-start | bytes 614408 | tf_op jit(solution)/shard_map/ppermute | solution.py:127
  144.4 20.4 %copy-start.12 = (f32[2,3,32,512]{3,2,0,1:T(8,128)S(1)}, f32[2,3,32,512]{3,2,0,1:T(8,128)}, u32[]{:S(2)}) copy-start(f32[2,3,32,512]{3,2,0,1:T(8,128)} %copy-done.11) | copy-start | bytes 1179652
  148.9 1.2 collective-permute-start.10
  150.8 12.2 %all-to-all-start = ((f32[16,16,128]{2,1,0:T(8,128)}), f32[16,16,128]{2,1,0:T(8,128)}, u32[]{:S(2)}, u32[]{:S(2)}) async-start(f32[16,16,128]{2,1,0:T(8,128)} %broadcast_in_dim.2), calls=%async_computation | async-start | bytes 262144 | tf_op jit(solution)/shard_map/all_to_all | solution.py:207
  (16 other events, 18.8 us)

commit v4 on v0

v4 whole, which is shorter than its diff:
```python
import functools

import jax
import jax.numpy as jnp
from jax import lax
from jax.experimental import pallas as pl
from jax.experimental.pallas import tpu as pltpu
from jax.sharding import Mesh, PartitionSpec as P

FIBER_NODES = 32
PIECES = 3
EXTRA = 16
NOTE = 8
SWAP = [(0, 1), (1, 0)]
TINY = 1e-06
F32 = jnp.float32
BF16 = jnp.bfloat16


def least_squares(beta, h_one_one, h_two_one, h_one_two, h_two_two, h_three_two):
    rho_one = jnp.sqrt(h_one_one * h_one_one + h_two_one * h_two_one)
    cos_one = h_one_one / rho_one
    sin_one = h_two_one / rho_one
    g_one = cos_one * beta
    g_two = -sin_one * beta
    top = cos_one * h_one_two + sin_one * h_two_two
    low = cos_one * h_two_two - sin_one * h_one_two
    rho_two = jnp.sqrt(low * low + h_three_two * h_three_two)
    cos_two = low / rho_two
    sin_two = h_three_two / rho_two
    y_two = cos_two * g_two / rho_two
    y_one = (g_one - top * y_two) / rho_one
    return (y_one, y_two, jnp.abs(sin_two * g_two))


def stack_rows(rows, count):
    blank = jnp.zeros_like(rows[0])
    return jnp.concatenate(list(rows) + [blank] * (count - len(rows)), axis=0)


class Scale:
    sent = F32

    def __init__(self, size):
        factors = []
        scale = jnp.ones_like(size)
        rest = size
        for _ in range(PIECES):
            factor = jnp.clip(rest, 2.0**-13, 2.0**15).astype(BF16).astype(F32)
            factors.append(factor)
            scale = scale * factor
            rest = rest / factor
        self.scale = scale
        self.inverse = 1.0 / scale
        self.packed = stack_rows(factors, EXTRA)

    def pack(self, body):
        return body * self.inverse

    @staticmethod
    def read(rows):
        return rows[0:1] * rows[1:2] * rows[2:3]

    @staticmethod
    def unpack(body, other):
        return body * other

    @classmethod
    def load(cls, note):
        return cls(note[0:1, :])

    def merge(self, other):
        return Scale(jnp.maximum(self.scale, other))

    def rows(self):
        return stack_rows([self.scale], NOTE)


class Sums:
    sent = BF16

    def __init__(self, total):
        pieces = []
        rest = total
        for _ in range(PIECES):
            piece = rest.astype(BF16).astype(F32)
            pieces.append(piece)
            rest = rest - piece
        self.total = total
        self.packed = stack_rows(pieces, EXTRA).astype(BF16) if total.shape[0] == 1 else stack_rows(
            [piece[k : k + 1] for piece in pieces for k in range(2)], EXTRA
        ).astype(BF16)

    def pack(self, body):
        return body.astype(BF16)

    @staticmethod
    def read(rows):
        wide = rows.astype(F32)
        return wide[0:2] + wide[2:4] + wide[4:6]

    @staticmethod
    def unpack(body, other):
        return body.astype(F32)

    @classmethod
    def load(cls, note):
        return cls(note[0:2, :])

    def merge(self, other):
        return Sums(self.total + other)

    def rows(self):
        return stack_rows([self.total[0:1], self.total[1:2]], NOTE)


def insert(slot, place, side):
    low = slot & ((1 << place) - 1)
    return ((slot >> place) << (place + 1)) + (side << place) + low


def blocks_times(precond, value):
    width = 3 * FIBER_NODES
    fibers = precond.shape[1] // width
    nodes = fibers * FIBER_NODES
    results = []
    for fiber in range(fibers):
        parts = []
        for comp in range(3):
            first = comp * nodes + fiber * FIBER_NODES
            parts.append(value[first : first + FIBER_NODES])
        column = jnp.concatenate(parts, axis=0)
        blank = jnp.zeros_like(column)
        tall = [column if k == fiber else blank for k in range(fibers)]
        results.append(
            jnp.dot(
                precond,
                jnp.concatenate(tall, axis=0),
                precision=lax.Precision.HIGHEST,
                preferred_element_type=F32,
            )
        )
    parts = []
    for comp in range(3):
        for fiber in range(fibers):
            parts.append(results[fiber][comp * FIBER_NODES : (comp + 1) * FIBER_NODES])
    return jnp.concatenate(parts, axis=0)


def row_sum(first, second):
    return jnp.sum(first * second, axis=0, keepdims=True)


def first_body(right_ref, precond_ref, start_ref, sent_ref):
    height = start_ref.shape[0]
    start = blocks_times(precond_ref[...], right_ref[...])
    start_ref[...] = start
    note = Scale(jnp.max(jnp.abs(start), axis=0, keepdims=True))
    sent_ref[0:height] = note.pack(start)
    sent_ref[height:] = note.packed


def couple_body(kind, places, sides_ref, tile_ref, got_ref, *refs):
    sends, keeps, note_ref, work_ref = refs[0:2], refs[2:4], refs[4], refs[5]
    sources = got_ref.shape[0]
    height = got_ref.shape[1] - EXTRA
    nodes = height // 3
    cases = got_ref.shape[2]
    half = cases // 2
    targets = tile_ref.shape[3] // nodes
    others = [kind.read(got_ref[k, height:]) for k in range(sources)]
    blocks = []
    for comp in range(3):
        for k in range(sources):
            block = got_ref[k, comp * nodes : (comp + 1) * nodes]
            if kind is Scale:
                block = block * others[k]
            blocks.append(block)
    value = jnp.concatenate(blocks, axis=0)
    terms = [value.astype(BF16)]
    if kind is Scale:
        note = Scale(functools.reduce(jnp.maximum, others))
        terms.append((value - terms[0].astype(F32)).astype(BF16))
    else:
        note = Sums(functools.reduce(jnp.add, others))
    note_ref[...] = note.rows()
    for comp in range(3):
        left = tile_ref[:, comp].reshape(value.shape[0], targets * nodes)
        total = 0.0
        for term in terms:
            total = total + lax.dot_general(
                left, term, (((0,), (0,)), ((), ())), preferred_element_type=F32
            )
        work_ref[comp] = total
    for colour in range(2):
        first = colour * half
        columns = slice(first, first + half)
        side = sides_ref[colour]
        inner_note = type(note).load(note_ref[:, columns])
        for slot in range(targets // 2):
            give = insert(slot, places[colour], 1 - side) * nodes
            keep = insert(slot, places[colour], side) * nodes
            for comp in range(3):
                row = slot * height + comp * nodes
                value = work_ref[comp, pl.ds(pl.multiple_of(give, nodes), nodes), columns]
                sends[colour][row : row + nodes] = inner_note.pack(value)
                value = work_ref[comp, pl.ds(pl.multiple_of(keep, nodes), nodes), columns]
                keeps[colour][row : row + nodes] = value
        sends[colour][targets // 2 * height :] = inner_note.packed


def merge_body(kind, places, joined, height, sides_ref, note_ref, *refs):
    kept, got, outs, next_ref = refs[0:2], refs[2:4], refs[4:-1], refs[-1]
    half = kept[0].shape[1]
    slots = kept[0].shape[0] // height
    for colour in range(2):
        columns = slice(colour * half, (colour + 1) * half)
        side = sides_ref[colour]
        other = kind.read(got[colour][slots * height :])
        note = kind.load(note_ref[:, columns]).merge(other)
        next_ref[:, columns] = note.rows()
        for slot in range(slots // 2):
            rows = slice(slot * height, (slot + 1) * height)
            give = pl.ds(pl.multiple_of(insert(slot, places[colour], 1 - side) * height, height), height)
            keep = pl.ds(pl.multiple_of(insert(slot, places[colour], side) * height, height), height)
            given = note.pack(kept[colour][give] + kind.unpack(got[colour][give], other))
            held = kept[colour][keep] + kind.unpack(got[colour][keep], other)
            if joined:
                outs[0][rows, columns] = given
                outs[1][rows, columns] = held
            else:
                outs[colour][rows] = given
                outs[2 + colour][rows] = held
        if joined:
            outs[0][slots // 2 * height :, columns] = note.packed
        else:
            outs[colour][slots // 2 * height :] = note.packed


def second_body(kept_ref, got_ref, start_ref, precond_ref, work_ref, sent_ref):
    height = start_ref.shape[0]
    other = Scale.read(got_ref[height:])
    start = start_ref[...]
    moved = start + (kept_ref[...] + Scale.unpack(got_ref[0:height], other))
    work = blocks_times(precond_ref[...], moved)
    work_ref[...] = work
    note = Sums(jnp.concatenate([row_sum(start, start), row_sum(start, work)], axis=0))
    sent_ref[0:height] = note.pack(work)
    sent_ref[height:] = note.packed


def third_body(kept_ref, got_ref, note_ref, start_ref, work_ref, precond_ref, side_ref, gram_ref, next_ref):
    height = start_ref.shape[0]
    note = Sums.load(note_ref[...]).merge(Sums.read(got_ref[height:]))
    next_ref[...] = note.rows()
    start = start_ref[...]
    work = work_ref[...]
    moved = work + (kept_ref[...] + got_ref[0:height].astype(F32))
    h_one_one = note.total[1:2] / (note.total[0:1] + TINY)
    other = blocks_times(precond_ref[...], moved) - h_one_one * work
    side = work - h_one_one * start
    side_ref[...] = side
    pairs = [(side, side), (start, other), (side, other), (other, other)]
    rows = [row_sum(*pair) for pair in pairs]
    width = gram_ref.shape[1]
    count = rows[0].shape[1] // width
    parts = [row[:, k * width : (k + 1) * width] for row in rows for k in range(count)]
    gram_ref[...] = jnp.concatenate(parts, axis=0)


def last_body(flat_ref, note_ref, start_ref, side_ref, solution_ref, arnoldi_ref):
    total = jnp.sum(flat_ref[...], axis=0)
    count = total.shape[0] // 4
    gram = [
        jnp.concatenate([total[k * count + q : k * count + q + 1] for q in range(count)], axis=1)
        for k in range(4)
    ]
    side_side, start_other, side_other, other_other = gram
    square = note_ref[0:1, :] + TINY
    beta = jnp.sqrt(square)
    h_one_one = note_ref[1:2, :] / square
    h_two_one = jnp.sqrt(side_side / square + TINY)
    length = beta * h_two_one
    h_one_two = start_other / (beta * length)
    h_two_two = side_other / (length * length)
    loss_one = TINY / square
    loss_two = TINY / (h_two_one * h_two_one)
    one_two = h_one_one * loss_one / h_two_one
    rest = (
        other_other / (length * length)
        - h_one_two * h_one_two * (1.0 + loss_one)
        - h_two_two * h_two_two * (1.0 + loss_two)
        + 2.0 * h_one_two * h_two_two * one_two
    )
    h_three_two = jnp.sqrt(jnp.maximum(rest, 0.0) + TINY)
    y_one, y_two, estimate = least_squares(
        beta, h_one_one, h_two_one, h_one_two, h_two_two, h_three_two
    )
    solution_ref[...] = (y_one / beta) * start_ref[...] + (y_two / length) * side_ref[...]
    rows = [h_one_one, h_one_two, h_two_one, h_two_two, estimate, h_three_two]
    arnoldi_ref[...] = jnp.concatenate(rows, axis=0)


def call(body, shapes, *args, scalars=0, scratch=()):
    spec = pl.BlockSpec(memory_space=pltpu.VMEM)
    small = pl.BlockSpec(memory_space=pltpu.SMEM)
    return pl.pallas_call(
        body,
        out_shape=[jax.ShapeDtypeStruct(shape, dtype) for shape, dtype in shapes],
        in_specs=[small] * scalars + [spec] * (len(args) - scalars),
        out_specs=[spec] * len(shapes),
        scratch_shapes=list(scratch),
        compiler_params=pltpu.CompilerParams(vmem_limit_bytes=56 * 1024 * 1024),
    )(*args)


def travel(array, kind, move):
    if kind is Scale:
        return move(array.astype(jnp.float16)).astype(F32)
    return move(array)


def build(bits):
    lower = bits[1:]
    orders = (list(reversed(lower)), list(lower))

    def local(mobility, right_side, precond):
        row_count = mobility.shape[5]
        sources = mobility.shape[2]
        node_dev = mobility.shape[4]
        cases = right_side.shape[2]
        height = 3 * node_dev
        half = cases // 2
        tile = mobility.reshape(3, 3, sources * node_dev, row_count)
        right = right_side.reshape(height, cases)

        def sides(names):
            return jnp.stack([lax.axis_index(name).astype(jnp.int32) for name in names])

        def gather(sent, kind):
            return travel(sent, kind, lambda a: lax.all_gather(a, ("row", "core")))

        def exchange(got, kind):
            left = [list(bits), list(bits)]
            slots = row_count // node_dev
            for step in range(len(lower) + 1):
                joined = step == len(lower)
                names = [bits[0]] * 2 if joined else [orders[0][step], orders[1][step]]
                places = [len(left[k]) - 1 - left[k].index(names[k]) for k in range(2)]
                slots = slots // 2
                tall = slots * height
                note = ((NOTE, cases), F32)
                if step == 0:
                    shapes = [((tall + EXTRA, half), kind.sent)] * 2 + [((tall, half), F32)] * 2
                    outs = call(
                        functools.partial(couple_body, kind, places),
                        shapes + [note],
                        sides(names),
                        tile,
                        got,
                        scalars=1,
                        scratch=[pltpu.VMEM((3, row_count, cases), F32)],
                    )
                else:
                    shapes = [((tall + EXTRA, half), kind.sent)] * 2 + [((tall, half), F32)] * 2
                    if joined:
                        shapes = [((tall + EXTRA, cases), kind.sent), ((tall, cases), F32)]
                    outs = call(
                        functools.partial(merge_body, kind, places, joined, height),
                        shapes + [note],
                        sides(names),
                        notes,
                        *kept,
                        *arrived,
                        scalars=1,
                    )
                notes = outs[-1]
                for k in range(2):
                    left[k].remove(names[k])
                if joined:
                    move = lambda a: lax.ppermute(a, bits[0], SWAP)
                    return outs[1], travel(outs[0], kind, move), notes
                kept = outs[2:4]
                casts = [a.astype(jnp.float16) if kind is Scale else a for a in outs[0:2]]
                moved = [lax.ppermute(a, name, SWAP) for a, name in zip(casts, names)]
                arrived = [a.astype(F32) if kind is Scale else a for a in moved]

        full = ((height, cases), F32)
        start, sent = call(first_body, [full, ((height + EXTRA, cases), F32)], right, precond)
        kept, got, _ = exchange(gather(sent, Scale), Scale)
        work, sent = call(
            second_body, [full, ((height + EXTRA, cases), BF16)], kept, got, start, precond
        )
        kept, got, notes = exchange(gather(sent, Sums), Sums)
        side, flat, notes = call(
            third_body,
            [full, ((4 * cases // 128, 128), F32), ((NOTE, cases), F32)],
            kept,
            got,
            notes,
            start,
            work,
            precond,
        )
        flat = flat + lax.ppermute(flat, "core", SWAP)
        members = sources // 2 * 2 ** len(bits)
        flat = lax.all_to_all(
            jnp.broadcast_to(flat, (members,) + flat.shape), ("row",) + tuple(bits), 0, 0
        )
        answer, arnoldi = call(last_body, [full, ((6, cases), F32)], flat, notes, start, side)
        return answer.reshape(3, node_dev, cases), arnoldi.reshape(3, 2, cases)

    return local


def solution(mesh):
    count_tgt, count_src = mesh.shape["tgt"], mesh.shape["src"]
    depth = count_src.bit_length() - 1
    bits = ["bit%d" % k for k in reversed(range(depth))]
    tgt = ("row", "core")
    src = tuple(bits)
    grid = mesh.devices.reshape((count_tgt // 2, 2) + (2,) * depth)
    placed = (
        P(None, None, None, src, None, tgt),
        P(None, tgt + src, None),
        P(None, tgt + src),
    )
    return jax.shard_map(
        build(bits),
        mesh=Mesh(grid, tgt + src),
        in_specs=placed,
        out_specs=(P(None, tgt + src, None), P()),
        check_vma=False,
    )
```

time: 449 us -> 143 us (0.32)
  blocking collectives: 260 us -> 32.6 us
  waiting for transfers between devices: 147 us -> 46.9 us
  Pallas kernels: 0 us -> 31.5 us
  between operations: 14.2 us -> 0.68 us
  starting transfers between devices: 0.08 us -> 12.6 us
  matrix products: 9.42 us -> 0 us
    psum x6 -> x0, blocking collectives: 241 us -> none  [the longest x1 42 us: local(): beta = jnp.sqrt(lax.psum(inner(initial, initial), ('tgt', 'src')) + 1e-06)]
    reduce_scatter x2 -> x0, waiting for transfers between devices: 147 us -> none  [operate(): lax.psum_scatter(partial_value, 'src', scatter_dimension=1, tiled=True)]
    ppermute x0 -> x11, waiting for transfers between devices: none -> 46.9 us  [the longest x8 28.6 us: exchange(): moved = [lax.ppermute(a, name, SWAP) for a, name in zip(casts, names)]]
    pallas_call x0 -> x10, Pallas kernels: none -> 31.5 us  [call(): pl.pallas_call(body, out_shape=[jax.ShapeDtypeStruct(shape, dtype) for sh...]
    ppermute x0 -> x11, starting transfers between devices: none -> 12.6 us  [the longest x8 7.57 us: exchange(): moved = [lax.ppermute(a, name, SWAP) for a, name in zip(casts, names)]]
    all_to_all x0 -> x1, blocking collectives: none -> 12.4 us  [local(): lax.all_to_all(jnp.broadcast_to(flat, (members,) + flat.shape), ('row',)...]
    convert_element_type x2 -> x12, other arithmetic: 1.88 us -> 12.3 us  [the longest x4 4.45 us: exchange(): casts = [a.astype(jnp.float16) if kind is Scale else a for a in outs[0:2]]]
    dot_general x5 -> x0, matrix products: 9.42 us -> none  [the longest x2 6.2 us: accumulate(): lax.dot_general(local_tile, piece, (((0, 2), (0, 1)), ((), ())), preferre...]
  transfers between devices with their start and end apart: 2 -> 11, of which waited for: 2 -> 11; matrix products, arithmetic and copies ran while one was open for 0% -> 4% of each run, Pallas kernels for 0% -> 0%
where the time goes in v4:
time: 143 us
  waiting for transfers between devices  46.9 us (33%)
  blocking collectives  32.6 us (23%)
  Pallas kernels  31.5 us (22%)
  other arithmetic  14.9 us (10%)
  starting transfers between devices  12.6 us (9%)
  local copies, waits for them, and re-layouts  3.45 us (2%)
    pallas_call x10, Pallas kernels, call(): pl.pallas_call(body, out_shape=[jax.ShapeDtypeStruct(shape, dtype) for sh...  31.5 us
    ppermute x8, waiting for transfers between devices, exchange(): moved = [lax.ppermute(a, name, SWAP) for a, name in zip(casts, names)]  28.6 us
    all_gather x2, blocking collectives, gather(): return travel(sent, kind, lambda a: lax.all_gather(a, ('row', 'core')))  20.2 us
    ppermute x2, waiting for transfers between devices, exchange(): move = lambda a: lax.ppermute(a, bits[0], SWAP)  17 us
    all_to_all x1, blocking collectives, local(): lax.all_to_all(jnp.broadcast_to(flat, (members,) + flat.shape), ('row',)...  12.4 us
    ppermute x8, starting transfers between devices, exchange(): moved = [lax.ppermute(a, name, SWAP) for a, name in zip(casts, names)]  7.57 us
    ppermute x2, starting transfers between devices, exchange(): move = lambda a: lax.ppermute(a, bits[0], SWAP)  5 us
    convert_element_type x4, other arithmetic, exchange(): casts = [a.astype(jnp.float16) if kind is Scale else a for a in outs[0:2]]  4.45 us
  transfers between devices with their start and end apart: 11, of which 11 were waited for; matrix products, arithmetic and copies ran while one was open for 4% of the time, Pallas kernels for 0%

profile of v4, /device:TPU:0, one launch (start us, length us, event | category | flops | bytes accessed | tf_op | source)
XLA Modules:
  0.0 142.6 jit_solution(14186324872690939517)
XLA Ops:
  0.6 2.4 %shard_map.50 = (f32[192,512]{1,0:T(8,128)}, f32[208,512]{1,0:T(8,128)}) custom-call(f32[192,512]{1,0:T(8,128)} %bitcast.13, f32[96,192]{1,0:T(8,128)} %precond_ref.5), custom_call_target="tpu_custom_call" | custom-call | tf_op jit(solution)/shard_map/pallas_call | solution.py:307
  4.1 10.5 %all-gather = f16[832,512]{1,0:T(8,128)(2,1)S(1)} all-gather(f16[208,512]{1,0:T(8,128)(2,1)S(1)} %convert_element_type.36), channel_id=2, replica_groups=mesh['row'=2,'core'=2,'bit2'=2,'bit1'=2,'bit0'=2] {'row','core'}, dimensions={0}, use_global_device_ids=true | all-gather | bytes 1064960 | tf_op jit(solution)/shard_map/all_gather | solution.py:341
  16.6 6.6 %shard_map.51 = (f32[784,256]{1,0:T(8,128)}, f32[784,256]{1,0:T(8,128)}, f32[768,256]{1,0:T(8,128)}, f32[768,256]{1,0:T(8,128)}, f32[8,512]{1,0:T(8,128)}) custom-call(s32[2]{0:T(128)} %pad_add_fusion.2.sides_ref, bf16[3,3,256,512]{3,2,1,0:T(8,128)(2,1)} %bitcast.9, f32[4,208,512]{2,1,0:T(8,128)} %convert.got_ref), custom_call_target="tpu_custom_call" | custom-call | tf_op jit(solution)/shard_map/pallas_call | solution.py:307
  24.4 1.6 %collective-permute-start.1 = (f16[784,256]{1,0:T(8,128)(2,1)S(1)}, f16[784,256]{1,0:T(8,128)(2,1)S(1)}, u32[]{:S(2)}, u32[]{:S(2)}) collective-permute-start(f16[784,256]{1,0:T(8,128)(2,1)S(1)} %convert_element_type.40), channel_id=1, source_target_pairs={{0,2},{2,0},{1,3},{3,1},{4,6},{6,4},{5,7},{7,5},{8,10},{10,8},{9,1... | collective-permute-start | bytes 1204232 | tf_op jit(solution)/shard_map/ppermute | solution.py:385
  27.2 1.6 %collective-permute-start = (f16[784,256]{1,0:T(8,128)(2,1)S(1)}, f16[784,256]{1,0:T(8,128)(2,1)S(1)}, u32[]{:S(2)}, u32[]{:S(2)}) collective-permute-start(f16[784,256]{1,0:T(8,128)(2,1)S(1)} %convert_element_type.38), channel_id=1, source_target_pairs={{0,1},{1,0},{2,3},{3,2},{4,5},{5,4},{6,7},{7,6},{8,9},{9,8},{10,11... | collective-permute-start | bytes 1204232 | tf_op jit(solution)/shard_map/ppermute | solution.py:385
  29.4 6.6 %collective-permute-done.1 = f16[784,256]{1,0:T(8,128)(2,1)S(1)} collective-permute-done((f16[784,256]{1,0:T(8,128)(2,1)S(1)}, f16[784,256]{1,0:T(8,128)(2,1)S(1)}, u32[]{:S(2)}, u32[]{:S(2)}) %collective-permute-start.1) | collective-permute-done | bytes 401440 | tf_op jit(solution)/shard_map/ppermute | solution.py:385
  37.0 1.6 %collective-permute-done = f16[784,256]{1,0:T(8,128)(2,1)S(1)} collective-permute-done((f16[784,256]{1,0:T(8,128)(2,1)S(1)}, f16[784,256]{1,0:T(8,128)(2,1)S(1)}, u32[]{:S(2)}, u32[]{:S(2)}) %collective-permute-start) | collective-permute-done | bytes 401440 | tf_op jit(solution)/shard_map/ppermute | solution.py:385
  39.5 3.2 %shard_map.52 = (f32[400,256]{1,0:T(8,128)}, f32[400,256]{1,0:T(8,128)}, f32[384,256]{1,0:T(8,128)}, f32[384,256]{1,0:T(8,128)}, f32[8,512]{1,0:T(8,128)}) custom-call(s32[2]{0:T(128)} %pad_add_fusion.1.sides_ref, f32[8,512]{1,0:T(8,128)} %get-tuple-element.37.note_ref, f32[768,256]{1,0:T(8,128)} %get-tuple-element.38.refs_0_, ...), custom_call_target="tpu_custom_call" | custom-call | tf_op jit(solution)/shard_map/pallas_call | solution.py:307
  47.4 2.6 %collective-permute-done.3 = f16[400,256]{1,0:T(8,128)(2,1)S(1)} collective-permute-done((f16[400,256]{1,0:T(8,128)(2,1)S(1)}, f16[400,256]{1,0:T(8,128)(2,1)S(1)}, u32[]{:S(2)}, u32[]{:S(2)}) %collective-permute-start.3) | collective-permute-done | bytes 204832 | tf_op jit(solution)/shard_map/ppermute | solution.py:385
  53.1 2.3 %shard_map.53 = (f32[208,512]{1,0:T(8,128)}, f32[192,512]{1,0:T(8,128)}, f32[8,512]{1,0:T(8,128)}) custom-call(s32[2]{0:T(128)} %pad_add_fusion.sides_ref, f32[8,512]{1,0:T(8,128)} %get-tuple-element.42.note_ref, f32[384,256]{1,0:T(8,128)} %get-tuple-element.43.refs_0_, f32[384,256]{1,0:T(8,128)} %get-tuple-element.44.refs_1_, ...), custom_call_target="tpu_custom_call" | custom-call | tf_op jit(solution)/shard_map/pallas_call | solution.py:307
  56.5 2.7 %collective-permute-start.4 = (f16[208,512]{1,0:T(8,128)(2,1)S(1)}, f16[208,512]{1,0:T(8,128)(2,1)S(1)}, u32[]{:S(2)}, u32[]{:S(2)}) collective-permute-start(f16[208,512]{1,0:T(8,128)(2,1)S(1)} %convert_element_type.46), channel_id=1, source_target_pairs={{0,4},{4,0},{1,5},{5,1},{2,6},{6,2},{3,7},{7,3},{8,12},{12,8},{9,1... | collective-permute-start | bytes 638984 | tf_op jit(solution)/shard_map/ppermute | solution.py:381
  59.1 8.0 %collective-permute-done.4 = f16[208,512]{1,0:T(8,128)(2,1)S(1)} collective-permute-done((f16[208,512]{1,0:T(8,128)(2,1)S(1)}, f16[208,512]{1,0:T(8,128)(2,1)S(1)}, u32[]{:S(2)}, u32[]{:S(2)}) %collective-permute-start.4) | collective-permute-done | bytes 213024 | tf_op jit(solution)/shard_map/ppermute | solution.py:381
  67.9 2.6 %shard_map.54 = (f32[192,512]{1,0:T(8,128)}, bf16[208,512]{1,0:T(8,128)(2,1)}) custom-call(f32[192,512]{1,0:T(8,128)} %get-tuple-element.47.kept_ref, f32[208,512]{1,0:T(8,128)} %convert_element_type.47.got_ref, f32[192,512]{1,0:T(8,128)} %get-tuple-element.49.start_ref, f32[96,192]{1,0:T(8,128)} %precond_ref.5), custom_call_target="tpu_custom_call" | custom-call | tf_op jit(solution)/shard_map/pallas_call | solution.py:307
  70.5 9.7 %all-gather.1 = bf16[832,512]{1,0:T(8,128)(2,1)} all-gather(bf16[208,512]{1,0:T(8,128)(2,1)} %get-tuple-element.50), channel_id=3, replica_groups=mesh['row'=2,'core'=2,'bit2'=2,'bit1'=2,'bit0'=2] {'row','core'}, dimensions={0}, use_global_device_ids=true | all-gather | bytes 1064960 | tf_op jit(solution)/shard_map/all_gather | solution.py:341
  80.2 4.8 %shard_map.55 = (bf16[784,256]{1,0:T(8,128)(2,1)}, bf16[784,256]{1,0:T(8,128)(2,1)}, f32[768,256]{1,0:T(8,128)}, f32[768,256]{1,0:T(8,128)}, f32[8,512]{1,0:T(8,128)}) custom-call(s32[2]{0:T(128)} %pad_add_fusion.2.sides_ref, bf16[3,3,256,512]{3,2,1,0:T(8,128)(2,1)} %bitcast.10, bf16[4,208,512]{2,1,0:T(8,128)(2,1)} %bitcast.12), custom_call_target="tpu_custom_call" | custom-call | tf_op jit(solution)/shard_map/pallas_call | solution.py:307
  85.5 11.2 %collective-permute-done.5.refs_2_ = bf16[784,256]{1,0:T(8,128)(2,1)S(1)} collective-permute-done((bf16[784,256]{1,0:T(8,128)(2,1)}, bf16[784,256]{1,0:T(8,128)(2,1)S(1)}, u32[]{:S(2)}, u32[]{:S(2)}) %collective-permute-start.5) | collective-permute-done | bytes 401440 | tf_op jit(solution)/shard_map/ppermute | solution.py:385
  97.8 2.8 %shard_map.56 = (bf16[400,256]{1,0:T(8,128)(2,1)}, bf16[400,256]{1,0:T(8,128)(2,1)}, f32[384,256]{1,0:T(8,128)}, f32[384,256]{1,0:T(8,128)}, f32[8,512]{1,0:T(8,128)}) custom-call(s32[2]{0:T(128)} %pad_add_fusion.1.sides_ref, f32[8,512]{1,0:T(8,128)} %get-tuple-element.51.note_ref, f32[768,256]{1,0:T(8,128)} %get-tuple-element.52.refs_0_, ...), custom_call_target="tpu_custom_call" | custom-call | tf_op jit(solution)/shard_map/pallas_call | solution.py:307
  102.3 4.8 %collective-permute-done.7.refs_2_ = bf16[400,256]{1,0:T(8,128)(2,1)S(1)} collective-permute-done((bf16[400,256]{1,0:T(8,128)(2,1)}, bf16[400,256]{1,0:T(8,128)(2,1)S(1)}, u32[]{:S(2)}, u32[]{:S(2)}) %collective-permute-start.7) | collective-permute-done | bytes 204832 | tf_op jit(solution)/shard_map/ppermute | solution.py:385
  107.9 2.2 %shard_map.57 = (bf16[208,512]{1,0:T(8,128)(2,1)}, f32[192,512]{1,0:T(8,128)}, f32[8,512]{1,0:T(8,128)}) custom-call(s32[2]{0:T(128)} %pad_add_fusion.sides_ref, f32[8,512]{1,0:T(8,128)} %get-tuple-element.56.note_ref, f32[384,256]{1,0:T(8,128)} %get-tuple-element.57.refs_0_, f32[384,256]{1,0:T(8,128)} %get-tuple-element.58.refs_1_, ...), custom_call_target="tpu_custom_call" | custom-call | tf_op jit(solution)/shard_map/pallas_call | solution.py:307
  110.1 2.3 %collective-permute-start.9 = (bf16[208,512]{1,0:T(8,128)(2,1)}, bf16[208,512]{1,0:T(8,128)(2,1)S(1)}, u32[]{:S(2)}, u32[]{:S(2)}) collective-permute-start(bf16[208,512]{1,0:T(8,128)(2,1)} %get-tuple-element.62), channel_id=1, source_target_pairs={{0,4},{4,0},{1,5},{5,1},{2,6},{6,2},{3,7},{7,3},{8,12},{12,8},{9,1... | collective-permute-start | bytes 638984 | tf_op jit(solution)/shard_map/ppermute | solution.py:381
  112.4 9.0 %collective-permute-done.9.got_ref = bf16[208,512]{1,0:T(8,128)(2,1)S(1)} collective-permute-done((bf16[208,512]{1,0:T(8,128)(2,1)}, bf16[208,512]{1,0:T(8,128)(2,1)S(1)}, u32[]{:S(2)}, u32[]{:S(2)}) %collective-permute-start.9) | collective-permute-done | bytes 213024 | tf_op jit(solution)/shard_map/ppermute | solution.py:381
  122.1 2.6 %shard_map.58 = (f32[192,512]{1,0:T(8,128)}, f32[16,128]{1,0:T(8,128)}, f32[8,512]{1,0:T(8,128)}) custom-call(f32[192,512]{1,0:T(8,128)} %get-tuple-element.61.kept_ref, bf16[208,512]{1,0:T(8,128)(2,1)} %copy-done.2, f32[8,512]{1,0:T(8,128)} %get-tuple-element.63.note_ref, f32[192,512]{1,0:T(8,128)} %get-tuple-element.49.start_ref, ...), custom_call_target="tpu_custom_call" | custom-call | tf_op jit(solution)/shard_map/pallas_call | solution.py:307
  126.8 12.4 %all_to_all.5.flat_ref = f32[16,16,128]{2,1,0:T(8,128)} all-to-all(f32[16,16,128]{2,1,0:T(8,128)S(1)} %broadcast_in_dim.3), channel_id=1, replica_groups=mesh['row'=2,'core'=2,'bit2'=2,'bit1'=2,'bit0'=2] {'row','bit2','bit1','..., dimensions={0} | all-to-all | bytes 262144 | tf_op jit(solution)/shard_map/all_to_all | solution.py:407
  139.2 2.1 %shard_map.59 = (f32[192,512]{1,0:T(8,128)}, f32[6,512]{1,0:T(8,128)}) custom-call(f32[16,16,128]{2,1,0:T(8,128)} %all_to_all.5.flat_ref, f32[8,512]{1,0:T(8,128)} %get-tuple-element.66.note_ref, f32[192,512]{1,0:T(8,128)} %get-tuple-element.49.start_ref, f32[192,512]{1,0:T(8,128)} %get-tuple-element.67.side_ref), custom_call_target="tpu_custom_call" | custom-call | tf_op jit(solution)/shard_map/pallas_call | solution.py:307
  (39 shorter events, 25.9 us)
Async XLA Ops:
  24.4 11.6 %collective-permute-start.1 = (f16[784,256]{1,0:T(8,128)(2,1)S(1)}, f16[784,256]{1,0:T(8,128)(2,1)S(1)}, u32[]{:S(2)}, u32[]{:S(2)}) collective-permute-start(f16[784,256]{1,0:T(8,128)(2,1)S(1)} %convert_element_type.40), channel_id=1, source_target_pairs={{0,2},{2,0},{1,3},{3,1},{4,6},{6,4},{5,7},{7,5},{8,10},{10,8},{9,1... | collective-permute-start | bytes 1204232 | tf_op jit(solution)/shard_map/ppermute | solution.py:385
  27.2 11.3 %collective-permute-start = (f16[784,256]{1,0:T(8,128)(2,1)S(1)}, f16[784,256]{1,0:T(8,128)(2,1)S(1)}, u32[]{:S(2)}, u32[]{:S(2)}) collective-permute-start(f16[784,256]{1,0:T(8,128)(2,1)S(1)} %convert_element_type.38), channel_id=1, source_target_pairs={{0,1},{1,0},{2,3},{3,2},{4,5},{5,4},{6,7},{7,6},{8,9},{9,8},{10,11... | collective-permute-start | bytes 1204232 | tf_op jit(solution)/shard_map/ppermute | solution.py:385
  43.7 6.3 %collective-permute-start.3 = (f16[400,256]{1,0:T(8,128)(2,1)S(1)}, f16[400,256]{1,0:T(8,128)(2,1)S(1)}, u32[]{:S(2)}, u32[]{:S(2)}) collective-permute-start(f16[400,256]{1,0:T(8,128)(2,1)S(1)} %convert_element_type.44), channel_id=1, source_target_pairs={{0,1},{1,0},{2,3},{3,2},{4,5},{5,4},{6,7},{7,6},{8,9},{9,8},{10,11... | collective-permute-start | bytes 614408 | tf_op jit(solution)/shard_map/ppermute | solution.py:385
  46.3 6.0 %collective-permute-start.2 = (f16[400,256]{1,0:T(8,128)(2,1)S(1)}, f16[400,256]{1,0:T(8,128)(2,1)S(1)}, u32[]{:S(2)}, u32[]{:S(2)}) collective-permute-start(f16[400,256]{1,0:T(8,128)(2,1)S(1)} %convert_element_type.42), channel_id=1, source_target_pairs={{0,2},{2,0},{1,3},{3,1},{4,6},{6,4},{5,7},{7,5},{8,10},{10,8},{9,1... | collective-permute-start | bytes 614408 | tf_op jit(solution)/shard_map/ppermute | solution.py:385
  56.5 10.7 %collective-permute-start.4 = (f16[208,512]{1,0:T(8,128)(2,1)S(1)}, f16[208,512]{1,0:T(8,128)(2,1)S(1)}, u32[]{:S(2)}, u32[]{:S(2)}) collective-permute-start(f16[208,512]{1,0:T(8,128)(2,1)S(1)} %convert_element_type.46), channel_id=1, source_target_pairs={{0,4},{4,0},{1,5},{5,1},{2,6},{6,2},{3,7},{7,3},{8,12},{12,8},{9,1... | collective-permute-start | bytes 638984 | tf_op jit(solution)/shard_map/ppermute | solution.py:381
  85.0 11.8 %collective-permute-start.5 = (bf16[784,256]{1,0:T(8,128)(2,1)}, bf16[784,256]{1,0:T(8,128)(2,1)S(1)}, u32[]{:S(2)}, u32[]{:S(2)}) collective-permute-start(bf16[784,256]{1,0:T(8,128)(2,1)} %get-tuple-element.54), channel_id=1, source_target_pairs={{0,1},{1,0},{2,3},{3,2},{4,5},{5,4},{6,7},{7,6},{8,9},{9,8},{10,11... | collective-permute-start | bytes 1204232 | tf_op jit(solution)/shard_map/ppermute | solution.py:385
  85.5 11.5 %collective-permute-start.6 = (bf16[784,256]{1,0:T(8,128)(2,1)}, bf16[784,256]{1,0:T(8,128)(2,1)S(1)}, u32[]{:S(2)}, u32[]{:S(2)}) collective-permute-start(bf16[784,256]{1,0:T(8,128)(2,1)} %get-tuple-element.55), channel_id=1, source_target_pairs={{0,2},{2,0},{1,3},{3,1},{4,6},{6,4},{5,7},{7,5},{8,10},{10,8},{9,1... | collective-permute-start | bytes 1204232 | tf_op jit(solution)/shard_map/ppermute | solution.py:385
  96.8 0.8 copy-start
  97.0 0.7 copy-start.1
  100.5 6.6 %collective-permute-start.7 = (bf16[400,256]{1,0:T(8,128)(2,1)}, bf16[400,256]{1,0:T(8,128)(2,1)S(1)}, u32[]{:S(2)}, u32[]{:S(2)}) collective-permute-start(bf16[400,256]{1,0:T(8,128)(2,1)} %get-tuple-element.59), channel_id=1, source_target_pairs={{0,2},{2,0},{1,3},{3,1},{4,6},{6,4},{5,7},{7,5},{8,10},{10,8},{9,1... | collective-permute-start | bytes 614408 | tf_op jit(solution)/shard_map/ppermute | solution.py:385
  100.8 6.4 %collective-permute-start.8 = (bf16[400,256]{1,0:T(8,128)(2,1)}, bf16[400,256]{1,0:T(8,128)(2,1)S(1)}, u32[]{:S(2)}, u32[]{:S(2)}) collective-permute-start(bf16[400,256]{1,0:T(8,128)(2,1)} %get-tuple-element.60), channel_id=1, source_target_pairs={{0,1},{1,0},{2,3},{3,2},{4,5},{5,4},{6,7},{7,6},{8,9},{9,8},{10,11... | collective-permute-start | bytes 614408 | tf_op jit(solution)/shard_map/ppermute | solution.py:385
  107.1 0.7 copy-start.3
  107.2 0.7 copy-start.4
  110.1 11.4 %collective-permute-start.9 = (bf16[208,512]{1,0:T(8,128)(2,1)}, bf16[208,512]{1,0:T(8,128)(2,1)S(1)}, u32[]{:S(2)}, u32[]{:S(2)}) collective-permute-start(bf16[208,512]{1,0:T(8,128)(2,1)} %get-tuple-element.62), channel_id=1, source_target_pairs={{0,4},{4,0},{1,5},{5,1},{2,6},{6,2},{3,7},{7,3},{8,12},{12,8},{9,1... | collective-permute-start | bytes 638984 | tf_op jit(solution)/shard_map/ppermute | solution.py:381
  121.4 0.7 copy-start.2
  124.7 1.4 collective-permute-start.10

commit v5 on v4

--- a/solution.py
+++ b/solution.py
@@ -87,9 +87,8 @@
             pieces.append(piece)
             rest = rest - piece
         self.total = total
-        self.packed = stack_rows(pieces, EXTRA).astype(BF16) if total.shape[0] == 1 else stack_rows(
-            [piece[k : k + 1] for piece in pieces for k in range(2)], EXTRA
-        ).astype(BF16)
+        rows = [piece[k : k + 1] for piece in pieces for k in range(2)]
+        self.packed = stack_rows(rows, EXTRA).astype(BF16)
 
     def pack(self, body):
         return body.astype(BF16)
@@ -301,17 +300,20 @@
     arnoldi_ref[...] = jnp.concatenate(rows, axis=0)
 
 
-def call(body, shapes, *args, scalars=0, scratch=()):
+def call(body, shapes, *args, scalars=0, outside=0, scratch=()):
     spec = pl.BlockSpec(memory_space=pltpu.VMEM)
     small = pl.BlockSpec(memory_space=pltpu.SMEM)
+    held = [pltpu.with_memory_space_constraint(arg, pltpu.VMEM) for arg in args[scalars:]]
+    inside = len(shapes) - outside
     return pl.pallas_call(
         body,
-        out_shape=[jax.ShapeDtypeStruct(shape, dtype) for shape, dtype in shapes],
-        in_specs=[small] * scalars + [spec] * (len(args) - scalars),
+        out_shape=[pltpu.VMEM(shape, dtype) for shape, dtype in shapes[:inside]]
+        + [jax.ShapeDtypeStruct(shape, dtype) for shape, dtype in shapes[inside:]],
+        in_specs=[small] * scalars + [spec] * len(held),
         out_specs=[spec] * len(shapes),
         scratch_shapes=list(scratch),
-        compiler_params=pltpu.CompilerParams(vmem_limit_bytes=56 * 1024 * 1024),
-    )(*args)
+        compiler_params=pltpu.CompilerParams(vmem_limit_bytes=24 * 1024 * 1024),
+    )(*args[:scalars], *held)
 
 
 def travel(array, kind, move):
@@ -407,7 +409,7 @@
         flat = lax.all_to_all(
             jnp.broadcast_to(flat, (members,) + flat.shape), ("row",) + tuple(bits), 0, 0
         )
-        answer, arnoldi = call(last_body, [full, ((6, cases), F32)], flat, notes, start, side)
+        answer, arnoldi = call(last_body, [full, ((6, cases), F32)], flat, notes, start, side, outside=2)
         return answer.reshape(3, node_dev, cases), arnoldi.reshape(3, 2, cases)
 
     return local

time: 143 us -> 113 us (0.79)
  Pallas kernels: 31.5 us -> 11.4 us
  other arithmetic: 14.9 us -> 3.44 us
    pallas_call x10, Pallas kernels: 31.5 us -> 11.4 us  [call(): pl.pallas_call(body, out_shape=[pltpu.VMEM(shape, dtype) for shape, dtype...]
    convert_element_type x4, other arithmetic: 4.34 us -> 0.32 us  [travel(): return move(array.astype(jnp.float16)).astype(F32)]
    convert_element_type x4, other arithmetic: 4.45 us -> 0.86 us  [exchange(): casts = [a.astype(jnp.float16) if kind is Scale else a for a in outs[0:2]]]
    ppermute x8, waiting for transfers between devices: 28.6 us -> 30.4 us  [exchange(): moved = [lax.ppermute(a, name, SWAP) for a, name in zip(casts, names)]]
    another operation x3, other arithmetic: 1.84 us -> 0.23 us  [sides(): return jnp.stack([lax.axis_index(name).astype(jnp.int32) for name in names])]
    convert_element_type x4, other arithmetic: 3.55 us -> 2.03 us  [exchange(): arrived = [a.astype(F32) if kind is Scale else a for a in moved]]
    unnamed x10 -> x12, local copies, waits for them, and re-layouts: 2.11 us -> 2.89 us
  transfers between devices with their start and end apart: 11 -> 11, of which waited for: 11 -> 11; matrix products, arithmetic and copies ran while one was open for 4% -> 2% of each run, Pallas kernels for 0% -> 0%
where the time goes in v5:
time: 113 us; the launch traced here: 112 us
  waiting for transfers between devices  48 us (42%)
  blocking collectives  31.9 us (28%)
  starting transfers between devices  13 us (12%)
  Pallas kernels  11.4 us (10%)
  local copies, waits for them, and re-layouts  3.51 us (3%)
  other arithmetic  3.44 us (3%)
    ppermute x8, waiting for transfers between devices, exchange(): moved = [lax.ppermute(a, name, SWAP) for a, name in zip(casts, names)]  30.4 us
    all_gather x2, blocking collectives, gather(): return travel(sent, kind, lambda a: lax.all_gather(a, ('row', 'core')))  19.2 us
    ppermute x2, waiting for transfers between devices, exchange(): move = lambda a: lax.ppermute(a, bits[0], SWAP)  16.5 us
    all_to_all x1, blocking collectives, local(): lax.all_to_all(jnp.broadcast_to(flat, (members,) + flat.shape), ('row',)...  12.8 us
    pallas_call x10, Pallas kernels, call(): pl.pallas_call(body, out_shape=[pltpu.VMEM(shape, dtype) for shape, dtype...  11.4 us
    ppermute x8, starting transfers between devices, exchange(): moved = [lax.ppermute(a, name, SWAP) for a, name in zip(casts, names)]  7.65 us
    ppermute x2, starting transfers between devices, exchange(): move = lambda a: lax.ppermute(a, bits[0], SWAP)  5.32 us
    unnamed x12, local copies, waits for them, and re-layouts  2.89 us
  transfers between devices with their start and end apart: 11, of which 11 were waited for; matrix products, arithmetic and copies ran while one was open for 2% of the time, Pallas kernels for 0%

profile of v5, /device:TPU:0, one launch (start us, length us, event | category | flops | bytes accessed | tf_op | source)
XLA Modules:
  0.0 112.2 jit_solution(4417378790403586788)
XLA Ops:
  1.5 1.0 copy-done.3
  3.1 10.6 %all-gather = f16[832,512]{1,0:T(8,128)(2,1)S(1)} all-gather(f16[208,512]{1,0:T(8,128)(2,1)S(1)} %convert_element_type.36), channel_id=2, replica_groups=mesh['row'=2,'core'=2,'bit2'=2,'bit1'=2,'bit0'=2] {'row','core'}, dimensions={0}, use_global_device_ids=true | all-gather | bytes 1064960 | tf_op jit(solution)/shard_map/all_gather | solution.py:343
  14.0 3.5 %shard_map.51 = (f32[784,256]{1,0:T(8,128)S(1)}, f32[784,256]{1,0:T(8,128)S(1)}, f32[768,256]{1,0:T(8,128)S(1)}, f32[768,256]{1,0:T(8,128)S(1)}, f32[8,512]{1,0:T(8,128)S(1)}) custom-call(s32[2]{0:T(128)S(1)} %pad_add_fusion.2.sides_ref, bf16[3,3,256,512]{3,2,1,0:T(8,128)(2,1)S(1)} %bitcast.9, f32[4,208,512]{2,1,0:T(8,128)S(1)} %convert.got_ref), custom_call_target="tpu_custom_call" | custom-call | tf_op jit(solution)/shard_map/pallas_call | solution.py:308
  17.5 1.6 %collective-permute-start.1 = (f16[784,256]{1,0:T(8,128)(2,1)S(1)}, f16[784,256]{1,0:T(8,128)(2,1)S(1)}, u32[]{:S(2)}, u32[]{:S(2)}) collective-permute-start(f16[784,256]{1,0:T(8,128)(2,1)S(1)} %convert_element_type.40), channel_id=1, source_target_pairs={{0,2},{2,0},{1,3},{3,1},{4,6},{6,4},{5,7},{7,5},{8,10},{10,8},{9,1... | collective-permute-start | bytes 1204232 | tf_op jit(solution)/shard_map/ppermute | solution.py:387
  19.3 1.6 %collective-permute-start = (f16[784,256]{1,0:T(8,128)(2,1)S(1)}, f16[784,256]{1,0:T(8,128)(2,1)S(1)}, u32[]{:S(2)}, u32[]{:S(2)}) collective-permute-start(f16[784,256]{1,0:T(8,128)(2,1)S(1)} %convert_element_type.38), channel_id=1, source_target_pairs={{0,1},{1,0},{2,3},{3,2},{4,5},{5,4},{6,7},{7,6},{8,9},{9,8},{10,11... | collective-permute-start | bytes 1204232 | tf_op jit(solution)/shard_map/ppermute | solution.py:387
  20.9 8.3 %collective-permute-done.1 = f16[784,256]{1,0:T(8,128)(2,1)S(1)} collective-permute-done((f16[784,256]{1,0:T(8,128)(2,1)S(1)}, f16[784,256]{1,0:T(8,128)(2,1)S(1)}, u32[]{:S(2)}, u32[]{:S(2)}) %collective-permute-start.1) | collective-permute-done | bytes 401440 | tf_op jit(solution)/shard_map/ppermute | solution.py:387
  29.2 1.4 %collective-permute-done = f16[784,256]{1,0:T(8,128)(2,1)S(1)} collective-permute-done((f16[784,256]{1,0:T(8,128)(2,1)S(1)}, f16[784,256]{1,0:T(8,128)(2,1)S(1)}, u32[]{:S(2)}, u32[]{:S(2)}) %collective-permute-start) | collective-permute-done | bytes 401440 | tf_op jit(solution)/shard_map/ppermute | solution.py:387
  31.4 1.5 %collective-permute-start.3 = (f16[400,256]{1,0:T(8,128)(2,1)S(1)}, f16[400,256]{1,0:T(8,128)(2,1)}, u32[]{:S(2)}, u32[]{:S(2)}) collective-permute-start(f16[400,256]{1,0:T(8,128)(2,1)S(1)} %convert_element_type.44), channel_id=1, source_target_pairs={{0,1},{1,0},{2,3},{3,2},{4,5},{5,4},{6,7},{7,6},{8,9},{9,8},{10,11... | collective-permute-start | bytes 614408 | tf_op jit(solution)/shard_map/ppermute | solution.py:387
  34.2 3.6 %collective-permute-done.3 = f16[400,256]{1,0:T(8,128)(2,1)} collective-permute-done((f16[400,256]{1,0:T(8,128)(2,1)S(1)}, f16[400,256]{1,0:T(8,128)(2,1)}, u32[]{:S(2)}, u32[]{:S(2)}) %collective-permute-start.3) | collective-permute-done | bytes 204832 | tf_op jit(solution)/shard_map/ppermute | solution.py:387
  37.8 1.0 convert_element_type.45.refs_3_
  38.8 1.1 %collective-permute-done.2 = f16[400,256]{1,0:T(8,128)(2,1)} collective-permute-done((f16[400,256]{1,0:T(8,128)(2,1)}, f16[400,256]{1,0:T(8,128)(2,1)}, u32[]{:S(2)}, u32[]{:S(2)}) %collective-permute-start.2) | collective-permute-done | bytes 204832 | tf_op jit(solution)/shard_map/ppermute | solution.py:387
  40.9 1.0 copy-done.5
  41.9 1.2 %shard_map.53 = (f32[208,512]{1,0:T(8,128)S(1)}, f32[192,512]{1,0:T(8,128)S(1)}, f32[8,512]{1,0:T(8,128)}) custom-call(s32[2]{0:T(128)S(1)} %pad_add_fusion.sides_ref, f32[8,512]{1,0:T(8,128)S(1)} %get-tuple-element.42.note_ref, f32[384,256]{1,0:T(8,128)S(1)} %get-tuple-element.43.refs_0_, f32[384,256]{1,0:T(8,128)S(1)} %copy-done.5, ...), custom_call_target="tpu_custom_call" | custom-call | tf_op jit(solution)/shard_map/pallas_call | solution.py:308
  43.1 2.7 %collective-permute-start.4 = (f16[208,512]{1,0:T(8,128)(2,1)S(1)}, f16[208,512]{1,0:T(8,128)(2,1)S(1)}, u32[]{:S(2)}, u32[]{:S(2)}) collective-permute-start(f16[208,512]{1,0:T(8,128)(2,1)S(1)} %convert_element_type.46), channel_id=1, source_target_pairs={{0,4},{4,0},{1,5},{5,1},{2,6},{6,2},{3,7},{7,3},{8,12},{12,8},{9,1... | collective-permute-start | bytes 638984 | tf_op jit(solution)/shard_map/ppermute | solution.py:383
  45.8 8.1 %collective-permute-done.4 = f16[208,512]{1,0:T(8,128)(2,1)S(1)} collective-permute-done((f16[208,512]{1,0:T(8,128)(2,1)S(1)}, f16[208,512]{1,0:T(8,128)(2,1)S(1)}, u32[]{:S(2)}, u32[]{:S(2)}) %collective-permute-start.4) | collective-permute-done | bytes 213024 | tf_op jit(solution)/shard_map/ppermute | solution.py:383
  54.5 8.6 %all-gather.1 = bf16[832,512]{1,0:T(8,128)(2,1)S(1)} all-gather(bf16[208,512]{1,0:T(8,128)(2,1)S(1)} %get-tuple-element.50), channel_id=3, replica_groups=mesh['row'=2,'core'=2,'bit2'=2,'bit1'=2,'bit0'=2] {'row','core'}, dimensions={0}, use_global_device_ids=true | all-gather | bytes 1064960 | tf_op jit(solution)/shard_map/all_gather | solution.py:343
  63.0 2.2 %shard_map.55 = (bf16[784,256]{1,0:T(8,128)(2,1)S(1)}, bf16[784,256]{1,0:T(8,128)(2,1)S(1)}, f32[768,256]{1,0:T(8,128)S(1)}, f32[768,256]{1,0:T(8,128)S(1)}, f32[8,512]{1,0:T(8,128)S(1)}) custom-call(s32[2]{0:T(128)S(1)} %pad_add_fusion.2.sides_ref, bf16[3,3,256,512]{3,2,1,0:T(8,128)(2,1)S(1)} %bitcast.10, bf16[4,208,512]{2,1,0:T(8,128)(2,1)S(1)} %bitcast.11), custom_call_target="tpu_custom_call" | custom-call | tf_op jit(solution)/shard_map/pallas_call | solution.py:308
  65.9 10.9 %collective-permute-done.5.refs_2_ = bf16[784,256]{1,0:T(8,128)(2,1)S(1)} collective-permute-done((bf16[784,256]{1,0:T(8,128)(2,1)S(1)}, bf16[784,256]{1,0:T(8,128)(2,1)S(1)}, u32[]{:S(2)}, u32[]{:S(2)}) %collective-permute-start.5) | collective-permute-done | bytes 401440 | tf_op jit(solution)/shard_map/ppermute | solution.py:387
  78.2 1.4 %collective-permute-start.8 = (bf16[400,256]{1,0:T(8,128)(2,1)S(1)}, bf16[400,256]{1,0:T(8,128)(2,1)S(1)}, u32[]{:S(2)}, u32[]{:S(2)}) collective-permute-start(bf16[400,256]{1,0:T(8,128)(2,1)S(1)} %get-tuple-element.60), channel_id=1, source_target_pairs={{0,1},{1,0},{2,3},{3,2},{4,5},{5,4},{6,7},{7,6},{8,9},{9,8},{10,11... | collective-permute-start | bytes 614408 | tf_op jit(solution)/shard_map/ppermute | solution.py:387
  79.6 4.5 %collective-permute-done.7.refs_2_ = bf16[400,256]{1,0:T(8,128)(2,1)S(1)} collective-permute-done((bf16[400,256]{1,0:T(8,128)(2,1)S(1)}, bf16[400,256]{1,0:T(8,128)(2,1)S(1)}, u32[]{:S(2)}, u32[]{:S(2)}) %collective-permute-start.7) | collective-permute-done | bytes 204832 | tf_op jit(solution)/shard_map/ppermute | solution.py:387
  85.0 2.7 %collective-permute-start.9 = (bf16[208,512]{1,0:T(8,128)(2,1)S(1)}, bf16[208,512]{1,0:T(8,128)(2,1)S(1)}, u32[]{:S(2)}, u32[]{:S(2)}) collective-permute-start(bf16[208,512]{1,0:T(8,128)(2,1)S(1)} %get-tuple-element.62), channel_id=1, source_target_pairs={{0,4},{4,0},{1,5},{5,1},{2,6},{6,2},{3,7},{7,3},{8,12},{12,8},{9,1... | collective-permute-start | bytes 638984 | tf_op jit(solution)/shard_map/ppermute | solution.py:383
  87.7 8.4 %collective-permute-done.9.got_ref = bf16[208,512]{1,0:T(8,128)(2,1)S(1)} collective-permute-done((bf16[208,512]{1,0:T(8,128)(2,1)S(1)}, bf16[208,512]{1,0:T(8,128)(2,1)S(1)}, u32[]{:S(2)}, u32[]{:S(2)}) %collective-permute-start.9) | collective-permute-done | bytes 213024 | tf_op jit(solution)/shard_map/ppermute | solution.py:383
  96.7 1.2 %collective-permute-done.10 = f32[16,128]{1,0:T(8,128)S(1)} collective-permute-done((f32[16,128]{1,0:T(8,128)S(1)}, f32[16,128]{1,0:T(8,128)S(1)}, u32[]{:S(2)}, u32[]{:S(2)}) %collective-permute-start.10) | collective-permute-done | bytes 8224 | tf_op jit(solution)/shard_map/ppermute | solution.py:407
  97.9 12.8 %all_to_all.5.flat_ref = f32[16,16,128]{2,1,0:T(8,128)S(1)} all-to-all(f32[16,16,128]{2,1,0:T(8,128)S(1)} %broadcast_in_dim.3), channel_id=1, replica_groups=mesh['row'=2,'core'=2,'bit2'=2,'bit1'=2,'bit0'=2] {'row','bit2','bit1','..., dimensions={0} | all-to-all | bytes 262144 | tf_op jit(solution)/shard_map/all_to_all | solution.py:409
  (41 shorter events, 10.7 us)
Async XLA Ops:
  0.6 0.9 copy-start.1
  1.5 1.0 copy-start.3
  2.5 11.5 %copy-start = (bf16[3,3,4,1,64,512]{5,4,3,2,1,0:T(8,128)(2,1)S(1)}, bf16[3,3,4,1,64,512]{5,4,3,2,1,0:T(8,128)(2,1)}, u32[]{:S(2)}) copy-start(bf16[3,3,4,1,64,512]{5,4,3,2,1,0:T(8,128)(2,1)} %param.3) | copy-start | bytes 7077892
  17.5 11.6 %collective-permute-start.1 = (f16[784,256]{1,0:T(8,128)(2,1)S(1)}, f16[784,256]{1,0:T(8,128)(2,1)S(1)}, u32[]{:S(2)}, u32[]{:S(2)}) collective-permute-start(f16[784,256]{1,0:T(8,128)(2,1)S(1)} %convert_element_type.40), channel_id=1, source_target_pairs={{0,2},{2,0},{1,3},{3,1},{4,6},{6,4},{5,7},{7,5},{8,10},{10,8},{9,1... | collective-permute-start | bytes 1204232 | tf_op jit(solution)/shard_map/ppermute | solution.py:387
  19.3 11.3 %collective-permute-start = (f16[784,256]{1,0:T(8,128)(2,1)S(1)}, f16[784,256]{1,0:T(8,128)(2,1)S(1)}, u32[]{:S(2)}, u32[]{:S(2)}) collective-permute-start(f16[784,256]{1,0:T(8,128)(2,1)S(1)} %convert_element_type.38), channel_id=1, source_target_pairs={{0,1},{1,0},{2,3},{3,2},{4,5},{5,4},{6,7},{7,6},{8,9},{9,8},{10,11... | collective-permute-start | bytes 1204232 | tf_op jit(solution)/shard_map/ppermute | solution.py:387
  31.4 2.3 %copy-start.4 = (f32[384,256]{1,0:T(8,128)}, f32[384,256]{1,0:T(8,128)S(1)}, u32[]{:S(2)}) copy-start(f32[384,256]{1,0:T(8,128)S(1)} %get-tuple-element.44.refs_1_) | copy-start | bytes 1179652
  31.4 6.4 %collective-permute-start.3 = (f16[400,256]{1,0:T(8,128)(2,1)S(1)}, f16[400,256]{1,0:T(8,128)(2,1)}, u32[]{:S(2)}, u32[]{:S(2)}) collective-permute-start(f16[400,256]{1,0:T(8,128)(2,1)S(1)} %convert_element_type.44), channel_id=1, source_target_pairs={{0,1},{1,0},{2,3},{3,2},{4,5},{5,4},{6,7},{7,6},{8,9},{9,8},{10,11... | collective-permute-start | bytes 614408 | tf_op jit(solution)/shard_map/ppermute | solution.py:387
  33.0 20.9 %copy-start.2 = (f32[96,192]{1,0:T(8,128)S(1)}, f32[96,192]{1,0:T(8,128)}, u32[]{:S(2)}) copy-start(f32[96,192]{1,0:T(8,128)} %precond_ref.5) | copy-start | bytes 221188
  33.7 6.2 %collective-permute-start.2 = (f16[400,256]{1,0:T(8,128)(2,1)}, f16[400,256]{1,0:T(8,128)(2,1)}, u32[]{:S(2)}, u32[]{:S(2)}) collective-permute-start(f16[400,256]{1,0:T(8,128)(2,1)} %convert_element_type.42), channel_id=1, source_target_pairs={{0,2},{2,0},{1,3},{3,1},{4,6},{6,4},{5,7},{7,5},{8,10},{10,8},{9,1... | collective-permute-start | bytes 614408 | tf_op jit(solution)/shard_map/ppermute | solution.py:387
  40.9 1.0 copy-start.5
  43.1 10.7 %collective-permute-start.4 = (f16[208,512]{1,0:T(8,128)(2,1)S(1)}, f16[208,512]{1,0:T(8,128)(2,1)S(1)}, u32[]{:S(2)}, u32[]{:S(2)}) collective-permute-start(f16[208,512]{1,0:T(8,128)(2,1)S(1)} %convert_element_type.46), channel_id=1, source_target_pairs={{0,4},{4,0},{1,5},{5,1},{2,6},{6,2},{3,7},{7,3},{8,12},{12,8},{9,1... | collective-permute-start | bytes 638984 | tf_op jit(solution)/shard_map/ppermute | solution.py:383
  65.2 11.6 %collective-permute-start.5 = (bf16[784,256]{1,0:T(8,128)(2,1)S(1)}, bf16[784,256]{1,0:T(8,128)(2,1)S(1)}, u32[]{:S(2)}, u32[]{:S(2)}) collective-permute-start(bf16[784,256]{1,0:T(8,128)(2,1)S(1)} %get-tuple-element.54), channel_id=1, source_target_pairs={{0,1},{1,0},{2,3},{3,2},{4,5},{5,4},{6,7},{7,6},{8,9},{9,8},{10,11... | collective-permute-start | bytes 1204232 | tf_op jit(solution)/shard_map/ppermute | solution.py:387
  65.9 11.3 %collective-permute-start.6 = (bf16[784,256]{1,0:T(8,128)(2,1)S(1)}, bf16[784,256]{1,0:T(8,128)(2,1)S(1)}, u32[]{:S(2)}, u32[]{:S(2)}) collective-permute-start(bf16[784,256]{1,0:T(8,128)(2,1)S(1)} %get-tuple-element.55), channel_id=1, source_target_pairs={{0,2},{2,0},{1,3},{3,1},{4,6},{6,4},{5,7},{7,5},{8,10},{10,8},{9,1... | collective-permute-start | bytes 1204232 | tf_op jit(solution)/shard_map/ppermute | solution.py:387
  77.9 6.3 %collective-permute-start.7 = (bf16[400,256]{1,0:T(8,128)(2,1)S(1)}, bf16[400,256]{1,0:T(8,128)(2,1)S(1)}, u32[]{:S(2)}, u32[]{:S(2)}) collective-permute-start(bf16[400,256]{1,0:T(8,128)(2,1)S(1)} %get-tuple-element.59), channel_id=1, source_target_pairs={{0,2},{2,0},{1,3},{3,1},{4,6},{6,4},{5,7},{7,5},{8,10},{10,8},{9,1... | collective-permute-start | bytes 614408 | tf_op jit(solution)/shard_map/ppermute | solution.py:387
  78.2 6.2 %collective-permute-start.8 = (bf16[400,256]{1,0:T(8,128)(2,1)S(1)}, bf16[400,256]{1,0:T(8,128)(2,1)S(1)}, u32[]{:S(2)}, u32[]{:S(2)}) collective-permute-start(bf16[400,256]{1,0:T(8,128)(2,1)S(1)} %get-tuple-element.60), channel_id=1, source_target_pairs={{0,1},{1,0},{2,3},{3,2},{4,5},{5,4},{6,7},{7,6},{8,9},{9,8},{10,11... | collective-permute-start | bytes 614408 | tf_op jit(solution)/shard_map/ppermute | solution.py:387
  85.0 11.0 %collective-permute-start.9 = (bf16[208,512]{1,0:T(8,128)(2,1)S(1)}, bf16[208,512]{1,0:T(8,128)(2,1)S(1)}, u32[]{:S(2)}, u32[]{:S(2)}) collective-permute-start(bf16[208,512]{1,0:T(8,128)(2,1)S(1)} %get-tuple-element.62), channel_id=1, source_target_pairs={{0,4},{4,0},{1,5},{5,1},{2,6},{6,2},{3,7},{7,3},{8,12},{12,8},{9,1... | collective-permute-start | bytes 638984 | tf_op jit(solution)/shard_map/ppermute | solution.py:383
  96.7 1.2 %collective-permute-start.10 = (f32[16,128]{1,0:T(8,128)S(1)}, f32[16,128]{1,0:T(8,128)S(1)}, u32[]{:S(2)}, u32[]{:S(2)}) collective-permute-start(f32[16,128]{1,0:T(8,128)S(1)} %get-tuple-element.65), channel_id=1, source_target_pairs={{0,8},{8,0},{1,9},{9,1},{2,10},{10,2},{3,11},{11,3},{4,12},{12,4},... | collective-permute-start | bytes 24584 | tf_op jit(solution)/shard_map/ppermute | solution.py:407

commit v6 on v5

--- a/solution.py
+++ b/solution.py
@@ -160,7 +160,7 @@
 
 
 def couple_body(kind, places, sides_ref, tile_ref, got_ref, *refs):
-    sends, keeps, note_ref, work_ref = refs[0:2], refs[2:4], refs[4], refs[5]
+    sends, keeps, note_ref, work_ref = refs[0:4], refs[4:8], refs[8], refs[9]
     sources = got_ref.shape[0]
     height = got_ref.shape[1] - EXTRA
     nodes = height // 3
@@ -191,25 +191,30 @@
                 left, term, (((0,), (0,)), ((), ())), preferred_element_type=F32
             )
         work_ref[comp] = total
+    slots = targets // 4
+    top = sides_ref[2]
     for colour in range(2):
         first = colour * half
         columns = slice(first, first + half)
         side = sides_ref[colour]
         inner_note = type(note).load(note_ref[:, columns])
-        for slot in range(targets // 2):
-            give = insert(slot, places[colour], 1 - side) * nodes
-            keep = insert(slot, places[colour], side) * nodes
-            for comp in range(3):
-                row = slot * height + comp * nodes
-                value = work_ref[comp, pl.ds(pl.multiple_of(give, nodes), nodes), columns]
-                sends[colour][row : row + nodes] = inner_note.pack(value)
-                value = work_ref[comp, pl.ds(pl.multiple_of(keep, nodes), nodes), columns]
-                keeps[colour][row : row + nodes] = value
-        sends[colour][targets // 2 * height :] = inner_note.packed
-
-
-def merge_body(kind, places, joined, height, sides_ref, note_ref, *refs):
-    kept, got, outs, next_ref = refs[0:2], refs[2:4], refs[4:-1], refs[-1]
+        for near in range(2):
+            base = (top if near else 1 - top) * (targets // 2)
+            send, kept = sends[near * 2 + colour], keeps[near * 2 + colour]
+            for slot in range(slots):
+                give = (base + insert(slot, places[colour], 1 - side)) * nodes
+                keep = (base + insert(slot, places[colour], side)) * nodes
+                for comp in range(3):
+                    row = slot * height + comp * nodes
+                    value = work_ref[comp, pl.ds(pl.multiple_of(give, nodes), nodes), columns]
+                    send[row : row + nodes] = inner_note.pack(value)
+                    value = work_ref[comp, pl.ds(pl.multiple_of(keep, nodes), nodes), columns]
+                    kept[row : row + nodes] = value
+            send[slots * height :] = inner_note.packed
+
+
+def merge_body(kind, places, height, sides_ref, note_ref, *refs):
+    kept, got, outs, next_ref = refs[0:2], refs[2:4], refs[4:8], refs[8]
     half = kept[0].shape[1]
     slots = kept[0].shape[0] // height
     for colour in range(2):
@@ -222,41 +227,58 @@
             rows = slice(slot * height, (slot + 1) * height)
             give = pl.ds(pl.multiple_of(insert(slot, places[colour], 1 - side) * height, height), height)
             keep = pl.ds(pl.multiple_of(insert(slot, places[colour], side) * height, height), height)
-            given = note.pack(kept[colour][give] + kind.unpack(got[colour][give], other))
-            held = kept[colour][keep] + kind.unpack(got[colour][keep], other)
-            if joined:
-                outs[0][rows, columns] = given
-                outs[1][rows, columns] = held
-            else:
-                outs[colour][rows] = given
-                outs[2 + colour][rows] = held
-        if joined:
-            outs[0][slots // 2 * height :, columns] = note.packed
-        else:
-            outs[colour][slots // 2 * height :] = note.packed
-
-
-def second_body(kept_ref, got_ref, start_ref, precond_ref, work_ref, sent_ref):
+            outs[colour][rows] = note.pack(kept[colour][give] + kind.unpack(got[colour][give], other))
+            outs[2 + colour][rows] = kept[colour][keep] + kind.unpack(got[colour][keep], other)
+        outs[colour][slots // 2 * height :] = note.packed
+
+
+def join_body(kind, note_ref, *refs):
+    kept, got, sent_ref, next_ref = refs[0:2], refs[2:4], refs[4], refs[5]
+    height, half = kept[0].shape
+    for colour in range(2):
+        columns = slice(colour * half, (colour + 1) * half)
+        other = kind.read(got[colour][height:])
+        note = kind.load(note_ref[:, columns]).merge(other)
+        next_ref[:, columns] = note.rows()
+        sent_ref[0:height, columns] = note.pack(
+            kept[colour][...] + kind.unpack(got[colour][0:height], other)
+        )
+        sent_ref[height:, columns] = note.packed
+
+
+def share_of(kind, kept, got, far_ref):
+    height = kept[0].shape[0]
+    parts = []
+    for colour in range(2):
+        other = kind.read(got[colour][height:])
+        parts.append(kept[colour][...] + kind.unpack(got[colour][0:height], other))
+    other = kind.read(far_ref[height:])
+    return jnp.concatenate(parts, axis=1) + kind.unpack(far_ref[0:height], other), other
+
+
+def second_body(*refs):
+    kept, got, far_ref = refs[0:2], refs[2:4], refs[4]
+    start_ref, precond_ref, work_ref, sent_ref = refs[5:]
     height = start_ref.shape[0]
-    other = Scale.read(got_ref[height:])
     start = start_ref[...]
-    moved = start + (kept_ref[...] + Scale.unpack(got_ref[0:height], other))
-    work = blocks_times(precond_ref[...], moved)
+    share, _ = share_of(Scale, kept, got, far_ref)
+    work = blocks_times(precond_ref[...], start + share)
     work_ref[...] = work
     note = Sums(jnp.concatenate([row_sum(start, start), row_sum(start, work)], axis=0))
     sent_ref[0:height] = note.pack(work)
     sent_ref[height:] = note.packed
 
 
-def third_body(kept_ref, got_ref, note_ref, start_ref, work_ref, precond_ref, side_ref, gram_ref, next_ref):
-    height = start_ref.shape[0]
-    note = Sums.load(note_ref[...]).merge(Sums.read(got_ref[height:]))
+def third_body(*refs):
+    kept, got, far_ref = refs[0:2], refs[2:4], refs[4]
+    note_ref, start_ref, work_ref, precond_ref, side_ref, gram_ref, next_ref = refs[5:]
+    share, sums = share_of(Sums, kept, got, far_ref)
+    note = Sums.load(note_ref[...]).merge(sums)
     next_ref[...] = note.rows()
     start = start_ref[...]
     work = work_ref[...]
-    moved = work + (kept_ref[...] + got_ref[0:height].astype(F32))
     h_one_one = note.total[1:2] / (note.total[0:1] + TINY)
-    other = blocks_times(precond_ref[...], moved) - h_one_one * work
+    other = blocks_times(precond_ref[...], work + share) - h_one_one * work
     side = work - h_one_one * start
     side_ref[...] = side
     pairs = [(side, side), (start, other), (side, other), (other, other)]
@@ -296,14 +318,17 @@
         beta, h_one_one, h_two_one, h_one_two, h_two_two, h_three_two
     )
     solution_ref[...] = (y_one / beta) * start_ref[...] + (y_two / length) * side_ref[...]
-    rows = [h_one_one, h_one_two, h_two_one, h_two_two, estimate, h_three_two]
-    arnoldi_ref[...] = jnp.concatenate(rows, axis=0)
-
-
-def call(body, shapes, *args, scalars=0, outside=0, scratch=()):
+    arnoldi_ref[0] = jnp.concatenate([h_one_one, h_one_two], axis=0)
+    arnoldi_ref[1] = jnp.concatenate([h_two_one, h_two_two], axis=0)
+    arnoldi_ref[2] = jnp.concatenate([estimate, h_three_two], axis=0)
+
+
+def call(body, shapes, *args, scalars=0, outside=0, scratch=(), hold=True):
     spec = pl.BlockSpec(memory_space=pltpu.VMEM)
     small = pl.BlockSpec(memory_space=pltpu.SMEM)
-    held = [pltpu.with_memory_space_constraint(arg, pltpu.VMEM) for arg in args[scalars:]]
+    held = list(args[scalars:])
+    if hold:
+        held = [pltpu.with_memory_space_constraint(arg, pltpu.VMEM) for arg in held]
     inside = len(shapes) - outside
     return pl.pallas_call(
         body,
@@ -312,7 +337,7 @@
         in_specs=[small] * scalars + [spec] * len(held),
         out_specs=[spec] * len(shapes),
         scratch_shapes=list(scratch),
-        compiler_params=pltpu.CompilerParams(vmem_limit_bytes=24 * 1024 * 1024),
+        compiler_params=pltpu.CompilerParams(vmem_limit_bytes=20 * 1024 * 1024),
     )(*args[:scalars], *held)
 
 
@@ -342,63 +367,99 @@
         def gather(sent, kind):
             return travel(sent, kind, lambda a: lax.all_gather(a, ("row", "core")))
 
+        def cast(array, kind):
+            return array.astype(jnp.float16) if kind is Scale else array
+
+        def widen(array, kind):
+            return array.astype(F32) if kind is Scale else array
+
+        def swap(arrays, names, kind):
+            moved = [lax.ppermute(cast(a, kind), name, SWAP) for a, name in zip(arrays, names)]
+            return [widen(a, kind) for a in moved]
+
         def exchange(got, kind):
-            left = [list(bits), list(bits)]
-            slots = row_count // node_dev
-            for step in range(len(lower) + 1):
-                joined = step == len(lower)
-                names = [bits[0]] * 2 if joined else [orders[0][step], orders[1][step]]
+            left = [list(lower), list(lower)]
+            note = ((NOTE, cases), F32)
+            slots = row_count // node_dev // 2
+
+            def take(step):
+                names = [orders[0][step], orders[1][step]]
                 places = [len(left[k]) - 1 - left[k].index(names[k]) for k in range(2)]
-                slots = slots // 2
-                tall = slots * height
-                note = ((NOTE, cases), F32)
-                if step == 0:
-                    shapes = [((tall + EXTRA, half), kind.sent)] * 2 + [((tall, half), F32)] * 2
+                for k in range(2):
+                    left[k].remove(names[k])
+                return names, places
+
+            def shapes(count):
+                tall = count * height
+                return [((tall + EXTRA, half), kind.sent)], [((tall, half), F32)]
+
+            names, places = take(0)
+            slots = slots // 2
+            sent, kept = shapes(slots)
+            outs = call(
+                functools.partial(couple_body, kind, places),
+                sent * 4 + kept * 4 + [note],
+                sides(names + [bits[0]]),
+                tile,
+                got,
+                scalars=1,
+                scratch=[pltpu.VMEM((3, row_count, cases), F32)],
+            )
+            near = [outs[2:4], outs[6:8], outs[8]]
+            far = [outs[0:2], outs[4:6], outs[8]]
+            plan = [(names, None)]
+            for step in range(1, len(lower)):
+                plan.append(take(step))
+
+            def reduce(state, tie):
+                count = slots
+                sends, kept, notes = state
+                arrived = swap(sends, plan[0][0], kind)
+                for names, places in plan[1:]:
+                    count = count // 2
+                    sent, keep = shapes(count)
                     outs = call(
-                        functools.partial(couple_body, kind, places),
-                        shapes + [note],
-                        sides(names),
-                        tile,
-                        got,
-                        scalars=1,
-                        scratch=[pltpu.VMEM((3, row_count, cases), F32)],
-                    )
-                else:
-                    shapes = [((tall + EXTRA, half), kind.sent)] * 2 + [((tall, half), F32)] * 2
-                    if joined:
-                        shapes = [((tall + EXTRA, cases), kind.sent), ((tall, cases), F32)]
-                    outs = call(
-                        functools.partial(merge_body, kind, places, joined, height),
-                        shapes + [note],
+                        functools.partial(merge_body, kind, places, height),
+                        sent * 2 + keep * 2 + [note],
                         sides(names),
                         notes,
                         *kept,
                         *arrived,
                         scalars=1,
                     )
-                notes = outs[-1]
-                for k in range(2):
-                    left[k].remove(names[k])
-                if joined:
-                    move = lambda a: lax.ppermute(a, bits[0], SWAP)
-                    return outs[1], travel(outs[0], kind, move), notes
-                kept = outs[2:4]
-                casts = [a.astype(jnp.float16) if kind is Scale else a for a in outs[0:2]]
-                moved = [lax.ppermute(a, name, SWAP) for a, name in zip(casts, names)]
-                arrived = [a.astype(F32) if kind is Scale else a for a in moved]
+                    if tie is not None:
+                        tie.append(outs[4])
+                    kept, notes = outs[2:4], outs[4]
+                    arrived = swap(outs[0:2], names, kind)
+                return kept, arrived, notes
+
+            ties = []
+            kept, arrived, notes = reduce(far, ties)
+            sent, notes = call(
+                functools.partial(join_body, kind),
+                [((height + EXTRA, cases), kind.sent), note],
+                notes,
+                *kept,
+                *arrived,
+            )
+            if ties:
+                tied = lax.optimization_barrier(tuple(near[0]) + (ties[0],))
+                near[0] = list(tied[:2])
+            (crossed,) = swap([sent], [bits[0]], kind)
+            kept, arrived, _ = reduce(near, None)
+            return list(kept) + list(arrived) + [crossed], notes
 
         full = ((height, cases), F32)
-        start, sent = call(first_body, [full, ((height + EXTRA, cases), F32)], right, precond)
-        kept, got, _ = exchange(gather(sent, Scale), Scale)
-        work, sent = call(
-            second_body, [full, ((height + EXTRA, cases), BF16)], kept, got, start, precond
-        )
-        kept, got, notes = exchange(gather(sent, Sums), Sums)
+        packed = ((height + EXTRA, cases), F32)
+        start, sent = call(first_body, [full, packed], right, precond, hold=False)
+        shares, _ = exchange(gather(sent, Scale), Scale)
+        packed = ((height + EXTRA, cases), BF16)
+        work, sent = call(second_body, [full, packed], *shares, start, precond)
+        shares, notes = exchange(gather(sent, Sums), Sums)
         side, flat, notes = call(
             third_body,
             [full, ((4 * cases // 128, 128), F32), ((NOTE, cases), F32)],
-            kept,
-            got,
+            *shares,
             notes,
             start,
             work,
@@ -409,8 +470,8 @@
         flat = lax.all_to_all(
             jnp.broadcast_to(flat, (members,) + flat.shape), ("row",) + tuple(bits), 0, 0
         )
-        answer, arnoldi = call(last_body, [full, ((6, cases), F32)], flat, notes, start, side, outside=2)
-        return answer.reshape(3, node_dev, cases), arnoldi.reshape(3, 2, cases)
+        answer, arnoldi = call(last_body, [full, ((3, 2, cases), F32)], flat, notes, start, side, outside=2)
+        return answer.reshape(3, node_dev, cases), arnoldi
 
     return local
 

time: 113 us -> 99.4 us (0.88)
  waiting for transfers between devices: 48 us -> 32.3 us
  starting transfers between devices: 13 us -> 19.8 us
  other arithmetic: 3.44 us -> 0.81 us
  local copies, waits for them, and re-layouts: 3.51 us -> 1.91 us
  Pallas kernels: 11.4 us -> 12.6 us
    ppermute x10 -> x18, waiting for transfers between devices: 46.9 us -> 31.1 us  [swap(): lax.ppermute(cast(a, kind), name, SWAP)]
    ppermute x10 -> x18, starting transfers between devices: 13 us -> 19.7 us  [swap(): lax.ppermute(cast(a, kind), name, SWAP)]
    convert_element_type x8 -> x18, other arithmetic: 2.89 us -> 0.4 us  [the longest x9 0.22 us: widen(): return array.astype(F32) if kind is Scale else array]
    pallas_call x10 -> x12, Pallas kernels: 11.4 us -> 12.6 us  [call(): pl.pallas_call(body, out_shape=[pltpu.VMEM(shape, dtype) for shape, dtype...]
    unnamed x12 -> x8, local copies, waits for them, and re-layouts: 2.89 us -> 1.89 us
  transfers between devices with their start and end apart: 11 -> 19, of which waited for: 11 -> 14; matrix products, arithmetic and copies ran while one was open for 2% -> 0% of each run, Pallas kernels for 0% -> 3%
where the time goes in v6:
time: 99.4 us; the launch traced here: 99.2 us
  waiting for transfers between devices  32.3 us (32%)
  blocking collectives  30.9 us (31%)
  starting transfers between devices  19.8 us (20%)
  Pallas kernels  12.6 us (13%)
  local copies, waits for them, and re-layouts  1.91 us (2%)
    ppermute x18, waiting for transfers between devices, swap(): lax.ppermute(cast(a, kind), name, SWAP)  31.1 us
    ppermute x18, starting transfers between devices, swap(): lax.ppermute(cast(a, kind), name, SWAP)  19.7 us
    all_gather x2, blocking collectives, gather(): return travel(sent, kind, lambda a: lax.all_gather(a, ('row', 'core')))  19.1 us
    pallas_call x12, Pallas kernels, call(): pl.pallas_call(body, out_shape=[pltpu.VMEM(shape, dtype) for shape, dtype...  12.6 us
    all_to_all x1, blocking collectives, local(): lax.all_to_all(jnp.broadcast_to(flat, (members,) + flat.shape), ('row',)...  11.8 us
  transfers between devices with their start and end apart: 19, of which 14 were waited for; matrix products, arithmetic and copies ran while one was open for 0% of the time, Pallas kernels for 3%

profile of v6, /device:TPU:0, one launch (start us, length us, event | category | flops | bytes accessed | tf_op | source)
XLA Modules:
  0.0 99.2 jit_solution(1834135821847821478)
XLA Ops:
  3.1 10.6 %all-gather = f16[832,512]{1,0:T(8,128)(2,1)S(1)} all-gather(f16[208,512]{1,0:T(8,128)(2,1)S(1)} %convert_element_type.60), channel_id=2, replica_groups=mesh['row'=2,'core'=2,'bit2'=2,'bit1'=2,'bit0'=2] {'row','core'}, dimensions={0}, use_global_device_ids=true | all-gather | bytes 1064960 | tf_op jit(solution)/shard_map/all_gather | solution.py:368
  14.0 3.4 %shard_map.51 = (f32[400,256]{1,0:T(8,128)S(1)}, f32[400,256]{1,0:T(8,128)S(1)}, f32[400,256]{1,0:T(8,128)S(1)}, f32[400,256]{1,0:T(8,128)S(1)}, f32[384,256]{1,...) custom-call(s32[3]{0:T(128)S(1)} %pad_add_fusion.1.sides_ref, ...), custom_call_target="tpu_custom_call" | custom-call | tf_op jit(solution)/shard_map/pallas_call | solution.py:333
  17.5 1.6 %collective-permute-start.1 = (f16[400,256]{1,0:T(8,128)(2,1)S(1)}, f16[400,256]{1,0:T(8,128)(2,1)S(1)}, u32[]{:S(2)}, u32[]{:S(2)}) collective-permute-start(f16[400,256]{1,0:T(8,128)(2,1)S(1)} %convert_element_type.64), channel_id=1, source_target_pairs={{0,2},{2,0},{1,3},{3,1},{4,6},{6,4},{5,7},{7,5},{8,10},{10,8},{9,1... | collective-permute-start | bytes 614408 | tf_op jit(solution)/shard_map/ppermute | solution.py:377
  19.2 1.6 %collective-permute-start = (f16[400,256]{1,0:T(8,128)(2,1)S(1)}, f16[400,256]{1,0:T(8,128)(2,1)S(1)}, u32[]{:S(2)}, u32[]{:S(2)}) collective-permute-start(f16[400,256]{1,0:T(8,128)(2,1)S(1)} %convert_element_type.62), channel_id=1, source_target_pairs={{0,1},{1,0},{2,3},{3,2},{4,5},{5,4},{6,7},{7,6},{8,9},{9,8},{10,11... | collective-permute-start | bytes 614408 | tf_op jit(solution)/shard_map/ppermute | solution.py:377
  20.8 4.1 %collective-permute-done.1 = f16[400,256]{1,0:T(8,128)(2,1)S(1)} collective-permute-done((f16[400,256]{1,0:T(8,128)(2,1)S(1)}, f16[400,256]{1,0:T(8,128)(2,1)S(1)}, u32[]{:S(2)}, u32[]{:S(2)}) %collective-permute-start.1) | collective-permute-done | bytes 204832 | tf_op jit(solution)/shard_map/ppermute | solution.py:377
  24.9 1.4 %collective-permute-done = f16[400,256]{1,0:T(8,128)(2,1)S(1)} collective-permute-done((f16[400,256]{1,0:T(8,128)(2,1)S(1)}, f16[400,256]{1,0:T(8,128)(2,1)S(1)}, u32[]{:S(2)}, u32[]{:S(2)}) %collective-permute-start) | collective-permute-done | bytes 204832 | tf_op jit(solution)/shard_map/ppermute | solution.py:377
  27.0 1.6 %collective-permute-start.7 = (f16[208,256]{1,0:T(8,128)(2,1)S(1)}, f16[208,256]{1,0:T(8,128)(2,1)S(1)}, u32[]{:S(2)}, u32[]{:S(2)}) collective-permute-start(f16[208,256]{1,0:T(8,128)(2,1)S(1)} %convert_element_type.76), channel_id=1, source_target_pairs={{0,1},{1,0},{2,3},{3,2},{4,5},{5,4},{6,7},{7,6},{8,9},{9,8},{10,11... | collective-permute-start | bytes 319496 | tf_op jit(solution)/shard_map/ppermute | solution.py:377
  29.1 1.6 %collective-permute-start.3 = (f16[400,256]{1,0:T(8,128)(2,1)S(1)}, f16[400,256]{1,0:T(8,128)(2,1)S(1)}, u32[]{:S(2)}, u32[]{:S(2)}) collective-permute-start(f16[400,256]{1,0:T(8,128)(2,1)S(1)} %convert_element_type.68), channel_id=1, source_target_pairs={{0,2},{2,0},{1,3},{3,1},{4,6},{6,4},{5,7},{7,5},{8,10},{10,8},{9,1... | collective-permute-start | bytes 614408 | tf_op jit(solution)/shard_map/ppermute | solution.py:377
  31.8 2.7 %collective-permute-done.6 = f16[208,256]{1,0:T(8,128)(2,1)S(1)} collective-permute-done((f16[208,256]{1,0:T(8,128)(2,1)S(1)}, f16[208,256]{1,0:T(8,128)(2,1)S(1)}, u32[]{:S(2)}, u32[]{:S(2)}) %collective-permute-start.6) | collective-permute-done | bytes 106528 | tf_op jit(solution)/shard_map/ppermute | solution.py:377
  35.2 2.7 %collective-permute-start.8 = (f16[208,512]{1,0:T(8,128)(2,1)S(1)}, f16[208,512]{1,0:T(8,128)(2,1)S(1)}, u32[]{:S(2)}, u32[]{:S(2)}) collective-permute-start(f16[208,512]{1,0:T(8,128)(2,1)S(1)} %convert_element_type.78), channel_id=1, source_target_pairs={{0,4},{4,0},{1,5},{5,1},{2,6},{6,2},{3,7},{7,3},{8,12},{12,8},{9,1... | collective-permute-start | bytes 638984 | tf_op jit(solution)/shard_map/ppermute | solution.py:377
  39.1 1.2 %shard_map.53 = (f32[208,256]{1,0:T(8,128)S(1)}, f32[208,256]{1,0:T(8,128)S(1)}, f32[192,256]{1,0:T(8,128)S(1)}, f32[192,256]{1,0:T(8,128)S(1)}, f32[8,512]{1,0:T(8,128)}) custom-call(s32[2]{0:T(128)S(1)} %pad_add_fusion.sides_ref, f32[8,512]{1,0:T(8,128)S(1)} %get-tuple-element.55.note_ref, f32[384,256]{1,0:T(8,128)S(1)} %get-tuple-element.56.refs_0_, ...), custom_call_target="tpu_custom_call" | custom-call | tf_op jit(solution)/shard_map/pallas_call | solution.py:333
  41.1 3.9 %collective-permute-done.5 = f16[208,256]{1,0:T(8,128)(2,1)S(1)} collective-permute-done((f16[208,256]{1,0:T(8,128)(2,1)S(1)}, f16[208,256]{1,0:T(8,128)(2,1)S(1)}, u32[]{:S(2)}, u32[]{:S(2)}) %collective-permute-start.5) | collective-permute-done | bytes 106528 | tf_op jit(solution)/shard_map/ppermute | solution.py:377
  45.1 1.2 %collective-permute-done.4 = f16[208,256]{1,0:T(8,128)(2,1)S(1)} collective-permute-done((f16[208,256]{1,0:T(8,128)(2,1)S(1)}, f16[208,256]{1,0:T(8,128)(2,1)S(1)}, u32[]{:S(2)}, u32[]{:S(2)}) %collective-permute-start.4) | collective-permute-done | bytes 106528 | tf_op jit(solution)/shard_map/ppermute | solution.py:377
  46.9 8.5 %all-gather.1 = bf16[832,512]{1,0:T(8,128)(2,1)S(1)} all-gather(bf16[208,512]{1,0:T(8,128)(2,1)S(1)} %get-tuple-element.77), channel_id=3, replica_groups=mesh['row'=2,'core'=2,'bit2'=2,'bit1'=2,'bit0'=2] {'row','core'}, dimensions={0}, use_global_device_ids=true | all-gather | bytes 1064960 | tf_op jit(solution)/shard_map/all_gather | solution.py:368
  55.5 2.2 %shard_map.56 = (bf16[400,256]{1,0:T(8,128)(2,1)S(1)}, bf16[400,256]{1,0:T(8,128)(2,1)S(1)}, bf16[400,256]{1,0:T(8,128)(2,1)S(1)}, bf16[400,256]{1,0:T(8,128)(2,...) custom-call(s32[3]{0:T(128)S(1)} %pad_add_fusion.1.sides_ref, ...), custom_call_target="tpu_custom_call" | custom-call | tf_op jit(solution)/shard_map/pallas_call | solution.py:333
  58.6 6.4 %collective-permute-done.9.refs_2_ = bf16[400,256]{1,0:T(8,128)(2,1)S(1)} collective-permute-done((bf16[400,256]{1,0:T(8,128)(2,1)S(1)}, bf16[400,256]{1,0:T(8,128)(2,1)S(1)}, u32[]{:S(2)}, u32[]{:S(2)}) %collective-permute-start.9) | collective-permute-done | bytes 204832 | tf_op jit(solution)/shard_map/ppermute | solution.py:377
  68.7 1.7 %collective-permute-start.12 = (bf16[400,256]{1,0:T(8,128)(2,1)S(1)}, bf16[400,256]{1,0:T(8,128)(2,1)S(1)}, u32[]{:S(2)}, u32[]{:S(2)}) collective-permute-start(bf16[400,256]{1,0:T(8,128)(2,1)S(1)} %get-tuple-element.89), channel_id=1, source_target_pairs={{0,2},{2,0},{1,3},{3,1},{4,6},{6,4},{5,7},{7,5},{8,10},{10,8},{9,1... | collective-permute-start | bytes 614408 | tf_op jit(solution)/shard_map/ppermute | solution.py:377
  70.4 1.8 %collective-permute-done.15.refs_2_ = bf16[208,256]{1,0:T(8,128)(2,1)S(1)} collective-permute-done((bf16[208,256]{1,0:T(8,128)(2,1)S(1)}, bf16[208,256]{1,0:T(8,128)(2,1)S(1)}, u32[]{:S(2)}, u32[]{:S(2)}) %collective-permute-start.15) | collective-permute-done | bytes 106528 | tf_op jit(solution)/shard_map/ppermute | solution.py:377
  72.5 2.5 %collective-permute-start.17 = (bf16[208,512]{1,0:T(8,128)(2,1)S(1)}, bf16[208,512]{1,0:T(8,128)(2,1)S(1)}, u32[]{:S(2)}, u32[]{:S(2)}) collective-permute-start(bf16[208,512]{1,0:T(8,128)(2,1)S(1)} %get-tuple-element.98), channel_id=1, source_target_pairs={{0,4},{4,0},{1,5},{5,1},{2,6},{6,2},{3,7},{7,3},{8,12},{12,8},{9,1... | collective-permute-start | bytes 638984 | tf_op jit(solution)/shard_map/ppermute | solution.py:377
  75.1 3.2 %collective-permute-done.12.refs_3_ = bf16[400,256]{1,0:T(8,128)(2,1)S(1)} collective-permute-done((bf16[400,256]{1,0:T(8,128)(2,1)S(1)}, bf16[400,256]{1,0:T(8,128)(2,1)S(1)}, u32[]{:S(2)}, u32[]{:S(2)}) %collective-permute-start.12) | collective-permute-done | bytes 204832 | tf_op jit(solution)/shard_map/ppermute | solution.py:377
  78.4 1.2 %shard_map.58 = (bf16[208,256]{1,0:T(8,128)(2,1)S(1)}, bf16[208,256]{1,0:T(8,128)(2,1)S(1)}, f32[192,256]{1,0:T(8,128)S(1)}, f32[192,256]{1,0:T(8,128)S(1)}, f32[8,512]{1,0:T(8,128)}) custom-call(s32[2]{0:T(128)S(1)} %pad_add_fusion.sides_ref, f32[8,512]{1,0:T(8,128)S(1)} %get-tuple-element.78.note_ref, f32[384,256]{1,0:T(8,128)S(1)} %get-tuple-element.79.refs_0_, ...), custom_call_target="tpu_custom_call" | custom-call | tf_op jit(solution)/shard_map/pallas_call | solution.py:333
  80.7 3.9 %collective-permute-done.13.refs_2_ = bf16[208,256]{1,0:T(8,128)(2,1)S(1)} collective-permute-done((bf16[208,256]{1,0:T(8,128)(2,1)S(1)}, bf16[208,256]{1,0:T(8,128)(2,1)S(1)}, u32[]{:S(2)}, u32[]{:S(2)}) %collective-permute-start.13) | collective-permute-done | bytes 106528 | tf_op jit(solution)/shard_map/ppermute | solution.py:377
  85.3 1.2 %collective-permute-done.18 = f32[16,128]{1,0:T(8,128)S(1)} collective-permute-done((f32[16,128]{1,0:T(8,128)S(1)}, f32[16,128]{1,0:T(8,128)S(1)}, u32[]{:S(2)}, u32[]{:S(2)}) %collective-permute-start.18) | collective-permute-done | bytes 8224 | tf_op jit(solution)/shard_map/ppermute | solution.py:468
  86.5 11.8 %all_to_all.5.flat_ref = f32[16,16,128]{2,1,0:T(8,128)S(1)} all-to-all(f32[16,16,128]{2,1,0:T(8,128)S(1)} %broadcast_in_dim.3), channel_id=1, replica_groups=mesh['row'=2,'core'=2,'bit2'=2,'bit1'=2,'bit0'=2] {'row','bit2','bit1','..., dimensions={0} | all-to-all | bytes 262144 | tf_op jit(solution)/shard_map/all_to_all | solution.py:470
  (61 shorter events, 16.2 us)
Async XLA Ops:
  0.6 0.9 copy-start.1
  1.5 1.0 %copy-start.3 = (f32[3,64,512]{2,1,0:T(8,128)S(1)}, f32[3,64,512]{2,1,0:T(8,128)}, u32[]{:S(2)}) copy-start(f32[3,64,512]{2,1,0:T(8,128)} %param.4) | copy-start | bytes 1179652
  2.5 11.5 %copy-start = (bf16[3,3,4,1,64,512]{5,4,3,2,1,0:T(8,128)(2,1)S(1)}, bf16[3,3,4,1,64,512]{5,4,3,2,1,0:T(8,128)(2,1)}, u32[]{:S(2)}) copy-start(bf16[3,3,4,1,64,512]{5,4,3,2,1,0:T(8,128)(2,1)} %param.3) | copy-start | bytes 7077892
  17.5 7.4 %collective-permute-start.1 = (f16[400,256]{1,0:T(8,128)(2,1)S(1)}, f16[400,256]{1,0:T(8,128)(2,1)S(1)}, u32[]{:S(2)}, u32[]{:S(2)}) collective-permute-start(f16[400,256]{1,0:T(8,128)(2,1)S(1)} %convert_element_type.64), channel_id=1, source_target_pairs={{0,2},{2,0},{1,3},{3,1},{4,6},{6,4},{5,7},{7,5},{8,10},{10,8},{9,1... | collective-permute-start | bytes 614408 | tf_op jit(solution)/shard_map/ppermute | solution.py:377
  19.2 7.1 %collective-permute-start = (f16[400,256]{1,0:T(8,128)(2,1)S(1)}, f16[400,256]{1,0:T(8,128)(2,1)S(1)}, u32[]{:S(2)}, u32[]{:S(2)}) collective-permute-start(f16[400,256]{1,0:T(8,128)(2,1)S(1)} %convert_element_type.62), channel_id=1, source_target_pairs={{0,1},{1,0},{2,3},{3,2},{4,5},{5,4},{6,7},{7,6},{8,9},{9,8},{10,11... | collective-permute-start | bytes 614408 | tf_op jit(solution)/shard_map/ppermute | solution.py:377
  27.0 4.8 %collective-permute-start.7 = (f16[208,256]{1,0:T(8,128)(2,1)S(1)}, f16[208,256]{1,0:T(8,128)(2,1)S(1)}, u32[]{:S(2)}, u32[]{:S(2)}) collective-permute-start(f16[208,256]{1,0:T(8,128)(2,1)S(1)} %convert_element_type.76), channel_id=1, source_target_pairs={{0,1},{1,0},{2,3},{3,2},{4,5},{5,4},{6,7},{7,6},{8,9},{9,8},{10,11... | collective-permute-start | bytes 319496 | tf_op jit(solution)/shard_map/ppermute | solution.py:377
  28.6 5.9 %collective-permute-start.6 = (f16[208,256]{1,0:T(8,128)(2,1)S(1)}, f16[208,256]{1,0:T(8,128)(2,1)S(1)}, u32[]{:S(2)}, u32[]{:S(2)}) collective-permute-start(f16[208,256]{1,0:T(8,128)(2,1)S(1)} %convert_element_type.74), channel_id=1, source_target_pairs={{0,2},{2,0},{1,3},{3,1},{4,6},{6,4},{5,7},{7,5},{8,10},{10,8},{9,1... | collective-permute-start | bytes 319496 | tf_op jit(solution)/shard_map/ppermute | solution.py:377
  29.1 9.9 %collective-permute-start.3 = (f16[400,256]{1,0:T(8,128)(2,1)S(1)}, f16[400,256]{1,0:T(8,128)(2,1)S(1)}, u32[]{:S(2)}, u32[]{:S(2)}) collective-permute-start(f16[400,256]{1,0:T(8,128)(2,1)S(1)} %convert_element_type.68), channel_id=1, source_target_pairs={{0,2},{2,0},{1,3},{3,1},{4,6},{6,4},{5,7},{7,5},{8,10},{10,8},{9,1... | collective-permute-start | bytes 614408 | tf_op jit(solution)/shard_map/ppermute | solution.py:377
  30.8 8.2 %collective-permute-start.2 = (f16[400,256]{1,0:T(8,128)(2,1)S(1)}, f16[400,256]{1,0:T(8,128)(2,1)S(1)}, u32[]{:S(2)}, u32[]{:S(2)}) collective-permute-start(f16[400,256]{1,0:T(8,128)(2,1)S(1)} %convert_element_type.66), channel_id=1, source_target_pairs={{0,1},{1,0},{2,3},{3,2},{4,5},{5,4},{6,7},{7,6},{8,9},{9,8},{10,11... | collective-permute-start | bytes 614408 | tf_op jit(solution)/shard_map/ppermute | solution.py:377
  35.2 11.2 %copy-start.2 = (f32[96,192]{1,0:T(8,128)S(1)}, f32[96,192]{1,0:T(8,128)}, u32[]{:S(2)}) copy-start(f32[96,192]{1,0:T(8,128)} %refs_8_.1) | copy-start | bytes 221188
  35.2 11.1 %collective-permute-start.8 = (f16[208,512]{1,0:T(8,128)(2,1)S(1)}, f16[208,512]{1,0:T(8,128)(2,1)S(1)}, u32[]{:S(2)}, u32[]{:S(2)}) collective-permute-start(f16[208,512]{1,0:T(8,128)(2,1)S(1)} %convert_element_type.78), channel_id=1, source_target_pairs={{0,4},{4,0},{1,5},{5,1},{2,6},{6,2},{3,7},{7,3},{8,12},{12,8},{9,1... | collective-permute-start | bytes 638984 | tf_op jit(solution)/shard_map/ppermute | solution.py:377
  40.3 4.8 %collective-permute-start.5 = (f16[208,256]{1,0:T(8,128)(2,1)S(1)}, f16[208,256]{1,0:T(8,128)(2,1)S(1)}, u32[]{:S(2)}, u32[]{:S(2)}) collective-permute-start(f16[208,256]{1,0:T(8,128)(2,1)S(1)} %convert_element_type.72), channel_id=1, source_target_pairs={{0,1},{1,0},{2,3},{3,2},{4,5},{5,4},{6,7},{7,6},{8,9},{9,8},{10,11... | collective-permute-start | bytes 319496 | tf_op jit(solution)/shard_map/ppermute | solution.py:377
  41.0 5.2 %collective-permute-start.4 = (f16[208,256]{1,0:T(8,128)(2,1)S(1)}, f16[208,256]{1,0:T(8,128)(2,1)S(1)}, u32[]{:S(2)}, u32[]{:S(2)}) collective-permute-start(f16[208,256]{1,0:T(8,128)(2,1)S(1)} %convert_element_type.70), channel_id=1, source_target_pairs={{0,2},{2,0},{1,3},{3,1},{4,6},{6,4},{5,7},{7,5},{8,10},{10,8},{9,1... | collective-permute-start | bytes 319496 | tf_op jit(solution)/shard_map/ppermute | solution.py:377
  57.6 7.4 %collective-permute-start.9 = (bf16[400,256]{1,0:T(8,128)(2,1)S(1)}, bf16[400,256]{1,0:T(8,128)(2,1)S(1)}, u32[]{:S(2)}, u32[]{:S(2)}) collective-permute-start(bf16[400,256]{1,0:T(8,128)(2,1)S(1)} %get-tuple-element.85), channel_id=1, source_target_pairs={{0,1},{1,0},{2,3},{3,2},{4,5},{5,4},{6,7},{7,6},{8,9},{9,8},{10,11... | collective-permute-start | bytes 614408 | tf_op jit(solution)/shard_map/ppermute | solution.py:377
  58.6 7.1 %collective-permute-start.10 = (bf16[400,256]{1,0:T(8,128)(2,1)S(1)}, bf16[400,256]{1,0:T(8,128)(2,1)S(1)}, u32[]{:S(2)}, u32[]{:S(2)}) collective-permute-start(bf16[400,256]{1,0:T(8,128)(2,1)S(1)} %get-tuple-element.86), channel_id=1, source_target_pairs={{0,2},{2,0},{1,3},{3,1},{4,6},{6,4},{5,7},{7,5},{8,10},{10,8},{9,1... | collective-permute-start | bytes 614408 | tf_op jit(solution)/shard_map/ppermute | solution.py:377
  66.3 5.9 %collective-permute-start.15 = (bf16[208,256]{1,0:T(8,128)(2,1)S(1)}, bf16[208,256]{1,0:T(8,128)(2,1)S(1)}, u32[]{:S(2)}, u32[]{:S(2)}) collective-permute-start(bf16[208,256]{1,0:T(8,128)(2,1)S(1)} %get-tuple-element.96), channel_id=1, source_target_pairs={{0,2},{2,0},{1,3},{3,1},{4,6},{6,4},{5,7},{7,5},{8,10},{10,8},{9,1... | collective-permute-start | bytes 319496 | tf_op jit(solution)/shard_map/ppermute | solution.py:377
  66.6 5.8 %collective-permute-start.16 = (bf16[208,256]{1,0:T(8,128)(2,1)S(1)}, bf16[208,256]{1,0:T(8,128)(2,1)S(1)}, u32[]{:S(2)}, u32[]{:S(2)}) collective-permute-start(bf16[208,256]{1,0:T(8,128)(2,1)S(1)} %get-tuple-element.97), channel_id=1, source_target_pairs={{0,1},{1,0},{2,3},{3,2},{4,5},{5,4},{6,7},{7,6},{8,9},{9,8},{10,11... | collective-permute-start | bytes 319496 | tf_op jit(solution)/shard_map/ppermute | solution.py:377
  67.8 7.3 %collective-permute-start.11 = (bf16[400,256]{1,0:T(8,128)(2,1)S(1)}, bf16[400,256]{1,0:T(8,128)(2,1)S(1)}, u32[]{:S(2)}, u32[]{:S(2)}) collective-permute-start(bf16[400,256]{1,0:T(8,128)(2,1)S(1)} %get-tuple-element.88), channel_id=1, source_target_pairs={{0,1},{1,0},{2,3},{3,2},{4,5},{5,4},{6,7},{7,6},{8,9},{9,8},{10,11... | collective-permute-start | bytes 614408 | tf_op jit(solution)/shard_map/ppermute | solution.py:377
  68.7 9.7 %collective-permute-start.12 = (bf16[400,256]{1,0:T(8,128)(2,1)S(1)}, bf16[400,256]{1,0:T(8,128)(2,1)S(1)}, u32[]{:S(2)}, u32[]{:S(2)}) collective-permute-start(bf16[400,256]{1,0:T(8,128)(2,1)S(1)} %get-tuple-element.89), channel_id=1, source_target_pairs={{0,2},{2,0},{1,3},{3,1},{4,6},{6,4},{5,7},{7,5},{8,10},{10,8},{9,1... | collective-permute-start | bytes 614408 | tf_op jit(solution)/shard_map/ppermute | solution.py:377
  72.5 12.1 %collective-permute-start.17 = (bf16[208,512]{1,0:T(8,128)(2,1)S(1)}, bf16[208,512]{1,0:T(8,128)(2,1)S(1)}, u32[]{:S(2)}, u32[]{:S(2)}) collective-permute-start(bf16[208,512]{1,0:T(8,128)(2,1)S(1)} %get-tuple-element.98), channel_id=1, source_target_pairs={{0,4},{4,0},{1,5},{5,1},{2,6},{6,2},{3,7},{7,3},{8,12},{12,8},{9,1... | collective-permute-start | bytes 638984 | tf_op jit(solution)/shard_map/ppermute | solution.py:377
  79.5 5.1 %collective-permute-start.13 = (bf16[208,256]{1,0:T(8,128)(2,1)S(1)}, bf16[208,256]{1,0:T(8,128)(2,1)S(1)}, u32[]{:S(2)}, u32[]{:S(2)}) collective-permute-start(bf16[208,256]{1,0:T(8,128)(2,1)S(1)} %get-tuple-element.92), channel_id=1, source_target_pairs={{0,2},{2,0},{1,3},{3,1},{4,6},{6,4},{5,7},{7,5},{8,10},{10,8},{9,1... | collective-permute-start | bytes 319496 | tf_op jit(solution)/shard_map/ppermute | solution.py:377
  79.5 5.1 %collective-permute-start.14 = (bf16[208,256]{1,0:T(8,128)(2,1)S(1)}, bf16[208,256]{1,0:T(8,128)(2,1)S(1)}, u32[]{:S(2)}, u32[]{:S(2)}) collective-permute-start(bf16[208,256]{1,0:T(8,128)(2,1)S(1)} %get-tuple-element.93), channel_id=1, source_target_pairs={{0,1},{1,0},{2,3},{3,2},{4,5},{5,4},{6,7},{7,6},{8,9},{9,8},{10,11... | collective-permute-start | bytes 319496 | tf_op jit(solution)/shard_map/ppermute | solution.py:377
  85.2 1.2 %collective-permute-start.18 = (f32[16,128]{1,0:T(8,128)S(1)}, f32[16,128]{1,0:T(8,128)S(1)}, u32[]{:S(2)}, u32[]{:S(2)}) collective-permute-start(f32[16,128]{1,0:T(8,128)S(1)} %get-tuple-element.101), channel_id=1, source_target_pairs={{0,8},{8,0},{1,9},{9,1},{2,10},{10,2},{3,11},{11,3},{4,12},{12,4},... | collective-permute-start | bytes 24584 | tf_op jit(solution)/shard_map/ppermute | solution.py:468

commit v7 on v6

--- a/solution.py
+++ b/solution.py
@@ -9,7 +9,7 @@
 
 FIBER_NODES = 32
 PIECES = 3
-EXTRA = 16
+EXTRA = 8
 NOTE = 8
 SWAP = [(0, 1), (1, 0)]
 TINY = 1e-06
@@ -150,8 +150,16 @@
     return jnp.sum(first * second, axis=0, keepdims=True)
 
 
-def first_body(right_ref, precond_ref, start_ref, sent_ref):
+def first_body(right_hbm, precond_hbm, start_ref, sent_ref, right_ref, precond_ref, marks):
     height = start_ref.shape[0]
+    loads = [
+        pltpu.make_async_copy(right_hbm, right_ref, marks.at[0]),
+        pltpu.make_async_copy(precond_hbm, precond_ref, marks.at[1]),
+    ]
+    for load in loads:
+        load.start()
+    for load in loads:
+        load.wait()
     start = blocks_times(precond_ref[...], right_ref[...])
     start_ref[...] = start
     note = Scale(jnp.max(jnp.abs(start), axis=0, keepdims=True))
@@ -159,8 +167,8 @@
     sent_ref[height:] = note.packed
 
 
-def couple_body(kind, places, sides_ref, tile_ref, got_ref, *refs):
-    sends, keeps, note_ref, work_ref = refs[0:4], refs[4:8], refs[8], refs[9]
+def couple_body(kind, places, near, sides_ref, tile_ref, got_ref, *refs):
+    sends, keeps, note_ref, work_ref = refs[0:2], refs[2:4], refs[4], refs[5]
     sources = got_ref.shape[0]
     height = got_ref.shape[1] - EXTRA
     nodes = height // 3
@@ -183,8 +191,11 @@
     else:
         note = Sums(functools.reduce(jnp.add, others))
     note_ref[...] = note.rows()
+    reach = targets // 2 * nodes
+    base = (sides_ref[2] if near else 1 - sides_ref[2]) * reach
     for comp in range(3):
-        left = tile_ref[:, comp].reshape(value.shape[0], targets * nodes)
+        left = tile_ref[:, comp, :, pl.ds(pl.multiple_of(base, reach), reach)]
+        left = left.reshape(value.shape[0], reach)
         total = 0.0
         for term in terms:
             total = total + lax.dot_general(
@@ -192,25 +203,22 @@
             )
         work_ref[comp] = total
     slots = targets // 4
-    top = sides_ref[2]
     for colour in range(2):
         first = colour * half
         columns = slice(first, first + half)
         side = sides_ref[colour]
         inner_note = type(note).load(note_ref[:, columns])
-        for near in range(2):
-            base = (top if near else 1 - top) * (targets // 2)
-            send, kept = sends[near * 2 + colour], keeps[near * 2 + colour]
-            for slot in range(slots):
-                give = (base + insert(slot, places[colour], 1 - side)) * nodes
-                keep = (base + insert(slot, places[colour], side)) * nodes
-                for comp in range(3):
-                    row = slot * height + comp * nodes
-                    value = work_ref[comp, pl.ds(pl.multiple_of(give, nodes), nodes), columns]
-                    send[row : row + nodes] = inner_note.pack(value)
-                    value = work_ref[comp, pl.ds(pl.multiple_of(keep, nodes), nodes), columns]
-                    kept[row : row + nodes] = value
-            send[slots * height :] = inner_note.packed
+        send, kept = sends[colour], keeps[colour]
+        for slot in range(slots):
+            give = insert(slot, places[colour], 1 - side) * nodes
+            keep = insert(slot, places[colour], side) * nodes
+            for comp in range(3):
+                row = slot * height + comp * nodes
+                value = work_ref[comp, pl.ds(pl.multiple_of(give, nodes), nodes), columns]
+                send[row : row + nodes] = inner_note.pack(value)
+                value = work_ref[comp, pl.ds(pl.multiple_of(keep, nodes), nodes), columns]
+                kept[row : row + nodes] = value
+        send[slots * height :] = inner_note.packed
 
 
 def merge_body(kind, places, height, sides_ref, note_ref, *refs):
@@ -325,16 +333,16 @@
 
 def call(body, shapes, *args, scalars=0, outside=0, scratch=(), hold=True):
     spec = pl.BlockSpec(memory_space=pltpu.VMEM)
+    far = pl.BlockSpec(memory_space=pltpu.HBM)
     small = pl.BlockSpec(memory_space=pltpu.SMEM)
-    held = list(args[scalars:])
-    if hold:
-        held = [pltpu.with_memory_space_constraint(arg, pltpu.VMEM) for arg in held]
+    place = pltpu.VMEM if hold else pltpu.HBM
+    held = [pltpu.with_memory_space_constraint(arg, place) for arg in args[scalars:]]
     inside = len(shapes) - outside
     return pl.pallas_call(
         body,
         out_shape=[pltpu.VMEM(shape, dtype) for shape, dtype in shapes[:inside]]
         + [jax.ShapeDtypeStruct(shape, dtype) for shape, dtype in shapes[inside:]],
-        in_specs=[small] * scalars + [spec] * len(held),
+        in_specs=[small] * scalars + [spec if hold else far] * len(held),
         out_specs=[spec] * len(shapes),
         scratch_shapes=list(scratch),
         compiler_params=pltpu.CompilerParams(vmem_limit_bytes=20 * 1024 * 1024),
@@ -396,17 +404,19 @@
             names, places = take(0)
             slots = slots // 2
             sent, kept = shapes(slots)
-            outs = call(
-                functools.partial(couple_body, kind, places),
-                sent * 4 + kept * 4 + [note],
-                sides(names + [bits[0]]),
-                tile,
-                got,
-                scalars=1,
-                scratch=[pltpu.VMEM((3, row_count, cases), F32)],
-            )
-            near = [outs[2:4], outs[6:8], outs[8]]
-            far = [outs[0:2], outs[4:6], outs[8]]
+            pair = []
+            for near in range(2):
+                outs = call(
+                    functools.partial(couple_body, kind, places, near),
+                    sent * 2 + kept * 2 + [note],
+                    sides(names + [bits[0]]),
+                    tile,
+                    got,
+                    scalars=1,
+                    scratch=[pltpu.VMEM((3, row_count // 2, cases), F32)],
+                )
+                pair.append([outs[0:2], outs[2:4], outs[4]])
+            far, near = pair
             plan = [(names, None)]
             for step in range(1, len(lower)):
                 plan.append(take(step))
@@ -415,6 +425,8 @@
                 count = slots
                 sends, kept, notes = state
                 arrived = swap(sends, plan[0][0], kind)
+                if tie is not None:
+                    arrived = list(lax.optimization_barrier(tuple(arrived) + (near[2],))[:2])
                 for names, places in plan[1:]:
                     count = count // 2
                     sent, keep = shapes(count)
@@ -451,7 +463,18 @@
 
         full = ((height, cases), F32)
         packed = ((height + EXTRA, cases), F32)
-        start, sent = call(first_body, [full, packed], right, precond, hold=False)
+        start, sent = call(
+            first_body,
+            [full, packed],
+            right,
+            precond,
+            hold=False,
+            scratch=[
+                pltpu.VMEM(right.shape, F32),
+                pltpu.VMEM(precond.shape, F32),
+                pltpu.SemaphoreType.DMA((2,)),
+            ],
+        )
         shares, _ = exchange(gather(sent, Scale), Scale)
         packed = ((height + EXTRA, cases), BF16)
         work, sent = call(second_body, [full, packed], *shares, start, precond)

time: 99.4 us -> 95.5 us (0.961)
  waiting for transfers between devices: 32.3 us -> 27.1 us
  Pallas kernels: 12.6 us -> 15.4 us
  local copies, waits for them, and re-layouts: 1.91 us -> 0.02 us
    ppermute x18, waiting for transfers between devices: 31.1 us -> 25.9 us  [swap(): lax.ppermute(cast(a, kind), name, SWAP)]
    pallas_call x12 -> x14, Pallas kernels: 12.6 us -> 15.4 us  [call(): pl.pallas_call(body, out_shape=[pltpu.VMEM(shape, dtype) for shape, dtype...]
    unnamed x8 -> x4, local copies, waits for them, and re-layouts: 1.89 us -> 0.01 us
  transfers between devices with their start and end apart: 19 -> 19, of which waited for: 14 -> 14; matrix products, arithmetic and copies ran while one was open for 0% -> 0% of each run, Pallas kernels for 3% -> 7%
where the time goes in v7:
time: 95.5 us; the launch traced here: 95.3 us
  blocking collectives  30.9 us (32%)
  waiting for transfers between devices  27.1 us (28%)
  starting transfers between devices  20.2 us (21%)
  Pallas kernels  15.4 us (16%)
    ppermute x18, waiting for transfers between devices, swap(): lax.ppermute(cast(a, kind), name, SWAP)  25.9 us
    ppermute x18, starting transfers between devices, swap(): lax.ppermute(cast(a, kind), name, SWAP)  20.1 us
    all_gather x2, blocking collectives, gather(): return travel(sent, kind, lambda a: lax.all_gather(a, ('row', 'core')))  18.6 us
    pallas_call x14, Pallas kernels, call(): pl.pallas_call(body, out_shape=[pltpu.VMEM(shape, dtype) for shape, dtype...  15.4 us
    all_to_all x1, blocking collectives, local(): lax.all_to_all(jnp.broadcast_to(flat, (members,) + flat.shape), ('row',)...  12.2 us
  transfers between devices with their start and end apart: 19, of which 14 were waited for; matrix products, arithmetic and copies ran while one was open for 0% of the time, Pallas kernels for 7%

profile of v7, /device:TPU:0, one launch (start us, length us, event | category | flops | bytes accessed | tf_op | source)
XLA Modules:
  0.0 95.3 jit_solution(14873183065817091674)
XLA Ops:
  0.6 1.7 %shard_map.50 = (f32[192,512]{1,0:T(8,128)S(1)}, f32[200,512]{1,0:T(8,128)S(1)}) custom-call(f32[192,512]{1,0:T(8,128)} %bitcast.16, f32[96,192]{1,0:T(8,128)} %refs_8_.1), custom_call_target="tpu_custom_call" | custom-call | tf_op jit(solution)/shard_map/pallas_call | solution.py:341
  2.4 10.3 %all-gather = f16[800,512]{1,0:T(8,128)(2,1)S(1)} all-gather(f16[200,512]{1,0:T(8,128)(2,1)S(1)} %convert_element_type.60), channel_id=2, replica_groups=mesh['row'=2,'core'=2,'bit2'=2,'bit1'=2,'bit0'=2] {'row','core'}, dimensions={0}, use_global_device_ids=true | all-gather | bytes 1024000 | tf_op jit(solution)/shard_map/all_gather | solution.py:376
  13.0 2.2 %shard_map.52 = (f32[392,256]{1,0:T(8,128)S(1)}, f32[392,256]{1,0:T(8,128)S(1)}, f32[384,256]{1,0:T(8,128)S(1)}, f32[384,256]{1,0:T(8,128)S(1)}, f32[8,512]{1,0:T(8,128)S(1)}) custom-call(s32[3]{0:T(128)S(1)} %pad_add_fusion.1.sides_ref, bf16[3,3,256,512]{3,2,1,0:T(8,128)(2,1)S(1)} %bitcast.9, f32[4,200,512]{2,1,0:T(8,128)S(1)} %convert.got_ref), custom_call_target="tpu_custom_call" | custom-call | tf_op jit(solution)/shard_map/pallas_call | solution.py:341
  15.2 1.6 %collective-permute-start.1 = (f16[392,256]{1,0:T(8,128)(2,1)S(1)}, f16[392,256]{1,0:T(8,128)(2,1)S(1)}, u32[]{:S(2)}, u32[]{:S(2)}) collective-permute-start(f16[392,256]{1,0:T(8,128)(2,1)S(1)} %convert_element_type.64), channel_id=1, source_target_pairs={{0,2},{2,0},{1,3},{3,1},{4,6},{6,4},{5,7},{7,5},{8,10},{10,8},{9,1... | collective-permute-start | bytes 602120 | tf_op jit(solution)/shard_map/ppermute | solution.py:385
  16.9 1.6 %collective-permute-start = (f16[392,256]{1,0:T(8,128)(2,1)S(1)}, f16[392,256]{1,0:T(8,128)(2,1)S(1)}, u32[]{:S(2)}, u32[]{:S(2)}) collective-permute-start(f16[392,256]{1,0:T(8,128)(2,1)S(1)} %convert_element_type.62), channel_id=1, source_target_pairs={{0,1},{1,0},{2,3},{3,2},{4,5},{5,4},{6,7},{7,6},{8,9},{9,8},{10,11... | collective-permute-start | bytes 602120 | tf_op jit(solution)/shard_map/ppermute | solution.py:385
  18.4 2.2 %shard_map.51 = (f32[392,256]{1,0:T(8,128)S(1)}, f32[392,256]{1,0:T(8,128)S(1)}, f32[384,256]{1,0:T(8,128)S(1)}, f32[384,256]{1,0:T(8,128)S(1)}, f32[8,512]{1,0:T(8,128)S(1)}) custom-call(s32[3]{0:T(128)S(1)} %pad_add_fusion.1.sides_ref, bf16[3,3,256,512]{3,2,1,0:T(8,128)(2,1)S(1)} %bitcast.10, f32[4,200,512]{2,1,0:T(8,128)S(1)} %convert.got_ref), custom_call_target="tpu_custom_call" | custom-call | tf_op jit(solution)/shard_map/pallas_call | solution.py:341
  20.7 1.8 %collective-permute-done.1 = f16[392,256]{1,0:T(8,128)(2,1)S(1)} collective-permute-done((f16[392,256]{1,0:T(8,128)(2,1)S(1)}, f16[392,256]{1,0:T(8,128)(2,1)S(1)}, u32[]{:S(2)}, u32[]{:S(2)}) %collective-permute-start.1) | collective-permute-done | bytes 200736 | tf_op jit(solution)/shard_map/ppermute | solution.py:385
  22.5 1.4 %collective-permute-done = f16[392,256]{1,0:T(8,128)(2,1)S(1)} collective-permute-done((f16[392,256]{1,0:T(8,128)(2,1)S(1)}, f16[392,256]{1,0:T(8,128)(2,1)S(1)}, u32[]{:S(2)}, u32[]{:S(2)}) %collective-permute-start) | collective-permute-done | bytes 200736 | tf_op jit(solution)/shard_map/ppermute | solution.py:385
  24.6 1.6 %collective-permute-start.7 = (f16[200,256]{1,0:T(8,128)(2,1)S(1)}, f16[200,256]{1,0:T(8,128)(2,1)S(1)}, u32[]{:S(2)}, u32[]{:S(2)}) collective-permute-start(f16[200,256]{1,0:T(8,128)(2,1)S(1)} %convert_element_type.76), channel_id=1, source_target_pairs={{0,1},{1,0},{2,3},{3,2},{4,5},{5,4},{6,7},{7,6},{8,9},{9,8},{10,11... | collective-permute-start | bytes 307208 | tf_op jit(solution)/shard_map/ppermute | solution.py:385
  26.7 1.6 %collective-permute-start.3 = (f16[392,256]{1,0:T(8,128)(2,1)S(1)}, f16[392,256]{1,0:T(8,128)(2,1)S(1)}, u32[]{:S(2)}, u32[]{:S(2)}) collective-permute-start(f16[392,256]{1,0:T(8,128)(2,1)S(1)} %convert_element_type.68), channel_id=1, source_target_pairs={{0,2},{2,0},{1,3},{3,1},{4,6},{6,4},{5,7},{7,5},{8,10},{10,8},{9,1... | collective-permute-start | bytes 602120 | tf_op jit(solution)/shard_map/ppermute | solution.py:385
  29.4 2.7 %collective-permute-done.6 = f16[200,256]{1,0:T(8,128)(2,1)S(1)} collective-permute-done((f16[200,256]{1,0:T(8,128)(2,1)S(1)}, f16[200,256]{1,0:T(8,128)(2,1)S(1)}, u32[]{:S(2)}, u32[]{:S(2)}) %collective-permute-start.6) | collective-permute-done | bytes 102432 | tf_op jit(solution)/shard_map/ppermute | solution.py:385
  32.8 2.6 %collective-permute-start.8 = (f16[200,512]{1,0:T(8,128)(2,1)S(1)}, f16[200,512]{1,0:T(8,128)(2,1)S(1)}, u32[]{:S(2)}, u32[]{:S(2)}) collective-permute-start(f16[200,512]{1,0:T(8,128)(2,1)S(1)} %convert_element_type.78), channel_id=1, source_target_pairs={{0,4},{4,0},{1,5},{5,1},{2,6},{6,2},{3,7},{7,3},{8,12},{12,8},{9,1... | collective-permute-start | bytes 614408 | tf_op jit(solution)/shard_map/ppermute | solution.py:385
  38.5 3.7 %collective-permute-done.5 = f16[200,256]{1,0:T(8,128)(2,1)S(1)} collective-permute-done((f16[200,256]{1,0:T(8,128)(2,1)S(1)}, f16[200,256]{1,0:T(8,128)(2,1)S(1)}, u32[]{:S(2)}, u32[]{:S(2)}) %collective-permute-start.5) | collective-permute-done | bytes 102432 | tf_op jit(solution)/shard_map/ppermute | solution.py:385
  42.2 1.2 %collective-permute-done.4 = f16[200,256]{1,0:T(8,128)(2,1)S(1)} collective-permute-done((f16[200,256]{1,0:T(8,128)(2,1)S(1)}, f16[200,256]{1,0:T(8,128)(2,1)S(1)}, u32[]{:S(2)}, u32[]{:S(2)}) %collective-permute-start.4) | collective-permute-done | bytes 102432 | tf_op jit(solution)/shard_map/ppermute | solution.py:385
  44.1 8.4 %all-gather.1 = bf16[800,512]{1,0:T(8,128)(2,1)S(1)} all-gather(bf16[200,512]{1,0:T(8,128)(2,1)S(1)} %get-tuple-element.86), channel_id=3, replica_groups=mesh['row'=2,'core'=2,'bit2'=2,'bit1'=2,'bit0'=2] {'row','core'}, dimensions={0}, use_global_device_ids=true | all-gather | bytes 1024000 | tf_op jit(solution)/shard_map/all_gather | solution.py:376
  52.5 1.4 %shard_map.58 = (bf16[392,256]{1,0:T(8,128)(2,1)S(1)}, bf16[392,256]{1,0:T(8,128)(2,1)S(1)}, f32[384,256]{1,0:T(8,128)S(1)}, f32[384,256]{1,0:T(8,128)S(1)}, f32[8,512]{1,0:T(8,128)S(1)}) custom-call(s32[3]{0:T(128)S(1)} %pad_add_fusion.1.sides_ref, bf16[3,3,256,512]{3,2,1,0:T(8,128)(2,1)S(1)} %bitcast.11, bf16[4,200,512]{2,1,0:T(8,128)(2,1)S(1)} %bitcast.13), custom_call_target="tpu_custom_call" | custom-call | tf_op jit(solution)/shard_map/pallas_call | solution.py:341
  54.9 1.5 %shard_map.57 = (bf16[392,256]{1,0:T(8,128)(2,1)S(1)}, bf16[392,256]{1,0:T(8,128)(2,1)S(1)}, f32[384,256]{1,0:T(8,128)S(1)}, f32[384,256]{1,0:T(8,128)S(1)}, f32[8,512]{1,0:T(8,128)S(1)}) custom-call(s32[3]{0:T(128)S(1)} %pad_add_fusion.1.sides_ref, bf16[3,3,256,512]{3,2,1,0:T(8,128)(2,1)S(1)} %bitcast.12, bf16[4,200,512]{2,1,0:T(8,128)(2,1)S(1)} %bitcast.14), custom_call_target="tpu_custom_call" | custom-call | tf_op jit(solution)/shard_map/pallas_call | solution.py:341
  56.3 4.9 %collective-permute-done.9.refs_2_ = bf16[392,256]{1,0:T(8,128)(2,1)S(1)} collective-permute-done((bf16[392,256]{1,0:T(8,128)(2,1)S(1)}, bf16[392,256]{1,0:T(8,128)(2,1)S(1)}, u32[]{:S(2)}, u32[]{:S(2)}) %collective-permute-start.9) | collective-permute-done | bytes 200736 | tf_op jit(solution)/shard_map/ppermute | solution.py:385
  64.8 1.7 %collective-permute-start.12 = (bf16[392,256]{1,0:T(8,128)(2,1)S(1)}, bf16[392,256]{1,0:T(8,128)(2,1)S(1)}, u32[]{:S(2)}, u32[]{:S(2)}) collective-permute-start(bf16[392,256]{1,0:T(8,128)(2,1)S(1)} %get-tuple-element.101), channel_id=1, source_target_pairs={{0,2},{2,0},{1,3},{3,1},{4,6},{6,4},{5,7},{7,5},{8,10},{10,8},{9,1... | collective-permute-start | bytes 602120 | tf_op jit(solution)/shard_map/ppermute | solution.py:385
  66.6 1.7 %collective-permute-done.15.refs_2_ = bf16[200,256]{1,0:T(8,128)(2,1)S(1)} collective-permute-done((bf16[200,256]{1,0:T(8,128)(2,1)S(1)}, bf16[200,256]{1,0:T(8,128)(2,1)S(1)}, u32[]{:S(2)}, u32[]{:S(2)}) %collective-permute-start.15) | collective-permute-done | bytes 102432 | tf_op jit(solution)/shard_map/ppermute | solution.py:385
  68.6 2.8 %collective-permute-start.17 = (bf16[200,512]{1,0:T(8,128)(2,1)S(1)}, bf16[200,512]{1,0:T(8,128)(2,1)S(1)}, u32[]{:S(2)}, u32[]{:S(2)}) collective-permute-start(bf16[200,512]{1,0:T(8,128)(2,1)S(1)} %get-tuple-element.110), channel_id=1, source_target_pairs={{0,4},{4,0},{1,5},{5,1},{2,6},{6,2},{3,7},{7,3},{8,12},{12,8},{9,1... | collective-permute-start | bytes 614408 | tf_op jit(solution)/shard_map/ppermute | solution.py:385
  71.4 2.8 %collective-permute-done.12.refs_3_ = bf16[392,256]{1,0:T(8,128)(2,1)S(1)} collective-permute-done((bf16[392,256]{1,0:T(8,128)(2,1)S(1)}, bf16[392,256]{1,0:T(8,128)(2,1)S(1)}, u32[]{:S(2)}, u32[]{:S(2)}) %collective-permute-start.12) | collective-permute-done | bytes 200736 | tf_op jit(solution)/shard_map/ppermute | solution.py:385
  76.5 3.8 %collective-permute-done.13.refs_2_ = bf16[200,256]{1,0:T(8,128)(2,1)S(1)} collective-permute-done((bf16[200,256]{1,0:T(8,128)(2,1)S(1)}, bf16[200,256]{1,0:T(8,128)(2,1)S(1)}, u32[]{:S(2)}, u32[]{:S(2)}) %collective-permute-start.13) | collective-permute-done | bytes 102432 | tf_op jit(solution)/shard_map/ppermute | solution.py:385
  82.2 12.2 %all_to_all.5.flat_ref = f32[16,16,128]{2,1,0:T(8,128)S(1)} all-to-all(f32[16,16,128]{2,1,0:T(8,128)S(1)} %broadcast_in_dim.3), channel_id=1, replica_groups=mesh['row'=2,'core'=2,'bit2'=2,'bit1'=2,'bit0'=2] {'row','bit2','bit1','..., dimensions={0} | all-to-all | bytes 262144 | tf_op jit(solution)/shard_map/all_to_all | solution.py:493
  (59 shorter events, 17.0 us)
Async XLA Ops:
  0.6 12.4 %copy-start = (bf16[3,3,4,1,64,512]{5,4,3,2,1,0:T(8,128)(2,1)S(1)}, bf16[3,3,4,1,64,512]{5,4,3,2,1,0:T(8,128)(2,1)}, u32[]{:S(2)}) copy-start(bf16[3,3,4,1,64,512]{5,4,3,2,1,0:T(8,128)(2,1)} %param.3) | copy-start | bytes 7077892
  15.2 7.3 %collective-permute-start.1 = (f16[392,256]{1,0:T(8,128)(2,1)S(1)}, f16[392,256]{1,0:T(8,128)(2,1)S(1)}, u32[]{:S(2)}, u32[]{:S(2)}) collective-permute-start(f16[392,256]{1,0:T(8,128)(2,1)S(1)} %convert_element_type.64), channel_id=1, source_target_pairs={{0,2},{2,0},{1,3},{3,1},{4,6},{6,4},{5,7},{7,5},{8,10},{10,8},{9,1... | collective-permute-start | bytes 602120 | tf_op jit(solution)/shard_map/ppermute | solution.py:385
  16.9 7.0 %collective-permute-start = (f16[392,256]{1,0:T(8,128)(2,1)S(1)}, f16[392,256]{1,0:T(8,128)(2,1)S(1)}, u32[]{:S(2)}, u32[]{:S(2)}) collective-permute-start(f16[392,256]{1,0:T(8,128)(2,1)S(1)} %convert_element_type.62), channel_id=1, source_target_pairs={{0,1},{1,0},{2,3},{3,2},{4,5},{5,4},{6,7},{7,6},{8,9},{9,8},{10,11... | collective-permute-start | bytes 602120 | tf_op jit(solution)/shard_map/ppermute | solution.py:385
  24.6 4.7 %collective-permute-start.7 = (f16[200,256]{1,0:T(8,128)(2,1)S(1)}, f16[200,256]{1,0:T(8,128)(2,1)S(1)}, u32[]{:S(2)}, u32[]{:S(2)}) collective-permute-start(f16[200,256]{1,0:T(8,128)(2,1)S(1)} %convert_element_type.76), channel_id=1, source_target_pairs={{0,1},{1,0},{2,3},{3,2},{4,5},{5,4},{6,7},{7,6},{8,9},{9,8},{10,11... | collective-permute-start | bytes 307208 | tf_op jit(solution)/shard_map/ppermute | solution.py:385
  26.2 5.8 %collective-permute-start.6 = (f16[200,256]{1,0:T(8,128)(2,1)S(1)}, f16[200,256]{1,0:T(8,128)(2,1)S(1)}, u32[]{:S(2)}, u32[]{:S(2)}) collective-permute-start(f16[200,256]{1,0:T(8,128)(2,1)S(1)} %convert_element_type.74), channel_id=1, source_target_pairs={{0,2},{2,0},{1,3},{3,1},{4,6},{6,4},{5,7},{7,5},{8,10},{10,8},{9,1... | collective-permute-start | bytes 307208 | tf_op jit(solution)/shard_map/ppermute | solution.py:385
  26.7 9.5 %collective-permute-start.3 = (f16[392,256]{1,0:T(8,128)(2,1)S(1)}, f16[392,256]{1,0:T(8,128)(2,1)S(1)}, u32[]{:S(2)}, u32[]{:S(2)}) collective-permute-start(f16[392,256]{1,0:T(8,128)(2,1)S(1)} %convert_element_type.68), channel_id=1, source_target_pairs={{0,2},{2,0},{1,3},{3,1},{4,6},{6,4},{5,7},{7,5},{8,10},{10,8},{9,1... | collective-permute-start | bytes 602120 | tf_op jit(solution)/shard_map/ppermute | solution.py:385
  28.4 7.8 %collective-permute-start.2 = (f16[392,256]{1,0:T(8,128)(2,1)S(1)}, f16[392,256]{1,0:T(8,128)(2,1)S(1)}, u32[]{:S(2)}, u32[]{:S(2)}) collective-permute-start(f16[392,256]{1,0:T(8,128)(2,1)S(1)} %convert_element_type.66), channel_id=1, source_target_pairs={{0,1},{1,0},{2,3},{3,2},{4,5},{5,4},{6,7},{7,6},{8,9},{9,8},{10,11... | collective-permute-start | bytes 602120 | tf_op jit(solution)/shard_map/ppermute | solution.py:385
  32.7 10.8 %copy-start.1 = (f32[96,192]{1,0:T(8,128)S(1)}, f32[96,192]{1,0:T(8,128)}, u32[]{:S(2)}) copy-start(f32[96,192]{1,0:T(8,128)} %refs_8_.1) | copy-start | bytes 221188
  32.8 10.7 %collective-permute-start.8 = (f16[200,512]{1,0:T(8,128)(2,1)S(1)}, f16[200,512]{1,0:T(8,128)(2,1)S(1)}, u32[]{:S(2)}, u32[]{:S(2)}) collective-permute-start(f16[200,512]{1,0:T(8,128)(2,1)S(1)} %convert_element_type.78), channel_id=1, source_target_pairs={{0,4},{4,0},{1,5},{5,1},{2,6},{6,2},{3,7},{7,3},{8,12},{12,8},{9,1... | collective-permute-start | bytes 614408 | tf_op jit(solution)/shard_map/ppermute | solution.py:385
  37.5 4.7 %collective-permute-start.5 = (f16[200,256]{1,0:T(8,128)(2,1)S(1)}, f16[200,256]{1,0:T(8,128)(2,1)S(1)}, u32[]{:S(2)}, u32[]{:S(2)}) collective-permute-start(f16[200,256]{1,0:T(8,128)(2,1)S(1)} %convert_element_type.72), channel_id=1, source_target_pairs={{0,1},{1,0},{2,3},{3,2},{4,5},{5,4},{6,7},{7,6},{8,9},{9,8},{10,11... | collective-permute-start | bytes 307208 | tf_op jit(solution)/shard_map/ppermute | solution.py:385
  38.4 5.1 %collective-permute-start.4 = (f16[200,256]{1,0:T(8,128)(2,1)S(1)}, f16[200,256]{1,0:T(8,128)(2,1)S(1)}, u32[]{:S(2)}, u32[]{:S(2)}) collective-permute-start(f16[200,256]{1,0:T(8,128)(2,1)S(1)} %convert_element_type.70), channel_id=1, source_target_pairs={{0,2},{2,0},{1,3},{3,1},{4,6},{6,4},{5,7},{7,5},{8,10},{10,8},{9,1... | collective-permute-start | bytes 307208 | tf_op jit(solution)/shard_map/ppermute | solution.py:385
  53.9 7.3 %collective-permute-start.9 = (bf16[392,256]{1,0:T(8,128)(2,1)S(1)}, bf16[392,256]{1,0:T(8,128)(2,1)S(1)}, u32[]{:S(2)}, u32[]{:S(2)}) collective-permute-start(bf16[392,256]{1,0:T(8,128)(2,1)S(1)} %get-tuple-element.95), channel_id=1, source_target_pairs={{0,1},{1,0},{2,3},{3,2},{4,5},{5,4},{6,7},{7,6},{8,9},{9,8},{10,11... | collective-permute-start | bytes 602120 | tf_op jit(solution)/shard_map/ppermute | solution.py:385
  54.9 7.0 %collective-permute-start.10 = (bf16[392,256]{1,0:T(8,128)(2,1)S(1)}, bf16[392,256]{1,0:T(8,128)(2,1)S(1)}, u32[]{:S(2)}, u32[]{:S(2)}) collective-permute-start(bf16[392,256]{1,0:T(8,128)(2,1)S(1)} %get-tuple-element.96), channel_id=1, source_target_pairs={{0,2},{2,0},{1,3},{3,1},{4,6},{6,4},{5,7},{7,5},{8,10},{10,8},{9,1... | collective-permute-start | bytes 602120 | tf_op jit(solution)/shard_map/ppermute | solution.py:385
  62.5 5.8 %collective-permute-start.15 = (bf16[200,256]{1,0:T(8,128)(2,1)S(1)}, bf16[200,256]{1,0:T(8,128)(2,1)S(1)}, u32[]{:S(2)}, u32[]{:S(2)}) collective-permute-start(bf16[200,256]{1,0:T(8,128)(2,1)S(1)} %get-tuple-element.108), channel_id=1, source_target_pairs={{0,2},{2,0},{1,3},{3,1},{4,6},{6,4},{5,7},{7,5},{8,10},{10,8},{9,1... | collective-permute-start | bytes 307208 | tf_op jit(solution)/shard_map/ppermute | solution.py:385
  62.8 5.8 %collective-permute-start.16 = (bf16[200,256]{1,0:T(8,128)(2,1)S(1)}, bf16[200,256]{1,0:T(8,128)(2,1)S(1)}, u32[]{:S(2)}, u32[]{:S(2)}) collective-permute-start(bf16[200,256]{1,0:T(8,128)(2,1)S(1)} %get-tuple-element.109), channel_id=1, source_target_pairs={{0,1},{1,0},{2,3},{3,2},{4,5},{5,4},{6,7},{7,6},{8,9},{9,8},{10,11... | collective-permute-start | bytes 307208 | tf_op jit(solution)/shard_map/ppermute | solution.py:385
  64.0 7.5 %collective-permute-start.11 = (bf16[392,256]{1,0:T(8,128)(2,1)S(1)}, bf16[392,256]{1,0:T(8,128)(2,1)S(1)}, u32[]{:S(2)}, u32[]{:S(2)}) collective-permute-start(bf16[392,256]{1,0:T(8,128)(2,1)S(1)} %get-tuple-element.100), channel_id=1, source_target_pairs={{0,1},{1,0},{2,3},{3,2},{4,5},{5,4},{6,7},{7,6},{8,9},{9,8},{10,11... | collective-permute-start | bytes 602120 | tf_op jit(solution)/shard_map/ppermute | solution.py:385
  64.8 9.3 %collective-permute-start.12 = (bf16[392,256]{1,0:T(8,128)(2,1)S(1)}, bf16[392,256]{1,0:T(8,128)(2,1)S(1)}, u32[]{:S(2)}, u32[]{:S(2)}) collective-permute-start(bf16[392,256]{1,0:T(8,128)(2,1)S(1)} %get-tuple-element.101), channel_id=1, source_target_pairs={{0,2},{2,0},{1,3},{3,1},{4,6},{6,4},{5,7},{7,5},{8,10},{10,8},{9,1... | collective-permute-start | bytes 602120 | tf_op jit(solution)/shard_map/ppermute | solution.py:385
  68.6 11.7 %collective-permute-start.17 = (bf16[200,512]{1,0:T(8,128)(2,1)S(1)}, bf16[200,512]{1,0:T(8,128)(2,1)S(1)}, u32[]{:S(2)}, u32[]{:S(2)}) collective-permute-start(bf16[200,512]{1,0:T(8,128)(2,1)S(1)} %get-tuple-element.110), channel_id=1, source_target_pairs={{0,4},{4,0},{1,5},{5,1},{2,6},{6,2},{3,7},{7,3},{8,12},{12,8},{9,1... | collective-permute-start | bytes 614408 | tf_op jit(solution)/shard_map/ppermute | solution.py:385
  75.3 4.9 %collective-permute-start.13 = (bf16[200,256]{1,0:T(8,128)(2,1)S(1)}, bf16[200,256]{1,0:T(8,128)(2,1)S(1)}, u32[]{:S(2)}, u32[]{:S(2)}) collective-permute-start(bf16[200,256]{1,0:T(8,128)(2,1)S(1)} %get-tuple-element.104), channel_id=1, source_target_pairs={{0,2},{2,0},{1,3},{3,1},{4,6},{6,4},{5,7},{7,5},{8,10},{10,8},{9,1... | collective-permute-start | bytes 307208 | tf_op jit(solution)/shard_map/ppermute | solution.py:385
  75.3 4.9 %collective-permute-start.14 = (bf16[200,256]{1,0:T(8,128)(2,1)S(1)}, bf16[200,256]{1,0:T(8,128)(2,1)S(1)}, u32[]{:S(2)}, u32[]{:S(2)}) collective-permute-start(bf16[200,256]{1,0:T(8,128)(2,1)S(1)} %get-tuple-element.105), channel_id=1, source_target_pairs={{0,1},{1,0},{2,3},{3,2},{4,5},{5,4},{6,7},{7,6},{8,9},{9,8},{10,11... | collective-permute-start | bytes 307208 | tf_op jit(solution)/shard_map/ppermute | solution.py:385
  80.9 1.2 %collective-permute-start.18 = (f32[16,128]{1,0:T(8,128)S(1)}, f32[16,128]{1,0:T(8,128)S(1)}, u32[]{:S(2)}, u32[]{:S(2)}) collective-permute-start(f32[16,128]{1,0:T(8,128)S(1)} %get-tuple-element.113), channel_id=1, source_target_pairs={{0,8},{8,0},{1,9},{9,1},{2,10},{10,2},{3,11},{11,3},{4,12},{12,4},... | collective-permute-start | bytes 24584 | tf_op jit(solution)/shard_map/ppermute | solution.py:491

commit v8 on v7

--- a/solution.py
+++ b/solution.py
@@ -357,7 +357,7 @@
 
 def build(bits):
     lower = bits[1:]
-    orders = (list(reversed(lower)), list(lower))
+    orders = (list(lower), list(reversed(lower)))
 
     def local(mobility, right_side, precond):
         row_count = mobility.shape[5]

time: 95.5 us -> 95 us (level)
  waiting for transfers between devices: 27.1 us -> 25 us
  starting transfers between devices: 20.2 us -> 21.8 us
    ppermute x18, waiting for transfers between devices: 25.9 us -> 23.9 us  [swap(): lax.ppermute(cast(a, kind), name, SWAP)]
    ppermute x18, starting transfers between devices: 20.1 us -> 21.7 us  [swap(): lax.ppermute(cast(a, kind), name, SWAP)]
  transfers between devices with their start and end apart: 19 -> 19, of which waited for: 14 -> 13; matrix products, arithmetic and copies ran while one was open for 0% -> 0% of each run, Pallas kernels for 7% -> 7%
where the time goes in v8:
time: 95 us; the launch traced here: 94.9 us
  blocking collectives  30.9 us (33%)
  waiting for transfers between devices  25 us (26%)
  starting transfers between devices  21.8 us (23%)
  Pallas kernels  15.4 us (16%)
    ppermute x18, waiting for transfers between devices, swap(): lax.ppermute(cast(a, kind), name, SWAP)  23.9 us
    ppermute x18, starting transfers between devices, swap(): lax.ppermute(cast(a, kind), name, SWAP)  21.7 us
    all_gather x2, blocking collectives, gather(): return travel(sent, kind, lambda a: lax.all_gather(a, ('row', 'core')))  18.6 us
    pallas_call x14, Pallas kernels, call(): pl.pallas_call(body, out_shape=[pltpu.VMEM(shape, dtype) for shape, dtype...  15.4 us
    all_to_all x1, blocking collectives, local(): lax.all_to_all(jnp.broadcast_to(flat, (members,) + flat.shape), ('row',)...  12.3 us
  transfers between devices with their start and end apart: 19, of which 13 were waited for; matrix products, arithmetic and copies ran while one was open for 0% of the time, Pallas kernels for 7%

profile of v8, /device:TPU:0, one launch (start us, length us, event | category | flops | bytes accessed | tf_op | source)
XLA Modules:
  0.0 94.9 jit_solution(677052942422395099)
XLA Ops:
  0.6 1.7 %shard_map.50 = (f32[192,512]{1,0:T(8,128)S(1)}, f32[200,512]{1,0:T(8,128)S(1)}) custom-call(f32[192,512]{1,0:T(8,128)} %bitcast.16, f32[96,192]{1,0:T(8,128)} %refs_8_.1), custom_call_target="tpu_custom_call" | custom-call | tf_op jit(solution)/shard_map/pallas_call | solution.py:341
  2.4 10.3 %all-gather = f16[800,512]{1,0:T(8,128)(2,1)S(1)} all-gather(f16[200,512]{1,0:T(8,128)(2,1)S(1)} %convert_element_type.60), channel_id=2, replica_groups=mesh['row'=2,'core'=2,'bit2'=2,'bit1'=2,'bit0'=2] {'row','core'}, dimensions={0}, use_global_device_ids=true | all-gather | bytes 1024000 | tf_op jit(solution)/shard_map/all_gather | solution.py:376
  13.0 2.2 %shard_map.52 = (f32[392,256]{1,0:T(8,128)S(1)}, f32[392,256]{1,0:T(8,128)S(1)}, f32[384,256]{1,0:T(8,128)S(1)}, f32[384,256]{1,0:T(8,128)S(1)}, f32[8,512]{1,0:T(8,128)S(1)}) custom-call(s32[3]{0:T(128)S(1)} %pad_add_fusion.1.sides_ref, bf16[3,3,256,512]{3,2,1,0:T(8,128)(2,1)S(1)} %bitcast.9, f32[4,200,512]{2,1,0:T(8,128)S(1)} %convert.got_ref), custom_call_target="tpu_custom_call" | custom-call | tf_op jit(solution)/shard_map/pallas_call | solution.py:341
  15.2 1.5 %collective-permute-start.1 = (f16[392,256]{1,0:T(8,128)(2,1)S(1)}, f16[392,256]{1,0:T(8,128)(2,1)S(1)}, u32[]{:S(2)}, u32[]{:S(2)}) collective-permute-start(f16[392,256]{1,0:T(8,128)(2,1)S(1)} %convert_element_type.64), channel_id=1, source_target_pairs={{0,1},{1,0},{2,3},{3,2},{4,5},{5,4},{6,7},{7,6},{8,9},{9,8},{10,11... | collective-permute-start | bytes 602120 | tf_op jit(solution)/shard_map/ppermute | solution.py:385
  16.8 1.6 %collective-permute-start = (f16[392,256]{1,0:T(8,128)(2,1)S(1)}, f16[392,256]{1,0:T(8,128)(2,1)S(1)}, u32[]{:S(2)}, u32[]{:S(2)}) collective-permute-start(f16[392,256]{1,0:T(8,128)(2,1)S(1)} %convert_element_type.62), channel_id=1, source_target_pairs={{0,2},{2,0},{1,3},{3,1},{4,6},{6,4},{5,7},{7,5},{8,10},{10,8},{9,1... | collective-permute-start | bytes 602120 | tf_op jit(solution)/shard_map/ppermute | solution.py:385
  18.4 2.2 %shard_map.51 = (f32[392,256]{1,0:T(8,128)S(1)}, f32[392,256]{1,0:T(8,128)S(1)}, f32[384,256]{1,0:T(8,128)S(1)}, f32[384,256]{1,0:T(8,128)S(1)}, f32[8,512]{1,0:T(8,128)S(1)}) custom-call(s32[3]{0:T(128)S(1)} %pad_add_fusion.1.sides_ref, bf16[3,3,256,512]{3,2,1,0:T(8,128)(2,1)S(1)} %bitcast.10, f32[4,200,512]{2,1,0:T(8,128)S(1)} %convert.got_ref), custom_call_target="tpu_custom_call" | custom-call | tf_op jit(solution)/shard_map/pallas_call | solution.py:341
  20.7 1.8 %collective-permute-done.1 = f16[392,256]{1,0:T(8,128)(2,1)S(1)} collective-permute-done((f16[392,256]{1,0:T(8,128)(2,1)S(1)}, f16[392,256]{1,0:T(8,128)(2,1)S(1)}, u32[]{:S(2)}, u32[]{:S(2)}) %collective-permute-start.1) | collective-permute-done | bytes 200736 | tf_op jit(solution)/shard_map/ppermute | solution.py:385
  24.5 1.6 %collective-permute-start.7 = (f16[200,256]{1,0:T(8,128)(2,1)S(1)}, f16[200,256]{1,0:T(8,128)(2,1)S(1)}, u32[]{:S(2)}, u32[]{:S(2)}) collective-permute-start(f16[200,256]{1,0:T(8,128)(2,1)S(1)} %convert_element_type.76), channel_id=1, source_target_pairs={{0,2},{2,0},{1,3},{3,1},{4,6},{6,4},{5,7},{7,5},{8,10},{10,8},{9,1... | collective-permute-start | bytes 307208 | tf_op jit(solution)/shard_map/ppermute | solution.py:385
  26.8 1.6 %collective-permute-start.3 = (f16[392,256]{1,0:T(8,128)(2,1)S(1)}, f16[392,256]{1,0:T(8,128)(2,1)S(1)}, u32[]{:S(2)}, u32[]{:S(2)}) collective-permute-start(f16[392,256]{1,0:T(8,128)(2,1)S(1)} %convert_element_type.68), channel_id=1, source_target_pairs={{0,1},{1,0},{2,3},{3,2},{4,5},{5,4},{6,7},{7,6},{8,9},{9,8},{10,11... | collective-permute-start | bytes 602120 | tf_op jit(solution)/shard_map/ppermute | solution.py:385
  29.3 2.7 %collective-permute-done.6 = f16[200,256]{1,0:T(8,128)(2,1)S(1)} collective-permute-done((f16[200,256]{1,0:T(8,128)(2,1)S(1)}, f16[200,256]{1,0:T(8,128)(2,1)S(1)}, u32[]{:S(2)}, u32[]{:S(2)}) %collective-permute-start.6) | collective-permute-done | bytes 102432 | tf_op jit(solution)/shard_map/ppermute | solution.py:385
  32.8 2.6 %collective-permute-start.8 = (f16[200,512]{1,0:T(8,128)(2,1)S(1)}, f16[200,512]{1,0:T(8,128)(2,1)S(1)}, u32[]{:S(2)}, u32[]{:S(2)}) collective-permute-start(f16[200,512]{1,0:T(8,128)(2,1)S(1)} %convert_element_type.78), channel_id=1, source_target_pairs={{0,4},{4,0},{1,5},{5,1},{2,6},{6,2},{3,7},{7,3},{8,12},{12,8},{9,1... | collective-permute-start | bytes 614408 | tf_op jit(solution)/shard_map/ppermute | solution.py:385
  37.8 4.5 %collective-permute-done.5 = f16[200,256]{1,0:T(8,128)(2,1)S(1)} collective-permute-done((f16[200,256]{1,0:T(8,128)(2,1)S(1)}, f16[200,256]{1,0:T(8,128)(2,1)S(1)}, u32[]{:S(2)}, u32[]{:S(2)}) %collective-permute-start.5) | collective-permute-done | bytes 102432 | tf_op jit(solution)/shard_map/ppermute | solution.py:385
  43.1 8.4 %all-gather.1 = bf16[800,512]{1,0:T(8,128)(2,1)S(1)} all-gather(bf16[200,512]{1,0:T(8,128)(2,1)S(1)} %get-tuple-element.86), channel_id=3, replica_groups=mesh['row'=2,'core'=2,'bit2'=2,'bit1'=2,'bit0'=2] {'row','core'}, dimensions={0}, use_global_device_ids=true | all-gather | bytes 1024000 | tf_op jit(solution)/shard_map/all_gather | solution.py:376
  51.4 1.4 %shard_map.58 = (bf16[392,256]{1,0:T(8,128)(2,1)S(1)}, bf16[392,256]{1,0:T(8,128)(2,1)S(1)}, f32[384,256]{1,0:T(8,128)S(1)}, f32[384,256]{1,0:T(8,128)S(1)}, f32[8,512]{1,0:T(8,128)S(1)}) custom-call(s32[3]{0:T(128)S(1)} %pad_add_fusion.1.sides_ref, bf16[3,3,256,512]{3,2,1,0:T(8,128)(2,1)S(1)} %bitcast.11, bf16[4,200,512]{2,1,0:T(8,128)(2,1)S(1)} %bitcast.13), custom_call_target="tpu_custom_call" | custom-call | tf_op jit(solution)/shard_map/pallas_call | solution.py:341
  54.6 1.5 %shard_map.57 = (bf16[392,256]{1,0:T(8,128)(2,1)S(1)}, bf16[392,256]{1,0:T(8,128)(2,1)S(1)}, f32[384,256]{1,0:T(8,128)S(1)}, f32[384,256]{1,0:T(8,128)S(1)}, f32[8,512]{1,0:T(8,128)S(1)}) custom-call(s32[3]{0:T(128)S(1)} %pad_add_fusion.1.sides_ref, bf16[3,3,256,512]{3,2,1,0:T(8,128)(2,1)S(1)} %bitcast.12, bf16[4,200,512]{2,1,0:T(8,128)(2,1)S(1)} %bitcast.14), custom_call_target="tpu_custom_call" | custom-call | tf_op jit(solution)/shard_map/pallas_call | solution.py:341
  56.1 4.1 %collective-permute-done.9.refs_2_ = bf16[392,256]{1,0:T(8,128)(2,1)S(1)} collective-permute-done((bf16[392,256]{1,0:T(8,128)(2,1)S(1)}, bf16[392,256]{1,0:T(8,128)(2,1)S(1)}, u32[]{:S(2)}, u32[]{:S(2)}) %collective-permute-start.9) | collective-permute-done | bytes 200736 | tf_op jit(solution)/shard_map/ppermute | solution.py:385
  64.3 1.5 %collective-permute-start.12 = (bf16[392,256]{1,0:T(8,128)(2,1)S(1)}, bf16[392,256]{1,0:T(8,128)(2,1)S(1)}, u32[]{:S(2)}, u32[]{:S(2)}) collective-permute-start(bf16[392,256]{1,0:T(8,128)(2,1)S(1)} %get-tuple-element.101), channel_id=1, source_target_pairs={{0,1},{1,0},{2,3},{3,2},{4,5},{5,4},{6,7},{7,6},{8,9},{9,8},{10,11... | collective-permute-start | bytes 602120 | tf_op jit(solution)/shard_map/ppermute | solution.py:385
  65.8 1.7 %collective-permute-done.15.refs_2_ = bf16[200,256]{1,0:T(8,128)(2,1)S(1)} collective-permute-done((bf16[200,256]{1,0:T(8,128)(2,1)S(1)}, bf16[200,256]{1,0:T(8,128)(2,1)S(1)}, u32[]{:S(2)}, u32[]{:S(2)}) %collective-permute-start.15) | collective-permute-done | bytes 102432 | tf_op jit(solution)/shard_map/ppermute | solution.py:385
  68.1 3.1 %collective-permute-start.17 = (bf16[200,512]{1,0:T(8,128)(2,1)S(1)}, bf16[200,512]{1,0:T(8,128)(2,1)S(1)}, u32[]{:S(2)}, u32[]{:S(2)}) collective-permute-start(bf16[200,512]{1,0:T(8,128)(2,1)S(1)} %get-tuple-element.110), channel_id=1, source_target_pairs={{0,4},{4,0},{1,5},{5,1},{2,6},{6,2},{3,7},{7,3},{8,12},{12,8},{9,1... | collective-permute-start | bytes 614408 | tf_op jit(solution)/shard_map/ppermute | solution.py:385
  71.2 1.3 %collective-permute-done.11.refs_2_ = bf16[392,256]{1,0:T(8,128)(2,1)S(1)} collective-permute-done((bf16[392,256]{1,0:T(8,128)(2,1)S(1)}, bf16[392,256]{1,0:T(8,128)(2,1)S(1)}, u32[]{:S(2)}, u32[]{:S(2)}) %collective-permute-start.11) | collective-permute-done | bytes 200736 | tf_op jit(solution)/shard_map/ppermute | solution.py:385
  73.7 1.5 %collective-permute-start.13 = (bf16[200,256]{1,0:T(8,128)(2,1)S(1)}, bf16[200,256]{1,0:T(8,128)(2,1)S(1)}, u32[]{:S(2)}, u32[]{:S(2)}) collective-permute-start(bf16[200,256]{1,0:T(8,128)(2,1)S(1)} %get-tuple-element.104), channel_id=1, source_target_pairs={{0,1},{1,0},{2,3},{3,2},{4,5},{5,4},{6,7},{7,6},{8,9},{9,8},{10,11... | collective-permute-start | bytes 307208 | tf_op jit(solution)/shard_map/ppermute | solution.py:385
  75.2 3.2 %collective-permute-done.13.refs_2_ = bf16[200,256]{1,0:T(8,128)(2,1)S(1)} collective-permute-done((bf16[200,256]{1,0:T(8,128)(2,1)S(1)}, bf16[200,256]{1,0:T(8,128)(2,1)S(1)}, u32[]{:S(2)}, u32[]{:S(2)}) %collective-permute-start.13) | collective-permute-done | bytes 102432 | tf_op jit(solution)/shard_map/ppermute | solution.py:385
  78.3 1.5 %collective-permute-done.14.refs_3_ = bf16[200,256]{1,0:T(8,128)(2,1)S(1)} collective-permute-done((bf16[200,256]{1,0:T(8,128)(2,1)S(1)}, bf16[200,256]{1,0:T(8,128)(2,1)S(1)}, u32[]{:S(2)}, u32[]{:S(2)}) %collective-permute-start.14) | collective-permute-done | bytes 102432 | tf_op jit(solution)/shard_map/ppermute | solution.py:385
  81.7 12.3 %all_to_all.5.flat_ref = f32[16,16,128]{2,1,0:T(8,128)S(1)} all-to-all(f32[16,16,128]{2,1,0:T(8,128)S(1)} %broadcast_in_dim.3), channel_id=1, replica_groups=mesh['row'=2,'core'=2,'bit2'=2,'bit1'=2,'bit0'=2] {'row','bit2','bit1','..., dimensions={0} | all-to-all | bytes 262144 | tf_op jit(solution)/shard_map/all_to_all | solution.py:493
  (59 shorter events, 18.2 us)
Async XLA Ops:
  0.6 12.4 %copy-start = (bf16[3,3,4,1,64,512]{5,4,3,2,1,0:T(8,128)(2,1)S(1)}, bf16[3,3,4,1,64,512]{5,4,3,2,1,0:T(8,128)(2,1)}, u32[]{:S(2)}) copy-start(bf16[3,3,4,1,64,512]{5,4,3,2,1,0:T(8,128)(2,1)} %param.3) | copy-start | bytes 7077892
  15.2 7.3 %collective-permute-start.1 = (f16[392,256]{1,0:T(8,128)(2,1)S(1)}, f16[392,256]{1,0:T(8,128)(2,1)S(1)}, u32[]{:S(2)}, u32[]{:S(2)}) collective-permute-start(f16[392,256]{1,0:T(8,128)(2,1)S(1)} %convert_element_type.64), channel_id=1, source_target_pairs={{0,1},{1,0},{2,3},{3,2},{4,5},{5,4},{6,7},{7,6},{8,9},{9,8},{10,11... | collective-permute-start | bytes 602120 | tf_op jit(solution)/shard_map/ppermute | solution.py:385
  16.8 7.0 %collective-permute-start = (f16[392,256]{1,0:T(8,128)(2,1)S(1)}, f16[392,256]{1,0:T(8,128)(2,1)S(1)}, u32[]{:S(2)}, u32[]{:S(2)}) collective-permute-start(f16[392,256]{1,0:T(8,128)(2,1)S(1)} %convert_element_type.62), channel_id=1, source_target_pairs={{0,2},{2,0},{1,3},{3,1},{4,6},{6,4},{5,7},{7,5},{8,10},{10,8},{9,1... | collective-permute-start | bytes 602120 | tf_op jit(solution)/shard_map/ppermute | solution.py:385
  24.5 4.8 %collective-permute-start.7 = (f16[200,256]{1,0:T(8,128)(2,1)S(1)}, f16[200,256]{1,0:T(8,128)(2,1)S(1)}, u32[]{:S(2)}, u32[]{:S(2)}) collective-permute-start(f16[200,256]{1,0:T(8,128)(2,1)S(1)} %convert_element_type.76), channel_id=1, source_target_pairs={{0,2},{2,0},{1,3},{3,1},{4,6},{6,4},{5,7},{7,5},{8,10},{10,8},{9,1... | collective-permute-start | bytes 307208 | tf_op jit(solution)/shard_map/ppermute | solution.py:385
  26.2 5.8 %collective-permute-start.6 = (f16[200,256]{1,0:T(8,128)(2,1)S(1)}, f16[200,256]{1,0:T(8,128)(2,1)S(1)}, u32[]{:S(2)}, u32[]{:S(2)}) collective-permute-start(f16[200,256]{1,0:T(8,128)(2,1)S(1)} %convert_element_type.74), channel_id=1, source_target_pairs={{0,1},{1,0},{2,3},{3,2},{4,5},{5,4},{6,7},{7,6},{8,9},{9,8},{10,11... | collective-permute-start | bytes 307208 | tf_op jit(solution)/shard_map/ppermute | solution.py:385
  26.8 8.6 %collective-permute-start.3 = (f16[392,256]{1,0:T(8,128)(2,1)S(1)}, f16[392,256]{1,0:T(8,128)(2,1)S(1)}, u32[]{:S(2)}, u32[]{:S(2)}) collective-permute-start(f16[392,256]{1,0:T(8,128)(2,1)S(1)} %convert_element_type.68), channel_id=1, source_target_pairs={{0,1},{1,0},{2,3},{3,2},{4,5},{5,4},{6,7},{7,6},{8,9},{9,8},{10,11... | collective-permute-start | bytes 602120 | tf_op jit(solution)/shard_map/ppermute | solution.py:385
  28.4 7.0 %collective-permute-start.2 = (f16[392,256]{1,0:T(8,128)(2,1)S(1)}, f16[392,256]{1,0:T(8,128)(2,1)S(1)}, u32[]{:S(2)}, u32[]{:S(2)}) collective-permute-start(f16[392,256]{1,0:T(8,128)(2,1)S(1)} %convert_element_type.66), channel_id=1, source_target_pairs={{0,2},{2,0},{1,3},{3,1},{4,6},{6,4},{5,7},{7,5},{8,10},{10,8},{9,1... | collective-permute-start | bytes 602120 | tf_op jit(solution)/shard_map/ppermute | solution.py:385
  32.7 9.7 %copy-start.1 = (f32[96,192]{1,0:T(8,128)S(1)}, f32[96,192]{1,0:T(8,128)}, u32[]{:S(2)}) copy-start(f32[96,192]{1,0:T(8,128)} %refs_8_.1) | copy-start | bytes 221188
  32.8 9.7 %collective-permute-start.8 = (f16[200,512]{1,0:T(8,128)(2,1)S(1)}, f16[200,512]{1,0:T(8,128)(2,1)S(1)}, u32[]{:S(2)}, u32[]{:S(2)}) collective-permute-start(f16[200,512]{1,0:T(8,128)(2,1)S(1)} %convert_element_type.78), channel_id=1, source_target_pairs={{0,4},{4,0},{1,5},{5,1},{2,6},{6,2},{3,7},{7,3},{8,12},{12,8},{9,1... | collective-permute-start | bytes 614408 | tf_op jit(solution)/shard_map/ppermute | solution.py:385
  36.7 5.7 %collective-permute-start.5 = (f16[200,256]{1,0:T(8,128)(2,1)S(1)}, f16[200,256]{1,0:T(8,128)(2,1)S(1)}, u32[]{:S(2)}, u32[]{:S(2)}) collective-permute-start(f16[200,256]{1,0:T(8,128)(2,1)S(1)} %convert_element_type.72), channel_id=1, source_target_pairs={{0,2},{2,0},{1,3},{3,1},{4,6},{6,4},{5,7},{7,5},{8,10},{10,8},{9,1... | collective-permute-start | bytes 307208 | tf_op jit(solution)/shard_map/ppermute | solution.py:385
  37.2 5.1 %collective-permute-start.4 = (f16[200,256]{1,0:T(8,128)(2,1)S(1)}, f16[200,256]{1,0:T(8,128)(2,1)S(1)}, u32[]{:S(2)}, u32[]{:S(2)}) collective-permute-start(f16[200,256]{1,0:T(8,128)(2,1)S(1)} %convert_element_type.70), channel_id=1, source_target_pairs={{0,1},{1,0},{2,3},{3,2},{4,5},{5,4},{6,7},{7,6},{8,9},{9,8},{10,11... | collective-permute-start | bytes 307208 | tf_op jit(solution)/shard_map/ppermute | solution.py:385
  52.9 7.3 %collective-permute-start.9 = (bf16[392,256]{1,0:T(8,128)(2,1)S(1)}, bf16[392,256]{1,0:T(8,128)(2,1)S(1)}, u32[]{:S(2)}, u32[]{:S(2)}) collective-permute-start(bf16[392,256]{1,0:T(8,128)(2,1)S(1)} %get-tuple-element.95), channel_id=1, source_target_pairs={{0,2},{2,0},{1,3},{3,1},{4,6},{6,4},{5,7},{7,5},{8,10},{10,8},{9,1... | collective-permute-start | bytes 602120 | tf_op jit(solution)/shard_map/ppermute | solution.py:385
  54.1 7.0 %collective-permute-start.10 = (bf16[392,256]{1,0:T(8,128)(2,1)S(1)}, bf16[392,256]{1,0:T(8,128)(2,1)S(1)}, u32[]{:S(2)}, u32[]{:S(2)}) collective-permute-start(bf16[392,256]{1,0:T(8,128)(2,1)S(1)} %get-tuple-element.96), channel_id=1, source_target_pairs={{0,1},{1,0},{2,3},{3,2},{4,5},{5,4},{6,7},{7,6},{8,9},{9,8},{10,11... | collective-permute-start | bytes 602120 | tf_op jit(solution)/shard_map/ppermute | solution.py:385
  61.7 5.8 %collective-permute-start.15 = (bf16[200,256]{1,0:T(8,128)(2,1)S(1)}, bf16[200,256]{1,0:T(8,128)(2,1)S(1)}, u32[]{:S(2)}, u32[]{:S(2)}) collective-permute-start(bf16[200,256]{1,0:T(8,128)(2,1)S(1)} %get-tuple-element.108), channel_id=1, source_target_pairs={{0,1},{1,0},{2,3},{3,2},{4,5},{5,4},{6,7},{7,6},{8,9},{9,8},{10,11... | collective-permute-start | bytes 307208 | tf_op jit(solution)/shard_map/ppermute | solution.py:385
  62.3 5.8 %collective-permute-start.16 = (bf16[200,256]{1,0:T(8,128)(2,1)S(1)}, bf16[200,256]{1,0:T(8,128)(2,1)S(1)}, u32[]{:S(2)}, u32[]{:S(2)}) collective-permute-start(bf16[200,256]{1,0:T(8,128)(2,1)S(1)} %get-tuple-element.109), channel_id=1, source_target_pairs={{0,2},{2,0},{1,3},{3,1},{4,6},{6,4},{5,7},{7,5},{8,10},{10,8},{9,1... | collective-permute-start | bytes 307208 | tf_op jit(solution)/shard_map/ppermute | solution.py:385
  63.4 9.1 %collective-permute-start.11 = (bf16[392,256]{1,0:T(8,128)(2,1)S(1)}, bf16[392,256]{1,0:T(8,128)(2,1)S(1)}, u32[]{:S(2)}, u32[]{:S(2)}) collective-permute-start(bf16[392,256]{1,0:T(8,128)(2,1)S(1)} %get-tuple-element.100), channel_id=1, source_target_pairs={{0,2},{2,0},{1,3},{3,1},{4,6},{6,4},{5,7},{7,5},{8,10},{10,8},{9,1... | collective-permute-start | bytes 602120 | tf_op jit(solution)/shard_map/ppermute | solution.py:385
  64.3 8.2 %collective-permute-start.12 = (bf16[392,256]{1,0:T(8,128)(2,1)S(1)}, bf16[392,256]{1,0:T(8,128)(2,1)S(1)}, u32[]{:S(2)}, u32[]{:S(2)}) collective-permute-start(bf16[392,256]{1,0:T(8,128)(2,1)S(1)} %get-tuple-element.101), channel_id=1, source_target_pairs={{0,1},{1,0},{2,3},{3,2},{4,5},{5,4},{6,7},{7,6},{8,9},{9,8},{10,11... | collective-permute-start | bytes 602120 | tf_op jit(solution)/shard_map/ppermute | solution.py:385
  68.1 11.7 %collective-permute-start.17 = (bf16[200,512]{1,0:T(8,128)(2,1)S(1)}, bf16[200,512]{1,0:T(8,128)(2,1)S(1)}, u32[]{:S(2)}, u32[]{:S(2)}) collective-permute-start(bf16[200,512]{1,0:T(8,128)(2,1)S(1)} %get-tuple-element.110), channel_id=1, source_target_pairs={{0,4},{4,0},{1,5},{5,1},{2,6},{6,2},{3,7},{7,3},{8,12},{12,8},{9,1... | collective-permute-start | bytes 614408 | tf_op jit(solution)/shard_map/ppermute | solution.py:385
  73.7 4.7 %collective-permute-start.13 = (bf16[200,256]{1,0:T(8,128)(2,1)S(1)}, bf16[200,256]{1,0:T(8,128)(2,1)S(1)}, u32[]{:S(2)}, u32[]{:S(2)}) collective-permute-start(bf16[200,256]{1,0:T(8,128)(2,1)S(1)} %get-tuple-element.104), channel_id=1, source_target_pairs={{0,1},{1,0},{2,3},{3,2},{4,5},{5,4},{6,7},{7,6},{8,9},{9,8},{10,11... | collective-permute-start | bytes 307208 | tf_op jit(solution)/shard_map/ppermute | solution.py:385
  75.2 4.7 %collective-permute-start.14 = (bf16[200,256]{1,0:T(8,128)(2,1)S(1)}, bf16[200,256]{1,0:T(8,128)(2,1)S(1)}, u32[]{:S(2)}, u32[]{:S(2)}) collective-permute-start(bf16[200,256]{1,0:T(8,128)(2,1)S(1)} %get-tuple-element.105), channel_id=1, source_target_pairs={{0,2},{2,0},{1,3},{3,1},{4,6},{6,4},{5,7},{7,5},{8,10},{10,8},{9,1... | collective-permute-start | bytes 307208 | tf_op jit(solution)/shard_map/ppermute | solution.py:385
  80.5 1.2 %collective-permute-start.18 = (f32[16,128]{1,0:T(8,128)S(1)}, f32[16,128]{1,0:T(8,128)S(1)}, u32[]{:S(2)}, u32[]{:S(2)}) collective-permute-start(f32[16,128]{1,0:T(8,128)S(1)} %get-tuple-element.113), channel_id=1, source_target_pairs={{0,8},{8,0},{1,9},{9,1},{2,10},{10,2},{3,11},{11,3},{4,12},{12,4},... | collective-permute-start | bytes 24584 | tf_op jit(solution)/shard_map/ppermute | solution.py:491
